TPU v7x, 8 devices: a whole 2x2x1 slice. The times are simulated.
8 devices in a mesh: data: 8 (over z, y, x, core).
Axes of the slice: x: 2, y: 2, z: 1, core: 2. Of those that a mesh axis runs over, the one named last changes fastest.
Arguments:
- feat_a: bfloat16 [2048, 512], P('data')
- feat_b: bfloat16 [2048, 512], P('data')
- w_one: bfloat16 [512, 2048], replicated
- w_two: bfloat16 [2048, 2048], replicated
- w_three: bfloat16 [2048, 2048], replicated
- g_one: float32 [2048], replicated
- b_one: float32 [2048], replicated
- g_two: float32 [2048], replicated
- b_two: float32 [2048], replicated
- lam_off: float32 [], replicated
Outputs:
- output 1: float32 [], replicated
- output 2: float32 [512, 2048], replicated
- output 3: float32 [2048, 2048], replicated
- output 4: float32 [2048, 2048], replicated
- output 5: float32 [2048], replicated
- output 6: float32 [2048], replicated
- output 7: float32 [2048], replicated
- output 8: float32 [2048], replicated
All inputs are finite; a program needn't handle non-finite values.
Results may differ from a plain program's by a relative error of at most 0.00599.
Values are sent between devices in bfloat16 or wider.
A program may use at most 1 GiB of HBM per device.

v0:
```python
import jax
import jax.numpy as jnp
from jax import lax
from jax.sharding import PartitionSpec as P

NORM_EPS = 1e-5
BATCH_AXIS = 'data'


def global_norm(pre, rows_all):
    stat_sums = lax.psum(jnp.stack([jnp.sum(pre, axis=1), jnp.sum(pre * pre, axis=1)]), BATCH_AXIS)
    mean_val = stat_sums[0] / rows_all
    var_val = stat_sums[1] / rows_all - mean_val * mean_val
    inv_std = lax.rsqrt(var_val + NORM_EPS)[:, None, :]
    return (pre - mean_val[:, None, :]) * inv_std, inv_std


def global_norm_back(grad_norm, normed, inv_std, rows_all):
    stat_sums = lax.psum(jnp.stack([jnp.sum(grad_norm, axis=1), jnp.sum(grad_norm * normed, axis=1)]), BATCH_AXIS)
    mean_grad = (stat_sums[0] / rows_all)[:, None, :]
    mean_cross = (stat_sums[1] / rows_all)[:, None, :]
    return inv_std * (grad_norm - mean_grad - normed * mean_cross)


def corr_loss(corr, lam_off, width):
    diag_c = jnp.diagonal(corr)
    loss_val = jnp.sum((1.0 - diag_c) ** 2) + lam_off * (jnp.sum(corr * corr) - jnp.sum(diag_c * diag_c))
    on_diag = jnp.arange(width)[:, None] == jnp.arange(width)[None, :]
    grad_c = jnp.where(on_diag, -2.0 * (1.0 - corr), 2.0 * lam_off * corr).astype(jnp.bfloat16)
    return loss_val, grad_c


def solution(mesh):
    num_devs = mesh.shape[BATCH_AXIS]

    def local_step(feat_a, feat_b, w_one, w_two, w_three, g_one, b_one, g_two, b_two, lam_off):
        rows_all = feat_a.shape[0] * num_devs
        width = w_two.shape[0]
        features = jnp.stack([feat_a, feat_b])
        pre_one = jnp.einsum('vnf,fd->vnd', features, w_one, preferred_element_type=jnp.float32)
        norm_one, inv_one = global_norm(pre_one, rows_all)
        aff_one = norm_one * g_one + b_one
        act_one = jnp.maximum(aff_one, 0.0).astype(jnp.bfloat16)
        pre_two = jnp.einsum('woe,ef->wof', act_one, w_two, preferred_element_type=jnp.float32)
        norm_two, inv_two = global_norm(pre_two, rows_all)
        aff_two = norm_two * g_two + b_two
        act_two = jnp.maximum(aff_two, 0.0).astype(jnp.bfloat16)
        proj_out = jnp.einsum('woe,ef->wof', act_two, w_three, preferred_element_type=jnp.float32)
        norm_out, inv_out = global_norm(proj_out, rows_all)
        emb = norm_out.astype(jnp.bfloat16)
        part_corr = jnp.einsum('nd,ne->de', emb[0], emb[1], preferred_element_type=jnp.float32)
        corr = lax.psum(part_corr, BATCH_AXIS) / rows_all
        loss_val, grad_c = corr_loss(corr, lam_off, width)
        grad_a = jnp.einsum('ne,de->nd', emb[1], grad_c, preferred_element_type=jnp.float32)
        grad_b = jnp.einsum('nd,de->ne', emb[0], grad_c, preferred_element_type=jnp.float32)
        grad_emb = jnp.stack([grad_a, grad_b]) / rows_all
        grad_proj = global_norm_back(grad_emb, norm_out, inv_out, rows_all).astype(jnp.bfloat16)
        dw_three = jnp.einsum('woe,wof->ef', act_two, grad_proj, preferred_element_type=jnp.float32)
        grad_act_two = jnp.einsum('wof,ef->woe', grad_proj, w_three, preferred_element_type=jnp.float32)
        grad_aff_two = jnp.where(aff_two > 0, grad_act_two, 0.0)
        dg_two = jnp.sum(grad_aff_two * norm_two, axis=(0, 1))
        db_two = jnp.sum(grad_aff_two, axis=(0, 1))
        grad_pre_two = global_norm_back(grad_aff_two * g_two, norm_two, inv_two, rows_all).astype(jnp.bfloat16)
        dw_two = jnp.einsum('woe,wof->ef', act_one, grad_pre_two, preferred_element_type=jnp.float32)
        grad_act_one = jnp.einsum('wof,ef->woe', grad_pre_two, w_two, preferred_element_type=jnp.float32)
        grad_aff_one = jnp.where(aff_one > 0, grad_act_one, 0.0)
        dg_one = jnp.sum(grad_aff_one * norm_one, axis=(0, 1))
        db_one = jnp.sum(grad_aff_one, axis=(0, 1))
        grad_pre_one = global_norm_back(grad_aff_one * g_one, norm_one, inv_one, rows_all).astype(jnp.bfloat16)
        dw_one = jnp.einsum('vnf,vnd->fd', features, grad_pre_one, preferred_element_type=jnp.float32)
        totals = lax.psum((dw_one, dw_two, dw_three, dg_one, db_one, dg_two, db_two), BATCH_AXIS)
        return (loss_val,) + tuple(totals)

    row_spec = P(BATCH_AXIS, None)
    return jax.shard_map(local_step, mesh=mesh, in_specs=(row_spec, row_spec, P(), P(), P(), P(), P(), P(), P(), P()), out_specs=(P(), P(), P(), P(), P(), P(), P(), P()), check_vma=False)
```

profile of v0, /device:TPU:0, one launch (start us, length us, event | category | flops | bytes accessed | tf_op | source)
XLA Modules:
  0.0 951.7 jit_solution(7898707112063435026)
XLA Ops:
  13.1 25.2 %psum.98 = f32[2,2,2048]{2,1,0:T(2,128)S(1)} all-reduce(f32[2,2,2048]{2,1,0:T(2,128)S(1)} %pad_maximum_fusion.3), channel_id=1, replica_groups=mesh['data'=8] {'data'}, use_global_device_ids=true, to_apply=%region_2.0 | all-reduce | flops 8192 | bytes 65536 | tf_op jit(solution)/shard_map/psum | solution.py:11
  38.5 11.3 %fusion.46 = (f32[2,2048]{1,0:T(2,128)S(1)}, f32[2,2048]{1,0:T(2,128)S(1)}, f32[2,256,2048]{2,1,0:T(8,128)}) fusion(bf16[2048,2048]{1,0:T(8,128)(2,1)} %param.13, f32[2,256,2048]{2,1,0:T(8,128)} %get-tuple-element.42, f32[2048]{0:T(1024)S(1)} %copy-done.18, f32[2048]{0:T(1024)S(1)} %copy-done.16, f32[2,2048]{1,0:T(2,128)S(1)} %fusion.41, ...), kind=kOutput, calls=%fused_computation.99 | convolution fusion | flops 4304396288 | bytes 16859136 | tf_op jit(solution)/shard_map/woe,ef->wof/dot_general | solution.py:44
  49.7 23.2 %psum.99 = f32[2,2,2048]{2,1,0:T(2,128)S(1)} all-reduce(f32[2,2,2048]{2,1,0:T(2,128)S(1)} %pad_maximum_fusion.4), channel_id=1, replica_groups=mesh['data'=8] {'data'}, use_global_device_ids=true, to_apply=%region_5.0 | all-reduce | flops 8192 | bytes 65536 | tf_op jit(solution)/shard_map/psum | solution.py:11
  73.0 11.2 %fusion.45 = (f32[2,2048]{1,0:T(2,128)S(1)}, f32[2,2048]{1,0:T(2,128)S(1)}, f32[2,256,2048]{2,1,0:T(8,128)}) fusion(bf16[2048,2048]{1,0:T(8,128)(2,1)} %param.14, f32[2,256,2048]{2,1,0:T(8,128)} %get-tuple-element.43, f32[2048]{0:T(1024)S(1)} %copy-done.20, f32[2048]{0:T(1024)S(1)} %copy-done.14, f32[2,2048]{1,0:T(2,128)S(1)} %fusion.36, ...), kind=kOutput, calls=%fused_computation.98 | convolution fusion | flops 4304396288 | bytes 16859136 | tf_op jit(solution)/shard_map/woe,ef->wof/dot_general | solution.py:48
  84.2 24.3 %psum.100 = f32[2,2,2048]{2,1,0:T(2,128)S(1)} all-reduce(f32[2,2,2048]{2,1,0:T(2,128)S(1)} %pad_maximum_fusion.5), channel_id=1, replica_groups=mesh['data'=8] {'data'}, use_global_device_ids=true, to_apply=%region_8.0 | all-reduce | flops 8192 | bytes 65536 | tf_op jit(solution)/shard_map/psum | solution.py:11
  111.3 8.5 fusion.21
  120.6 206.5 %all-reduce.6.cloned.1.call-done = f32[2048,2048]{1,0:T(8,128)} async-done(((f32[2048,2048]{1,0:T(8,128)}), f32[2048,2048]{1,0:T(8,128)}) %all-reduce.6.cloned.1.call-update) | async-done | bytes 16777232 | tf_op jit(solution)/shard_map/psum | solution.py:52
  327.1 10.5 %convolution_bitcast_fusion.4 = f32[1,256,2048]{2,1,0:T(8,128)S(1)} fusion(bf16[2,256,2048]{2,1,0:T(8,128)(2,1)S(1)} %fusion.8, f32[2048,2048]{1,0:T(8,128)} %all-reduce.6.cloned.1.call-done, f32[]{:T(128)S(6)} %mul.183), kind=kOutput, calls=%fused_computation.41 | convolution fusion | flops 2176843776 | bytes 19922948 | tf_op jit(solution)/shard_map/ne,de->nd/dot_general | solution.py:54
  341.9 22.6 %psum.102 = f32[2,2,2048]{2,1,0:T(2,128)S(1)} all-reduce(f32[2,2,2048]{2,1,0:T(2,128)S(1)} %pad_maximum_fusion.6), channel_id=1, replica_groups=mesh['data'=8] {'data'}, use_global_device_ids=true, to_apply=%region_15.16 | all-reduce | flops 8192 | bytes 65536 | tf_op jit(solution)/shard_map/psum | solution.py:19
  364.6 4.7 multiply_convert_fusion.2
  369.3 11.5 %multiply_reduce_fusion.1 = (f32[2048]{0:T(1024)}, f32[2,2048]{1,0:T(2,128)S(1)}, f32[2,2048]{1,0:T(2,128)S(1)}, f32[2048]{0:T(1024)}, f32[2,256,2048]{2,1,0:T(8,128)}) fusion(f32[2,256,2048]{2,1,0:T(8,128)S(1)} %copy-done.6, f32[2,2048]{1,0:T(2,128)S(1)} %fusion.36, f32[2,2048]{1,0:T(2,128)S(1)} %fusion.37, f32[2048]{0:T(1024)S(1)} %copy-done.15, ...), kind=kOutput, calls=%fused_computation.16 | convolution fusion | flops 4308586496 | bytes 18972672 | tf_op jit(solution)/shard_map/wof,ef->woe/dot_general | solution.py:59
  380.8 24.1 %psum.103 = f32[2,2,2048]{2,1,0:T(2,128)S(1)} all-reduce(f32[2,2,2048]{2,1,0:T(2,128)S(1)} %pad_maximum_fusion.7), channel_id=1, replica_groups=mesh['data'=8] {'data'}, use_global_device_ids=true, to_apply=%region_18.19 | all-reduce | flops 8192 | bytes 65536 | tf_op jit(solution)/shard_map/psum | solution.py:19
  405.0 4.7 multiply_convert_fusion.1
  409.8 11.5 %multiply_reduce_fusion.2 = (f32[2048]{0:T(1024)}, f32[2,2048]{1,0:T(2,128)S(1)}, f32[2,2048]{1,0:T(2,128)S(1)}, f32[2048]{0:T(1024)}, f32[2,256,2048]{2,1,0:T(8,128)}) fusion(f32[2,256,2048]{2,1,0:T(8,128)S(1)} %copy-done.7, f32[2,2048]{1,0:T(2,128)S(1)} %fusion.41, f32[2,2048]{1,0:T(2,128)S(1)} %fusion.42, f32[2048]{0:T(1024)S(1)} %copy-done.17, ...), kind=kOutput, calls=%fused_computation.17 | convolution fusion | flops 4308586496 | bytes 18972672 | tf_op jit(solution)/shard_map/wof,ef->woe/dot_general | solution.py:65
  421.2 8.6 convolution_bitcast_fusion.1
  430.8 10.3 %convolution_bitcast_fusion = f32[2048,2048]{1,0:T(8,128)} fusion(bf16[2,256,2048]{2,1,0:T(8,128)(2,1)S(1)} %multiply_convert_fusion.2, f32[2,256,2048]{2,1,0:T(8,128)} %get-tuple-element.43, f32[2048]{0:T(1024)S(1)} %copy-done.21, f32[2048]{0:T(1024)S(1)} %copy-done.15, f32[2,2048]{1,0:T(2,128)S(1)} %fusion.36, f32[2,2048]{1,0:T(2,128)S(1)} %fusion.37), kind=kOutput, calls=%fused_computation.4 | convolution fusion | flops 4301258752 | bytes 23117824 | tf_op jit(solution)/shard_map/woe,wof->ef/dot_general | solution.py:58
  441.1 33.6 %all-reduce.8.cloned.1.call-done = (f32[2,2,2048]{2,1,0:T(2,128)}, f32[2048]{0:T(1024)}, f32[2048]{0:T(1024)}, f32[2048]{0:T(1024)}, f32[2048]{0:T(1024)}) async-done(((f32[2,2,2048]{2,1,0:T(2,128)}, f32[2048]{0:T(1024)}, f32[2048]{0:T(1024)}, f32[2048]{0:T(1024)}, f32[2048]{0:T(1024)}), (f32[2,2,2048]{2,1,0:T(2,128)}, f32[2048]{0:T(1024)}, f32[2048]{0:T(1024)}, f32[2048]{0:T(1024)}, ...) | async-done | bytes 65552 | tf_op jit(solution)/shard_map/psum | solution.py:19
  475.5 6.9 convolution_bitcast_fusion.2
  482.5 13.5 %multiply_reduce_fusion = (f32[]{:T(128)}, f32[2048,2048]{1,0:T(8,128)}) fusion(f32[2048,2048]{1,0:T(8,128)} %all-reduce.6.cloned.1.call-done), kind=kLoop, calls=%fused_computation.3 | loop fusion | flops 12582911 | bytes 33554436 | tf_op jit(solution)/shard_map/reduce_sum | solution.py:27
  496.0 33.5 %gather_fusion = f32[2048]{0:T(1024)S(1)} fusion(f32[2048,2048]{1,0:T(8,128)} %get-tuple-element.35, s32[2048]{0:T(1024)S(1)} %bitcast.112), kind=kCustom, calls=%fused_computation | custom fusion | bytes 32768 | tf_op jit(solution)/shard_map/jit(diagonal)/cond/branch_0_fun/gather | solution.py:26
  532.0 382.7 %all-reduce.10.cloned.1.call-done = (f32[512,2048]{1,0:T(8,128)}, f32[2048,2048]{1,0:T(8,128)}, f32[2048,2048]{1,0:T(8,128)}) async-done(((f32[512,2048]{1,0:T(8,128)}, f32[2048,2048]{1,0:T(8,128)}, f32[2048,2048]{1,0:T(8,128)}), (f32[512,2048]{1,0:T(8,128)}, f32[2048,2048]{1,0:T(8,128)}, f32[2048,2048]{1,0:T(8,128)})) %all-reduce.10.cloned.1.call-update) | async-done | bytes 37748752 | tf_op jit(solution)/shard_map/psum | solution.py:71
  914.7 4.8 copy.37
  919.6 13.6 %copy.38 = f32[2048,2048]{1,0:T(8,128)} copy(f32[2048,2048]{1,0:T(8,128)} %get-tuple-element.49) | data formatting | bytes 33554432
  934.9 6.3 copy.39
  (84 shorter events, 19.8 us)
Async XLA Ops:
  7.2 31.2 %copy-start.16 = (f32[2048]{0:T(1024)S(1)}, f32[2048]{0:T(1024)}, u32[]{:S(2)}) copy-start(f32[2048]{0:T(1024)} %param.15) | copy-start | bytes 24580
  7.2 31.2 %copy-start.18 = (f32[2048]{0:T(1024)S(1)}, f32[2048]{0:T(1024)}, u32[]{:S(2)}) copy-start(f32[2048]{0:T(1024)} %param.16) | copy-start | bytes 24580
  7.2 319.9 %all-reduce.6.cloned.1.call-start = ((), (), s32[]{:S(2)}) async-start(), calls=%async_computation | async-start | bytes 33554432 | tf_op jit(solution)/shard_map/psum | solution.py:52
  38.4 34.5 %copy-start.14 = (f32[2048]{0:T(1024)S(1)}, f32[2048]{0:T(1024)}, u32[]{:S(2)}) copy-start(f32[2048]{0:T(1024)} %param.17) | copy-start | bytes 24580
  38.4 34.5 %copy-start.20 = (f32[2048]{0:T(1024)S(1)}, f32[2048]{0:T(1024)}, u32[]{:S(2)}) copy-start(f32[2048]{0:T(1024)} %param.18) | copy-start | bytes 24580
  119.9 354.9 %all-reduce.8.cloned.1.call-start = ((), (), s32[]{:S(2)}) async-start(), calls=%async_computation.1 | async-start | bytes 131072 | tf_op jit(solution)/shard_map/psum | solution.py:19
  327.1 10.5 %copy-start.3 = (f32[2048,2048]{1,0:T(8,128)S(1)}, f32[2048,2048]{1,0:T(8,128)}, u32[]{:S(2)}) copy-start(f32[2048,2048]{1,0:T(8,128)} %all-reduce.6.cloned.1.call-done) | copy-start | bytes 50331652
  364.5 4.8 copy-start.6
  364.6 4.8 copy-start.15
  405.0 4.8 copy-start.7
  405.0 4.8 copy-start.17
  405.0 4.8 copy-start.19
  430.5 45.0 %copy-start.8 = (bf16[256,512]{1,0:T(8,128)(2,1)S(1)}, bf16[256,512]{1,0:T(8,128)(2,1)}, u32[]{:S(2)}) copy-start(bf16[256,512]{1,0:T(8,128)(2,1)} %param.11) | copy-start | bytes 786436
  430.5 45.0 %copy-start.9 = (bf16[256,512]{1,0:T(8,128)(2,1)S(1)}, bf16[256,512]{1,0:T(8,128)(2,1)}, u32[]{:S(2)}) copy-start(bf16[256,512]{1,0:T(8,128)(2,1)} %param.10) | copy-start | bytes 786436
  430.5 484.2 %all-reduce.10.cloned.1.call-start = ((), (), s32[]{:S(2)}) async-start(), calls=%async_computation.2 | async-start | bytes 75497472 | tf_op jit(solution)/shard_map/psum | solution.py:71
  914.7 18.4 %slice-start = ((s8[16777216]{0:T(1024)(128)(4,1)}), s8[4194304]{0:T(1024)(128)(4,1)S(1)}, s32[]{:S(2)}) async-start(s8[16777216]{0:T(1024)(128)(4,1)} %bitcast.113), calls=%async_computation.3 | async-start | bytes 8388608
  919.5 13.6 %slice-start.1 = ((s8[16777216]{0:T(1024)(128)(4,1)}), s8[4194304]{0:T(1024)(128)(4,1)S(1)}, s32[]{:S(2)}) async-start(s8[16777216]{0:T(1024)(128)(4,1)} %bitcast.113), calls=%async_computation.4 | async-start | bytes 8388608
  919.6 13.6 %slice-start.2 = ((s8[16777216]{0:T(1024)(128)(4,1)}), s8[4194304]{0:T(1024)(128)(4,1)S(1)}, s32[]{:S(2)}) async-start(s8[16777216]{0:T(1024)(128)(4,1)} %bitcast.113), calls=%async_computation.5 | async-start | bytes 8388608
  919.6 15.3 %slice-start.3 = ((s8[16777216]{0:T(1024)(128)(4,1)}), s8[4194304]{0:T(1024)(128)(4,1)S(1)}, s32[]{:S(2)}) async-start(s8[16777216]{0:T(1024)(128)(4,1)} %bitcast.113), calls=%async_computation.6 | async-start | bytes 8388608
  934.9 6.4 copy-start.13
  934.9 7.0 copy-start.12
  934.9 7.6 copy-start.11
  934.9 8.2 copy-start.10
  934.9 8.8 copy-start.1
  (5 other events, 13.0 us)
Sparse Core Ops, SparseCore 0:
  120.0 207.0 all-reduce.5
  430.6 44.0 all-reduce.7
  482.6 432.0 all-reduce.9
where the time goes:
time: 960 us; the launch traced here: 952 us
  waiting for transfers between devices  623 us (65%)
  blocking collectives  119 us (12%)
  matrix products  97 us (10%)
  local copies, waits for them, and re-layouts  64.8 us (7%)
  other arithmetic  29 us (3%)
  between operations  18.4 us (2%)
    psum x1, waiting for transfers between devices, local_step(): lax.psum((dw_one, dw_two, dw_three, dg_one, db_one, dg_two, db_two), BATC...  383 us
    psum x1, waiting for transfers between devices, local_step(): corr = lax.psum(part_corr, BATCH_AXIS) / rows_all  206 us
    psum x3, blocking collectives, global_norm(): lax.psum(jnp.stack([jnp.sum(pre, axis=1), jnp.sum(pre * pre, axis=1)]), B...  72.7 us
    psum x2, blocking collectives, global_norm_back(): lax.psum(jnp.stack([jnp.sum(grad_norm, axis=1), jnp.sum(grad_norm * norme...  46.7 us
    psum x1, waiting for transfers between devices, global_norm_back(): lax.psum(jnp.stack([jnp.sum(grad_norm, axis=1), jnp.sum(grad_norm * norme...  33.6 us
    gather x1, local copies, waits for them, and re-layouts, corr_loss(): diag_c = jnp.diagonal(corr)  33.5 us
    unnamed x59, local copies, waits for them, and re-layouts  31.3 us
  transfers between devices with their start and end apart: 3, of which 3 were waited for; matrix products, arithmetic and copies ran while one was open for 6% of the time, Pallas kernels for 0%

commit v1 on v0

v1 whole, which is shorter than its diff:
```python
import functools

import jax
import jax.numpy as jnp
from jax import lax
from jax.experimental import pallas as pl
from jax.experimental.pallas import tpu as pltpu
from jax.sharding import PartitionSpec as P

NORM_EPS = 1e-5
AXIS = 'data'
MESH = pl.DeviceIdType.MESH
F32 = jnp.float32
BF16 = jnp.bfloat16
ONCE = pl.Buffered(1)
VMEM_LIMIT = 60 * 1024 * 1024


def dot(a, b, dims=((1,), (0,))):
    return lax.dot_general(a, b, (dims, ((), ())), preferred_element_type=F32)


def gather_kernel(n, fa_ref, fb_ref, out_ref, local_sem, send_sem, recv_sem):
    me = lax.axis_index(AXIS)
    rows = fa_ref.shape[0]
    barrier = pltpu.get_barrier_semaphore()
    for off in range(1, n):
        pl.semaphore_signal(barrier, inc=1, device_id=(lax.rem(me + off, n),), device_id_type=MESH)
    pl.semaphore_wait(barrier, n - 1)
    dst = out_ref.at[pl.ds(pl.multiple_of(me * rows, rows), rows), :]

    def each(view, src):
        @pl.when(lax.rem(me, 2) == view)
        def _():
            for off in range(1, n):
                if off % 2 == 0:
                    remote(src, off).start()
            pltpu.make_async_copy(src, dst, local_sem).start()

        @pl.when(lax.rem(me, 2) == 1 - view)
        def _():
            for off in range(1, n):
                if off % 2 == 1:
                    remote(src, off).start()

    def remote(src, off):
        return pltpu.make_async_remote_copy(
            src_ref=src, dst_ref=dst, send_sem=send_sem.at[off], recv_sem=recv_sem.at[off],
            device_id=(lax.rem(me + off, n),), device_id_type=MESH)

    each(0, fa_ref)
    each(1, fb_ref)
    pltpu.make_async_copy(fa_ref, dst, local_sem).wait()
    for off in range(1, n):
        remote(fa_ref, off).wait()


def gather_view(fa, fb, n):
    rows, width = fa.shape
    return pl.pallas_call(
        functools.partial(gather_kernel, n),
        out_shape=jax.ShapeDtypeStruct((rows * n, width), fa.dtype),
        in_specs=[pl.BlockSpec(memory_space=pltpu.VMEM)] * 2,
        out_specs=pl.BlockSpec(memory_space=pltpu.VMEM),
        scratch_shapes=[pltpu.SemaphoreType.DMA, pltpu.SemaphoreType.DMA((n,)), pltpu.SemaphoreType.DMA((n,))],
        compiler_params=pltpu.CompilerParams(collective_id=0, has_side_effects=True),
        name='gather_view',
    )(fa, fb)


def fwd_kernel(rows, tile, affine, x_ref, w_ref, g_ref, b_ref, norm_ref, inv_ref, act_ref):
    total = jnp.zeros((1, w_ref.shape[1]), F32)
    square = jnp.zeros((1, w_ref.shape[1]), F32)
    for r in range(0, rows, tile):
        pre = dot(x_ref[r:r + tile, :], w_ref[...])
        norm_ref[r:r + tile, :] = pre
        total += jnp.sum(pre, axis=0, keepdims=True)
        square += jnp.sum(pre * pre, axis=0, keepdims=True)
    mean = total / rows
    inv = lax.rsqrt(square / rows - mean * mean + NORM_EPS)
    inv_ref[...] = inv
    for r in range(0, rows, tile):
        norm = (norm_ref[r:r + tile, :] - mean) * inv
        norm_ref[r:r + tile, :] = norm
        if affine:
            norm = jnp.maximum(norm * g_ref[...] + b_ref[...], 0.0)
        act_ref[r:r + tile, :] = norm.astype(BF16)


def forward_layer(x, w, g, b, affine, bn=256, tile=512):
    rows, k = x.shape
    d = w.shape[1]
    col = pl.BlockSpec((1, bn), lambda j: (0, j))
    return pl.pallas_call(
        functools.partial(fwd_kernel, rows, tile, affine),
        grid=(d // bn,),
        in_specs=[pl.BlockSpec((rows, k), lambda j: (0, 0), pipeline_mode=ONCE), pl.BlockSpec((k, bn), lambda j: (0, j)), col, col],
        out_specs=[pl.BlockSpec((rows, bn), lambda j: (0, j)), col, pl.BlockSpec((rows, bn), lambda j: (0, j))],
        out_shape=[jax.ShapeDtypeStruct((rows, d), F32), jax.ShapeDtypeStruct((1, d), F32), jax.ShapeDtypeStruct((rows, d), BF16)],
        compiler_params=pltpu.CompilerParams(vmem_limit_bytes=VMEM_LIMIT),
        cost_estimate=pl.CostEstimate(flops=2 * rows * k * d, bytes_accessed=rows * d * 6 + rows * k * 2, transcendentals=0),
        name='forward_layer',
    )(x, w, g, b)


def loss_kernel(rows, tile, lam_ref, own_ref, other_ref, norm_ref, inv_ref, loss_ref, out_ref, grad, dn):
    j = pl.program_id(0)
    bn = own_ref.shape[1]
    d = other_ref.shape[1]
    lam = lam_ref[0, 0]
    own = own_ref[...]
    loss = jnp.zeros((1, tile), F32)
    for c in range(0, d, tile):
        corr = dot(own, other_ref[:, c:c + tile], ((0,), (0,))) * (1.0 / rows)
        row_id = lax.broadcasted_iota(jnp.int32, (bn, tile), 0) + j * bn
        col_id = lax.broadcasted_iota(jnp.int32, (bn, tile), 1) + c
        diag = row_id == col_id
        loss += jnp.sum(jnp.where(diag, (1.0 - corr) * (1.0 - corr), lam * (corr * corr)), axis=0, keepdims=True)
        grad[:, c:c + tile] = jnp.where(diag, -2.0 * (1.0 - corr), (2.0 * lam) * corr).astype(BF16)

    @pl.when(j == 0)
    def _():
        loss_ref[...] = jnp.zeros_like(loss_ref)

    loss_ref[...] += loss
    total = jnp.zeros((1, bn), F32)
    cross = jnp.zeros((1, bn), F32)
    for r in range(0, rows, tile):
        part = dot(other_ref[r:r + tile, :], grad[...], ((1,), (1,))) * (1.0 / rows)
        dn[r:r + tile, :] = part
        total += jnp.sum(part, axis=0, keepdims=True)
        cross += jnp.sum(part * norm_ref[r:r + tile, :], axis=0, keepdims=True)
    total, cross = total / rows, cross / rows
    for r in range(0, rows, tile):
        out_ref[r:r + tile, :] = (inv_ref[...] * (dn[r:r + tile, :] - total - norm_ref[r:r + tile, :] * cross)).astype(BF16)


def loss_layer(own, other, norm, inv, lam, bn=256, tile=512):
    rows, d = own.shape
    col = pl.BlockSpec((1, bn), lambda j: (0, j))
    blk = pl.BlockSpec((rows, bn), lambda j: (0, j))
    return pl.pallas_call(
        functools.partial(loss_kernel, rows, tile),
        grid=(d // bn,),
        in_specs=[pl.BlockSpec(memory_space=pltpu.SMEM), blk, pl.BlockSpec((rows, d), lambda j: (0, 0), pipeline_mode=ONCE), blk, col],
        out_specs=[pl.BlockSpec((1, tile), lambda j: (0, 0)), blk],
        out_shape=[jax.ShapeDtypeStruct((1, tile), F32), jax.ShapeDtypeStruct((rows, d), BF16)],
        scratch_shapes=[pltpu.VMEM((bn, d), BF16), pltpu.VMEM((rows, bn), F32)],
        compiler_params=pltpu.CompilerParams(vmem_limit_bytes=VMEM_LIMIT),
        cost_estimate=pl.CostEstimate(flops=4 * rows * d * d, bytes_accessed=rows * d * 10, transcendentals=0),
        name='loss_layer',
    )(lam, own, other, norm, inv)


def bwd_kernel(rows, tile, x_ref, w_ref, norm_ref, inv_ref, g_ref, b_ref, out_ref, dg_ref, db_ref, da):
    total = jnp.zeros((1, w_ref.shape[0]), F32)
    cross = jnp.zeros((1, w_ref.shape[0]), F32)
    g = g_ref[...]
    for r in range(0, rows, tile):
        part = dot(x_ref[r:r + tile, :], w_ref[...], ((1,), (1,)))
        norm = norm_ref[r:r + tile, :]
        part = jnp.where(norm * g + b_ref[...] > 0.0, part, 0.0)
        da[r:r + tile, :] = part
        total += jnp.sum(part, axis=0, keepdims=True)
        cross += jnp.sum(part * norm, axis=0, keepdims=True)
    dg_ref[...] = cross
    db_ref[...] = total
    total, cross = total * g / rows, cross * g / rows
    for r in range(0, rows, tile):
        out_ref[r:r + tile, :] = (inv_ref[...] * (da[r:r + tile, :] * g - total - norm_ref[r:r + tile, :] * cross)).astype(BF16)


def backward_layer(x, w, norm, inv, g, b, bn=256, tile=512):
    rows, k = x.shape
    d = w.shape[0]
    col = pl.BlockSpec((1, bn), lambda j: (0, j))
    blk = pl.BlockSpec((rows, bn), lambda j: (0, j))
    return pl.pallas_call(
        functools.partial(bwd_kernel, rows, tile),
        grid=(d // bn,),
        in_specs=[pl.BlockSpec((rows, k), lambda j: (0, 0), pipeline_mode=ONCE), pl.BlockSpec((bn, k), lambda j: (j, 0)), blk, col, col, col],
        out_specs=[blk, col, col],
        out_shape=[jax.ShapeDtypeStruct((rows, d), BF16), jax.ShapeDtypeStruct((1, d), F32), jax.ShapeDtypeStruct((1, d), F32)],
        scratch_shapes=[pltpu.VMEM((rows, bn), F32)],
        compiler_params=pltpu.CompilerParams(vmem_limit_bytes=VMEM_LIMIT),
        cost_estimate=pl.CostEstimate(flops=2 * rows * k * d, bytes_accessed=rows * d * 6 + rows * k * 2, transcendentals=0),
        name='backward_layer',
    )(x, w, norm, inv, g, b)


def dw_kernel(tile, x_ref, y_ref, out_ref):
    x = x_ref[...]
    for c in range(0, y_ref.shape[1], tile):
        out_ref[:, c:c + tile] = dot(x, y_ref[:, c:c + tile], ((0,), (0,)))


def weight_grad(x, y, bm=256, tile=512):
    rows, k = x.shape
    d = y.shape[1]
    return pl.pallas_call(
        functools.partial(dw_kernel, tile),
        grid=(k // bm,),
        in_specs=[pl.BlockSpec((rows, bm), lambda j: (0, j)), pl.BlockSpec((rows, d), lambda j: (0, 0), pipeline_mode=ONCE)],
        out_specs=pl.BlockSpec((bm, d), lambda j: (j, 0)),
        out_shape=jax.ShapeDtypeStruct((k, d), F32),
        compiler_params=pltpu.CompilerParams(vmem_limit_bytes=VMEM_LIMIT),
        cost_estimate=pl.CostEstimate(flops=2 * rows * k * d, bytes_accessed=k * d * 4 + rows * (k + d) * 2, transcendentals=0),
        name='weight_grad',
    )(x, y)


def solution(mesh):
    n = mesh.shape[AXIS]
    pair = [(i, i + 1 - 2 * (i % 2)) for i in range(n)]

    def swap(x):
        return lax.ppermute(x, AXIS, pair)

    def local_step(feat_a, feat_b, w_one, w_two, w_three, g_one, b_one, g_two, b_two, lam_off):
        width = w_two.shape[0]
        g1, b1, g2, b2 = (v.reshape(1, width) for v in (g_one, b_one, g_two, b_two))
        x = gather_view(feat_a, feat_b, n)
        norm1, inv1, act1 = forward_layer(x, w_one, g1, b1, True)
        norm2, inv2, act2 = forward_layer(act1, w_two, g2, b2, True)
        norm3, inv3, emb = forward_layer(act2, w_three, g2, b2, False)
        other = swap(emb)
        loss, d_out = loss_layer(emb, other, norm3, inv3, lam_off.reshape(1, 1))
        dw3 = weight_grad(act2, d_out)
        dw3_other = swap(dw3)
        d_pre2, dg2, db2 = backward_layer(d_out, w_three, norm2, inv2, g2, b2)
        dw2 = weight_grad(act1, d_pre2)
        dw2_other = swap(dw2)
        d_pre1, dg1, db1 = backward_layer(d_pre2, w_two, norm1, inv1, g1, b1)
        dw1 = weight_grad(x, d_pre1)
        dw1_other = swap(dw1)
        small = jnp.concatenate([dg1, db1, dg2, db2, loss], axis=1)
        small = small + swap(small)
        dg1, db1, dg2, db2 = (small[0, i * width:(i + 1) * width] for i in range(4))
        loss_val = jnp.sum(small[0, 4 * width:]) * 0.5
        return (loss_val, dw1 + dw1_other, dw2 + dw2_other, dw3 + dw3_other, dg1, db1, dg2, db2)

    row_spec = P(AXIS, None)
    return jax.shard_map(local_step, mesh=mesh, in_specs=(row_spec, row_spec) + (P(),) * 8, out_specs=(P(),) * 8, check_vma=False)
```

time: 960 us -> 353 us (0.37)
  waiting for transfers between devices: 623 us -> 18.8 us
  Pallas kernels: 0 us -> 288 us
  blocking collectives: 119 us -> 0 us
  matrix products: 97 us -> 0 us
  local copies, waits for them, and re-layouts: 64.8 us -> 2.88 us
  between operations: 18.4 us -> 3.18 us
    psum x3 -> x0, waiting for transfers between devices: 623 us -> none  [the longest x1 383 us: local_step(): lax.psum((dw_one, dw_two, dw_three, dg_one, db_one, dg_two, db_two), BATC...]
    pallas_call x0 -> x10, Pallas kernels: none -> 288 us  [the longest x3 80.8 us: forward_layer(): pl.pallas_call(functools.partial(fwd_kernel, rows, tile, affine), grid=(d...]
    psum x5 -> x0, blocking collectives: 119 us -> none  [the longest x3 72.7 us: global_norm(): lax.psum(jnp.stack([jnp.sum(pre, axis=1), jnp.sum(pre * pre, axis=1)]), B...]
    dot_general x11 -> x0, matrix products: 97 us -> none  [the longest x1 11.5 us: local_step(): jnp.einsum('wof,ef->woe', grad_pre_two, w_two, preferred_element_type=jnp...]
    add x0 -> x4, other arithmetic: none -> 37.1 us  [the longest x1 18.1 us: local_step(): dw3 + dw3_other]
    gather x1 -> x0, local copies, waits for them, and re-layouts: 33.5 us -> none  [corr_loss(): diag_c = jnp.diagonal(corr)]
    unnamed x59 -> x22, local copies, waits for them, and re-layouts: 31.3 us -> 2.25 us
    ppermute x0 -> x5, waiting for transfers between devices: none -> 18.8 us  [swap(): return lax.ppermute(x, AXIS, pair)]
  transfers between devices with their start and end apart: 3 -> 5, of which waited for: 3 -> 2; matrix products, arithmetic and copies ran while one was open for 6% -> 7% of each run, Pallas kernels for 0% -> 28%
where the time goes in v1:
time: 353 us
  Pallas kernels  288 us (82%)
  other arithmetic  37.7 us (11%)
  waiting for transfers between devices  18.8 us (5%)
    pallas_call x3, Pallas kernels, forward_layer(): pl.pallas_call(functools.partial(fwd_kernel, rows, tile, affine), grid=(d...  80.8 us
    pallas_call x2, Pallas kernels, backward_layer(): pl.pallas_call(functools.partial(bwd_kernel, rows, tile), grid=(d // bn,)...  64.2 us
    pallas_call x3, Pallas kernels, weight_grad(): pl.pallas_call(functools.partial(dw_kernel, tile), grid=(k // bm,), in_sp...  57.9 us
    pallas_call x1, Pallas kernels, loss_layer(): pl.pallas_call(functools.partial(loss_kernel, rows, tile), grid=(d // bn,...  55.4 us
    pallas_call x1, Pallas kernels, gather_view(): pl.pallas_call(functools.partial(gather_kernel, n), out_shape=jax.ShapeDt...  30 us
    ppermute x5, waiting for transfers between devices, swap(): return lax.ppermute(x, AXIS, pair)  18.8 us
    add x1, other arithmetic, local_step(): dw3 + dw3_other  18.1 us
    add x1, other arithmetic, local_step(): dw2 + dw2_other  12.3 us
  transfers between devices with their start and end apart: 5, of which 2 were waited for; matrix products, arithmetic and copies ran while one was open for 7% of the time, Pallas kernels for 28%

profile of v1, /device:TPU:0, one launch (start us, length us, event | category | flops | bytes accessed | tf_op | source)
XLA Modules:
  0.0 352.5 jit_solution(5038070861586008062)
XLA Ops:
  0.6 30.0 %gather_view.1.x_ref = bf16[2048,512]{1,0:T(8,128)(2,1)} custom-call(bf16[256,512]{1,0:T(8,128)(2,1)} %fa_ref.1, bf16[256,512]{1,0:T(8,128)(2,1)} %fb_ref.1), custom_call_target="tpu_custom_call" | custom-call | tf_op jit(solution)/shard_map/gather_view/pallas_call | solution.py:60
  30.7 17.3 %forward_layer.3 = (f32[2048,2048]{1,0:T(8,128)}, f32[1,2048]{1,0:T(1,128)}, bf16[2048,2048]{1,0:T(8,128)(2,1)}) custom-call(bf16[2048,512]{1,0:T(8,128)(2,1)} %gather_view.1.x_ref, bf16[512,2048]{1,0:T(8,128)(2,1)} %w_ref.5, f32[1,2048]{1,0:T(1,128)} %bitcast.22, f32[1,2048]{1,0:T(1,128)} %bitcast.24), custom_call_target="tpu_custom_call" | custom-call | flops 4294967296 | bytes 27262976 | tf_op jit(solution)/shard_map/forward_layer/pallas_call | solution.py:94
  47.9 33.0 %forward_layer.4 = (f32[2048,2048]{1,0:T(8,128)}, f32[1,2048]{1,0:T(1,128)}, bf16[2048,2048]{1,0:T(8,128)(2,1)}) custom-call(bf16[2048,2048]{1,0:T(8,128)(2,1)} %get-tuple-element.25.x_ref, bf16[2048,2048]{1,0:T(8,128)(2,1)} %w_ref.9, f32[1,2048]{1,0:T(1,128)} %bitcast.16, f32[1,2048]{1,0:T(1,128)} %bitcast.19), custom_call_target="tpu_custom_call" | custom-call | flops 17179869184 | bytes 33554432 | tf_op jit(solution)/shard_map/forward_layer/pallas_call | solution.py:94
  80.9 30.5 %forward_layer.5 = (f32[2048,2048]{1,0:T(8,128)}, f32[1,2048]{1,0:T(1,128)}, bf16[2048,2048]{1,0:T(8,128)(2,1)}) custom-call(bf16[2048,2048]{1,0:T(8,128)(2,1)} %get-tuple-element.26.x_ref, bf16[2048,2048]{1,0:T(8,128)(2,1)} %w_ref.8, f32[1,2048]{1,0:T(1,128)} %bitcast.17, f32[1,2048]{1,0:T(1,128)} %bitcast.20), custom_call_target="tpu_custom_call" | custom-call | flops 17179869184 | bytes 33554432 | tf_op jit(solution)/shard_map/forward_layer/pallas_call | solution.py:94
  111.5 0.6 collective-permute-start
  112.8 12.1 %collective-permute-done.other_ref = bf16[2048,2048]{1,0:T(8,128)(2,1)} collective-permute-done((bf16[2048,2048]{1,0:T(8,128)(2,1)}, bf16[2048,2048]{1,0:T(8,128)(2,1)}, u32[]{:S(2)}, u32[]{:S(2)}) %collective-permute-start) | collective-permute-done | bytes 8388640 | tf_op jit(solution)/shard_map/ppermute | solution.py:217
  124.9 55.4 %loss_layer.1 = (f32[1,512]{1,0:T(1,128)}, bf16[2048,2048]{1,0:T(8,128)(2,1)}) custom-call(f32[1,1]{1,0:T(1,128)} %bitcast.9.lam_ref, bf16[2048,2048]{1,0:T(8,128)(2,1)} %get-tuple-element.27.own_ref, bf16[2048,2048]{1,0:T(8,128)(2,1)} %collective-permute-done.other_ref, f32[2048,2048]{1,0:T(8,128)} %get-tuple-element.28.norm_ref, ...), custom_call_target="tpu_custom_call" | custom-call | flops 34359738368 | bytes 41943040 | tf_op jit(solution)/shard_map/loss_layer/pallas_call | solution.py:142
  180.3 24.0 %weight_grad.5 = f32[2048,2048]{1,0:T(8,128)} custom-call(bf16[2048,2048]{1,0:T(8,128)(2,1)} %get-tuple-element.26.x_ref, bf16[2048,2048]{1,0:T(8,128)(2,1)} %get-tuple-element.30.x_ref.y_ref), custom_call_target="tpu_custom_call" | custom-call | flops 17179869184 | bytes 33554432 | tf_op jit(solution)/shard_map/weight_grad/pallas_call | solution.py:200
  204.3 0.3 collective-permute-start.4
  204.6 32.1 %backward_layer.2 = (bf16[2048,2048]{1,0:T(8,128)(2,1)}, f32[1,2048]{1,0:T(1,128)}, f32[1,2048]{1,0:T(1,128)}) custom-call(bf16[2048,2048]{1,0:T(8,128)(2,1)} %get-tuple-element.30.x_ref.y_ref, bf16[2048,2048]{1,0:T(8,128)(2,1)} %w_ref.8, f32[2048,2048]{1,0:T(8,128)} %get-tuple-element.31.norm_ref, f32[1,2048]{1,0:T(1,128)} %get-tuple-element.32.inv_ref, ...), custom_call_target="tpu_custom_call" | custom-call | flops 17179869184 | bytes 33554432 | tf_op jit(solution)/shard_map/backward_layer/pallas_call | solution.py:178
  236.8 24.1 %weight_grad.4 = f32[2048,2048]{1,0:T(8,128)} custom-call(bf16[2048,2048]{1,0:T(8,128)(2,1)} %get-tuple-element.25.x_ref, bf16[2048,2048]{1,0:T(8,128)(2,1)} %get-tuple-element.33.x_ref.y_ref), custom_call_target="tpu_custom_call" | custom-call | flops 17179869184 | bytes 33554432 | tf_op jit(solution)/shard_map/weight_grad/pallas_call | solution.py:200
  260.8 0.1 collective-permute-start.3
  261.0 32.1 %backward_layer.3 = (bf16[2048,2048]{1,0:T(8,128)(2,1)}, f32[1,2048]{1,0:T(1,128)}, f32[1,2048]{1,0:T(1,128)}) custom-call(bf16[2048,2048]{1,0:T(8,128)(2,1)} %get-tuple-element.33.x_ref.y_ref, bf16[2048,2048]{1,0:T(8,128)(2,1)} %w_ref.9, f32[2048,2048]{1,0:T(8,128)} %get-tuple-element.34.norm_ref, f32[1,2048]{1,0:T(1,128)} %get-tuple-element.35.inv_ref, ...), custom_call_target="tpu_custom_call" | custom-call | flops 17179869184 | bytes 33554432 | tf_op jit(solution)/shard_map/backward_layer/pallas_call | solution.py:178
  293.1 9.8 %weight_grad.3 = f32[512,2048]{1,0:T(8,128)} custom-call(bf16[2048,512]{1,0:T(8,128)(2,1)} %gather_view.1.x_ref, bf16[2048,2048]{1,0:T(8,128)(2,1)} %get-tuple-element.41.y_ref), custom_call_target="tpu_custom_call" | custom-call | flops 4294967296 | bytes 14680064 | tf_op jit(solution)/shard_map/weight_grad/pallas_call | solution.py:200
  302.9 0.4 collective-permute-start.2
  303.4 0.1 collective-permute-start.1
  303.5 6.7 %collective-permute-done.1 = f32[1,8704]{1,0:T(1,128)S(1)} collective-permute-done((f32[1,8704]{1,0:T(1,128)S(1)}, f32[1,8704]{1,0:T(1,128)S(1)}, u32[]{:S(2)}, u32[]{:S(2)}) %collective-permute-start.1) | collective-permute-done | bytes 34848 | tf_op jit(solution)/shard_map/ppermute | solution.py:217
  310.2 0.6 slice_reduce_fusion
  311.5 0.6 fusion
  312.1 6.7 %add.13 = f32[512,2048]{1,0:T(8,128)} add(f32[512,2048]{1,0:T(8,128)} %weight_grad.3, f32[512,2048]{1,0:T(8,128)} %collective-permute-done.2) | non-fusion elementwise | flops 1048576 | bytes 12582912 | tf_op jit(solution)/shard_map/add | solution.py:240
  318.8 18.1 %add.15 = f32[2048,2048]{1,0:T(8,128)} add(f32[2048,2048]{1,0:T(8,128)} %weight_grad.5, f32[2048,2048]{1,0:T(8,128)} %collective-permute-done.4) | non-fusion elementwise | flops 4194304 | bytes 50331648 | tf_op jit(solution)/shard_map/add | solution.py:240
  336.9 1.0 slice-done.2
  337.9 1.2 slice-done.3
  339.1 12.3 %add.14 = f32[2048,2048]{1,0:T(8,128)} add(f32[2048,2048]{1,0:T(8,128)S(1)} %bitcast.11, f32[2048,2048]{1,0:T(8,128)} %collective-permute-done.3) | non-fusion elementwise | flops 4194304 | bytes 50331648 | tf_op jit(solution)/shard_map/add | solution.py:240
  (26 shorter events, 0.1 us)
Async XLA Ops:
  111.5 13.4 %collective-permute-start = (bf16[2048,2048]{1,0:T(8,128)(2,1)}, bf16[2048,2048]{1,0:T(8,128)(2,1)}, u32[]{:S(2)}, u32[]{:S(2)}) collective-permute-start(bf16[2048,2048]{1,0:T(8,128)(2,1)} %get-tuple-element.27.own_ref), channel_id=1, source_target_pairs={{0,1},{1,0},{2,3},{3,2},{4,5},{5,4},{6,7},{7,6}} | collective-permute-start | bytes 25165832 | tf_op jit(solution)/shard_map/ppermute | solution.py:217
  204.3 114.5 %collective-permute-start.4 = (f32[2048,2048]{1,0:T(8,128)}, f32[2048,2048]{1,0:T(8,128)}, u32[]{:S(2)}, u32[]{:S(2)}) collective-permute-start(f32[2048,2048]{1,0:T(8,128)} %weight_grad.5), channel_id=1, source_target_pairs={{0,1},{1,0},{2,3},{3,2},{4,5},{5,4},{6,7},{7,6}} | collective-permute-start | bytes 50331656 | tf_op jit(solution)/shard_map/ppermute | solution.py:217
  260.8 76.1 %collective-permute-start.3 = (f32[2048,2048]{1,0:T(8,128)}, f32[2048,2048]{1,0:T(8,128)}, u32[]{:S(2)}, u32[]{:S(2)}) collective-permute-start(f32[2048,2048]{1,0:T(8,128)} %weight_grad.4), channel_id=1, source_target_pairs={{0,1},{1,0},{2,3},{3,2},{4,5},{5,4},{6,7},{7,6}} | collective-permute-start | bytes 50331656 | tf_op jit(solution)/shard_map/ppermute | solution.py:217
  293.1 10.3 %copy-start.3 = (f32[1,2048]{1,0:T(1,128)S(1)}, f32[1,2048]{1,0:T(1,128)}, u32[]{:S(2)}) copy-start(f32[1,2048]{1,0:T(1,128)} %get-tuple-element.36) | copy-start | bytes 24580
  293.1 10.3 %copy-start.2 = (f32[1,2048]{1,0:T(1,128)S(1)}, f32[1,2048]{1,0:T(1,128)}, u32[]{:S(2)}) copy-start(f32[1,2048]{1,0:T(1,128)} %get-tuple-element.37) | copy-start | bytes 24580
  293.1 10.3 %copy-start.1 = (f32[1,2048]{1,0:T(1,128)S(1)}, f32[1,2048]{1,0:T(1,128)}, u32[]{:S(2)}) copy-start(f32[1,2048]{1,0:T(1,128)} %get-tuple-element.38) | copy-start | bytes 24580
  293.1 10.3 %copy-start = (f32[1,2048]{1,0:T(1,128)S(1)}, f32[1,2048]{1,0:T(1,128)}, u32[]{:S(2)}) copy-start(f32[1,2048]{1,0:T(1,128)} %get-tuple-element.39) | copy-start | bytes 24580
  293.1 10.3 %copy-start.4 = (f32[1,512]{1,0:T(1,128)S(1)}, f32[1,512]{1,0:T(1,128)}, u32[]{:S(2)}) copy-start(f32[1,512]{1,0:T(1,128)} %get-tuple-element.40) | copy-start | bytes 6148
  302.9 9.2 %collective-permute-start.2 = (f32[512,2048]{1,0:T(8,128)}, f32[512,2048]{1,0:T(8,128)}, u32[]{:S(2)}, u32[]{:S(2)}) collective-permute-start(f32[512,2048]{1,0:T(8,128)} %weight_grad.3), channel_id=1, source_target_pairs={{0,1},{1,0},{2,3},{3,2},{4,5},{5,4},{6,7},{7,6}} | collective-permute-start | bytes 12582920 | tf_op jit(solution)/shard_map/ppermute | solution.py:217
  303.4 6.8 %collective-permute-start.1 = (f32[1,8704]{1,0:T(1,128)S(1)}, f32[1,8704]{1,0:T(1,128)S(1)}, u32[]{:S(2)}, u32[]{:S(2)}) collective-permute-start(f32[1,8704]{1,0:T(1,128)S(1)} %constant_dynamic-update-slice_fusion), channel_id=1, source_target_pairs={{0,1},{1,0},{2,3},{3,2},{4,5},{5,4},{6,7},{7,6}} | collective-permute-start | bytes 104456 | tf_op jit(solution)/shard_map/ppermute | solution.py:217
  312.1 24.8 %slice-start = ((s8[16777216]{0:T(1024)(128)(4,1)}), s8[4194304]{0:T(1024)(128)(4,1)S(1)}, s32[]{:S(2)}) async-start(s8[16777216]{0:T(1024)(128)(4,1)} %bitcast.10), calls=%async_computation | async-start | bytes 8388608
  318.8 18.1 %slice-start.1 = ((s8[16777216]{0:T(1024)(128)(4,1)}), s8[4194304]{0:T(1024)(128)(4,1)S(1)}, s32[]{:S(2)}) async-start(s8[16777216]{0:T(1024)(128)(4,1)} %bitcast.10), calls=%async_computation.1 | async-start | bytes 8388608
  318.8 19.1 %slice-start.2 = ((s8[16777216]{0:T(1024)(128)(4,1)}), s8[4194304]{0:T(1024)(128)(4,1)S(1)}, s32[]{:S(2)}) async-start(s8[16777216]{0:T(1024)(128)(4,1)} %bitcast.10), calls=%async_computation.2 | async-start | bytes 8388608
  318.8 20.3 %slice-start.3 = ((s8[16777216]{0:T(1024)(128)(4,1)}), s8[4194304]{0:T(1024)(128)(4,1)S(1)}, s32[]{:S(2)}) async-start(s8[16777216]{0:T(1024)(128)(4,1)} %bitcast.10), calls=%async_computation.3 | async-start | bytes 8388608

commit v2 on v1

--- a/solution.py
+++ b/solution.py
@@ -14,93 +14,171 @@
 BF16 = jnp.bfloat16
 ONCE = pl.Buffered(1)
 VMEM_LIMIT = 60 * 1024 * 1024
+TILE = 256
+CHUNK = 64
+
+
+def fold(v):
+    return jnp.sum(v.reshape(v.shape[0] // 8, 8, v.shape[1]), axis=0)
 
 
 def dot(a, b, dims=((1,), (0,))):
     return lax.dot_general(a, b, (dims, ((), ())), preferred_element_type=F32)
 
 
-def gather_kernel(n, fa_ref, fb_ref, out_ref, local_sem, send_sem, recv_sem):
+def forward_kernel(nb, rows, fa_ref, fb_ref, w1_ref, w2_ref, w3_ref, g1_ref, b1_ref, g2_ref, b2_ref,
+                   n1_ref, n2_ref, n3_ref, i1_ref, i2_ref, i3_ref, x_hbm, act1_hbm, act2_hbm, emb_hbm, other_hbm,
+                   xs, bufa, bufb, acc, copy_sem, feat_sem, send_sem, recv_sem, esend_sem, erecv_sem):
+    j = pl.program_id(0)
     me = lax.axis_index(AXIS)
-    rows = fa_ref.shape[0]
-    barrier = pltpu.get_barrier_semaphore()
-    for off in range(1, n):
-        pl.semaphore_signal(barrier, inc=1, device_id=(lax.rem(me + off, n),), device_id_type=MESH)
-    pl.semaphore_wait(barrier, n - 1)
-    dst = out_ref.at[pl.ds(pl.multiple_of(me * rows, rows), rows), :]
-
-    def each(view, src):
-        @pl.when(lax.rem(me, 2) == view)
-        def _():
-            for off in range(1, n):
-                if off % 2 == 0:
-                    remote(src, off).start()
-            pltpu.make_async_copy(src, dst, local_sem).start()
-
-        @pl.when(lax.rem(me, 2) == 1 - view)
-        def _():
-            for off in range(1, n):
-                if off % 2 == 1:
-                    remote(src, off).start()
-
-    def remote(src, off):
-        return pltpu.make_async_remote_copy(
-            src_ref=src, dst_ref=dst, send_sem=send_sem.at[off], recv_sem=recv_sem.at[off],
-            device_id=(lax.rem(me + off, n),), device_id_type=MESH)
-
-    each(0, fa_ref)
-    each(1, fb_ref)
-    pltpu.make_async_copy(fa_ref, dst, local_sem).wait()
-    for off in range(1, n):
-        remote(fa_ref, off).wait()
-
-
-def gather_view(fa, fb, n):
-    rows, width = fa.shape
+    core = lax.rem(me, 2)
+    chip = me // 2
+    x_pos, y_pos = lax.rem(chip, 2), chip // 2
+    partner = me + 1 - 2 * core
+    x_chip, y_chip = chip + 1 - 2 * x_pos, chip + 2 - 4 * y_pos
+    piece = fa_ref.shape[0]
+    bn = acc.shape[1]
+
+    def remote(src, dst, send, recv, dev):
+        return pltpu.make_async_remote_copy(src_ref=src, dst_ref=dst, send_sem=send, recv_sem=recv, device_id=(dev,), device_id_type=MESH)
+
+    def part(dev):
+        return xs.at[pl.ds(pl.multiple_of(dev * piece, piece), piece), :]
+
+    def gather():
+        barrier = pltpu.get_barrier_semaphore()
+        for dev in (partner, 2 * x_chip, 2 * x_chip + 1, 2 * y_chip, 2 * y_chip + 1):
+            pl.semaphore_signal(barrier, inc=1, device_id=(dev,), device_id_type=MESH)
+        pl.semaphore_wait(barrier, 5)
+
+        def sends(mine, mine_src, theirs_src):
+            for view, src in ((mine, mine_src), (1 - mine, theirs_src)):
+                remote(src, part(me), send_sem.at[1 + view], recv_sem.at[1 + mine], 2 * x_chip + view).start()
+                remote(src, part(me), send_sem.at[3 + view], recv_sem.at[3 + mine], 2 * y_chip + view).start()
+            remote(theirs_src, part(me), send_sem.at[0], recv_sem.at[0], partner).start()
+            pltpu.make_async_copy(mine_src, part(me), feat_sem).start()
+
+        pl.when(core == 0)(lambda: sends(0, fa_ref, fb_ref))
+        pl.when(core == 1)(lambda: sends(1, fb_ref, fa_ref))
+        remote(fa_ref, part(2 * x_chip), send_sem.at[1], recv_sem.at[1], me).wait_recv()
+        relay_y = remote(part(2 * x_chip), part(2 * x_chip), send_sem.at[5], recv_sem.at[5], 2 * y_chip + core)
+        relay_y.start()
+        remote(fa_ref, part(2 * y_chip + 1), send_sem.at[4], recv_sem.at[4], me).wait_recv()
+        relay_x = remote(part(2 * y_chip + 1), part(2 * y_chip + 1), send_sem.at[6], recv_sem.at[6], 2 * x_chip + core)
+        relay_x.start()
+        pltpu.make_async_copy(fa_ref, part(me), feat_sem).wait()
+        remote(fa_ref, part(me), send_sem.at[0], recv_sem.at[0], me).wait()
+        remote(fa_ref, part(me), send_sem.at[1], recv_sem.at[2], me).wait()
+        remote(fa_ref, part(me), send_sem.at[2], recv_sem.at[3], me).wait()
+        remote(fa_ref, part(me), send_sem.at[3], recv_sem.at[5], me).wait()
+        remote(fa_ref, part(me), send_sem.at[4], recv_sem.at[6], me).wait()
+        relay_y.wait_send()
+        relay_x.wait_send()
+
+    def fin(layer):
+        norm_ref, inv_ref = ((n1_ref, i1_ref), (n2_ref, i2_ref), (n3_ref, i3_ref))[layer]
+        buf = (bufa, bufb, bufa)[layer]
+        base = pl.multiple_of((j - 1 - layer * nb) * bn, bn)
+        total = jnp.zeros((8, bn), F32)
+        square = jnp.zeros((8, bn), F32)
+        for r in range(0, rows, CHUNK):
+            pre = acc[r:r + CHUNK, :]
+            total += fold(pre)
+            square += fold(pre * pre)
+        mean = jnp.sum(total, axis=0, keepdims=True) / rows
+        inv = lax.rsqrt(jnp.sum(square, axis=0, keepdims=True) / rows - mean * mean + NORM_EPS)
+        inv_ref[...] = inv
+        if layer < 2:
+            g_ref, b_ref = ((g1_ref, b1_ref), (g2_ref, b2_ref))[layer]
+            g, b = g_ref[...], b_ref[...]
+        for r in range(0, rows, CHUNK):
+            norm = (acc[r:r + CHUNK, :] - mean) * inv
+            norm_ref[r:r + CHUNK, :] = norm
+            if layer < 2:
+                norm = jnp.maximum(norm * g + b, 0.0)
+            buf[r:r + CHUNK, pl.ds(base, bn)] = norm.astype(BF16)
+
+    def mm(layer):
+        x_ref, w_ref = ((xs, w1_ref), (bufa, w2_ref), (bufb, w3_ref))[layer]
+        for r in range(0, rows, TILE):
+            acc[r:r + TILE, :] = dot(x_ref[r:r + TILE, :], w_ref[...])
+
+    def out_copy(layer, block):
+        cols = pl.ds(pl.multiple_of(block * bn, bn), bn)
+        src = (bufa, bufb, bufa)[layer].at[:, cols]
+        dst = (act1_hbm, act2_hbm, emb_hbm)[layer].at[:, cols]
+        return pltpu.make_async_copy(src, dst, copy_sem.at[layer * nb + block])
+
+    def emb_copy(block):
+        cols = pl.ds(pl.multiple_of(block * bn, bn), bn)
+        return remote(bufa.at[:, cols], other_hbm.at[:, cols], esend_sem.at[block], erecv_sem.at[block], partner)
+
+    @pl.when(j == 0)
+    def _():
+        gather()
+        pltpu.make_async_copy(xs, x_hbm, feat_sem).start()
+        mm(0)
+
+    for layer in range(3):
+        @pl.when((j >= layer * nb + 2) & (j < (layer + 1) * nb + 2))
+        def _(layer=layer):
+            block = j - 2 - layer * nb
+            out_copy(layer, block).start()
+            if layer == 2:
+                emb_copy(block).start()
+
+        @pl.when((j > layer * nb) & (j < (layer + 1) * nb))
+        def _(layer=layer):
+            fin(layer)
+            mm(layer)
+
+        @pl.when(j == (layer + 1) * nb)
+        def _(layer=layer):
+            if layer == 1:
+                for block in range(nb):
+                    out_copy(0, block).wait()
+            fin(layer)
+            if layer < 2:
+                mm(layer + 1)
+
+    @pl.when(j == 3 * nb + 1)
+    def _():
+        for layer in (1, 2):
+            for block in range(nb):
+                out_copy(layer, block).wait()
+        pltpu.make_async_copy(xs, x_hbm, feat_sem).wait()
+        for block in range(nb):
+            emb_copy(block).wait()
+
+
+def forward(fa, fb, w1, w2, w3, g1, b1, g2, b2, n, bn=256):
+    piece, k = fa.shape
+    rows, d = piece * n, w2.shape[1]
+    nb = d // bn
+
+    def at(layer, delay):
+        return lambda j: (0, jnp.clip(j - layer * nb - delay, 0, nb - 1))
+
+    whole = pl.BlockSpec((piece, k), lambda j: (0, 0), pipeline_mode=ONCE)
+    any_spec = pl.BlockSpec(memory_space=pl.ANY)
+    col = [pl.BlockSpec((1, bn), at(layer, 1)) for layer in range(3)]
+    norm = [pl.BlockSpec((rows, bn), at(layer, 1)) for layer in range(3)]
+    big = jax.ShapeDtypeStruct((rows, d), BF16)
     return pl.pallas_call(
-        functools.partial(gather_kernel, n),
-        out_shape=jax.ShapeDtypeStruct((rows * n, width), fa.dtype),
-        in_specs=[pl.BlockSpec(memory_space=pltpu.VMEM)] * 2,
-        out_specs=pl.BlockSpec(memory_space=pltpu.VMEM),
-        scratch_shapes=[pltpu.SemaphoreType.DMA, pltpu.SemaphoreType.DMA((n,)), pltpu.SemaphoreType.DMA((n,))],
-        compiler_params=pltpu.CompilerParams(collective_id=0, has_side_effects=True),
-        name='gather_view',
-    )(fa, fb)
-
-
-def fwd_kernel(rows, tile, affine, x_ref, w_ref, g_ref, b_ref, norm_ref, inv_ref, act_ref):
-    total = jnp.zeros((1, w_ref.shape[1]), F32)
-    square = jnp.zeros((1, w_ref.shape[1]), F32)
-    for r in range(0, rows, tile):
-        pre = dot(x_ref[r:r + tile, :], w_ref[...])
-        norm_ref[r:r + tile, :] = pre
-        total += jnp.sum(pre, axis=0, keepdims=True)
-        square += jnp.sum(pre * pre, axis=0, keepdims=True)
-    mean = total / rows
-    inv = lax.rsqrt(square / rows - mean * mean + NORM_EPS)
-    inv_ref[...] = inv
-    for r in range(0, rows, tile):
-        norm = (norm_ref[r:r + tile, :] - mean) * inv
-        norm_ref[r:r + tile, :] = norm
-        if affine:
-            norm = jnp.maximum(norm * g_ref[...] + b_ref[...], 0.0)
-        act_ref[r:r + tile, :] = norm.astype(BF16)
-
-
-def forward_layer(x, w, g, b, affine, bn=256, tile=512):
-    rows, k = x.shape
-    d = w.shape[1]
-    col = pl.BlockSpec((1, bn), lambda j: (0, j))
-    return pl.pallas_call(
-        functools.partial(fwd_kernel, rows, tile, affine),
-        grid=(d // bn,),
-        in_specs=[pl.BlockSpec((rows, k), lambda j: (0, 0), pipeline_mode=ONCE), pl.BlockSpec((k, bn), lambda j: (0, j)), col, col],
-        out_specs=[pl.BlockSpec((rows, bn), lambda j: (0, j)), col, pl.BlockSpec((rows, bn), lambda j: (0, j))],
-        out_shape=[jax.ShapeDtypeStruct((rows, d), F32), jax.ShapeDtypeStruct((1, d), F32), jax.ShapeDtypeStruct((rows, d), BF16)],
-        compiler_params=pltpu.CompilerParams(vmem_limit_bytes=VMEM_LIMIT),
-        cost_estimate=pl.CostEstimate(flops=2 * rows * k * d, bytes_accessed=rows * d * 6 + rows * k * 2, transcendentals=0),
-        name='forward_layer',
-    )(x, w, g, b)
+        functools.partial(forward_kernel, nb, rows),
+        grid=(3 * nb + 2,),
+        in_specs=[whole, whole, pl.BlockSpec((k, bn), at(0, 0)), pl.BlockSpec((d, bn), at(1, 0)), pl.BlockSpec((d, bn), at(2, 0)),
+                  col[0], col[0], col[1], col[1]],
+        out_specs=norm + col + [any_spec] * 5,
+        out_shape=[jax.ShapeDtypeStruct((rows, d), F32)] * 3 + [jax.ShapeDtypeStruct((1, d), F32)] * 3
+        + [jax.ShapeDtypeStruct((rows, k), BF16)] + [big] * 4,
+        scratch_shapes=[pltpu.VMEM((rows, k), BF16), pltpu.VMEM((rows, d), BF16), pltpu.VMEM((rows, d), BF16), pltpu.VMEM((rows, bn), F32),
+                        pltpu.SemaphoreType.DMA((3 * nb,)), pltpu.SemaphoreType.DMA, pltpu.SemaphoreType.DMA((7,)), pltpu.SemaphoreType.DMA((7,)),
+                        pltpu.SemaphoreType.DMA((nb,)), pltpu.SemaphoreType.DMA((nb,))],
+        compiler_params=pltpu.CompilerParams(collective_id=0, has_side_effects=True, vmem_limit_bytes=VMEM_LIMIT),
+        cost_estimate=pl.CostEstimate(flops=2 * rows * d * (k + 2 * d), bytes_accessed=rows * d * 20, transcendentals=0),
+        name='forward',
+    )(fa, fb, w1, w2, w3, g1, b1, g2, b2)
 
 
 def loss_kernel(rows, tile, lam_ref, own_ref, other_ref, norm_ref, inv_ref, loss_ref, out_ref, grad, dn):
@@ -219,11 +297,8 @@
     def local_step(feat_a, feat_b, w_one, w_two, w_three, g_one, b_one, g_two, b_two, lam_off):
         width = w_two.shape[0]
         g1, b1, g2, b2 = (v.reshape(1, width) for v in (g_one, b_one, g_two, b_two))
-        x = gather_view(feat_a, feat_b, n)
-        norm1, inv1, act1 = forward_layer(x, w_one, g1, b1, True)
-        norm2, inv2, act2 = forward_layer(act1, w_two, g2, b2, True)
-        norm3, inv3, emb = forward_layer(act2, w_three, g2, b2, False)
-        other = swap(emb)
+        norm1, norm2, norm3, inv1, inv2, inv3, x, act1, act2, emb, other = forward(
+            feat_a, feat_b, w_one, w_two, w_three, g1, b1, g2, b2, n)
         loss, d_out = loss_layer(emb, other, norm3, inv3, lam_off.reshape(1, 1))
         dw3 = weight_grad(act2, d_out)
         dw3_other = swap(dw3)

time: 353 us -> 324 us (0.918)
  Pallas kernels: 288 us -> 272 us
  waiting for transfers between devices: 18.8 us -> 6.61 us
    pallas_call x4 -> x1, Pallas kernels: 111 us -> 94.7 us  [forward(): pl.pallas_call(functools.partial(forward_kernel, nb, rows), grid=(3 * nb...]
    ppermute x5 -> x4, waiting for transfers between devices: 18.8 us -> 6.61 us  [swap(): return lax.ppermute(x, AXIS, pair)]
  transfers between devices with their start and end apart: 5 -> 4, of which waited for: 2 -> 1; matrix products, arithmetic and copies ran while one was open for 7% -> 8% of each run, Pallas kernels for 28% -> 30%
where the time goes in v2:
time: 324 us
  Pallas kernels  272 us (84%)
  other arithmetic  37.7 us (12%)
  waiting for transfers between devices  6.61 us (2%)
    pallas_call x1, Pallas kernels, forward(): pl.pallas_call(functools.partial(forward_kernel, nb, rows), grid=(3 * nb...  94.7 us
    pallas_call x2, Pallas kernels, backward_layer(): pl.pallas_call(functools.partial(bwd_kernel, rows, tile), grid=(d // bn,)...  64.4 us
    pallas_call x3, Pallas kernels, weight_grad(): pl.pallas_call(functools.partial(dw_kernel, tile), grid=(k // bm,), in_sp...  57.9 us
    pallas_call x1, Pallas kernels, loss_layer(): pl.pallas_call(functools.partial(loss_kernel, rows, tile), grid=(d // bn,...  55.4 us
    add x1, other arithmetic, local_step(): dw3 + dw3_other  18.1 us
    add x1, other arithmetic, local_step(): dw2 + dw2_other  12.3 us
    add x1, other arithmetic, local_step(): dw1 + dw1_other  6.7 us
    ppermute x4, waiting for transfers between devices, swap(): return lax.ppermute(x, AXIS, pair)  6.61 us
  transfers between devices with their start and end apart: 4, of which 1 were waited for; matrix products, arithmetic and copies ran while one was open for 8% of the time, Pallas kernels for 30%

profile of v2, /device:TPU:0, one launch (start us, length us, event | category | flops | bytes accessed | tf_op | source)
XLA Modules:
  0.0 323.7 jit_solution(12426317867056667541)
XLA Ops:
  1.3 94.7 %forward.1 = (f32[2048,2048]{1,0:T(8,128)}, f32[2048,2048]{1,0:T(8,128)}, f32[2048,2048]{1,0:T(8,128)}, f32[1,2048]{1,0:T(1,128)}, f32[1,2048]{1,0:T(1,128)}, /*...) custom-call(bf16[256,512]{1,0:T(8,128)(2,1)} %fa_ref.1, ...), custom_call_target="tpu_custom_call" | custom-call | flops 38654705664 | bytes 83886080 | tf_op jit(solution)/shard_map/forward/pallas_call | solution.py:167
  96.0 55.4 %loss_layer.1 = (f32[1,512]{1,0:T(1,128)}, bf16[2048,2048]{1,0:T(8,128)(2,1)}) custom-call(f32[1,1]{1,0:T(1,128)} %bitcast.9.lam_ref, bf16[2048,2048]{1,0:T(8,128)(2,1)} %get-tuple-element.27.own_ref, bf16[2048,2048]{1,0:T(8,128)(2,1)} %get-tuple-element.28.other_ref, f32[2048,2048]{1,0:T(8,128)} %get-tuple-element.29.norm_ref, ...), custom_call_target="tpu_custom_call" | custom-call | flops 34359738368 | bytes 41943040 | tf_op jit(solution)/shard_map/loss_layer/pallas_call | solution.py:220
  151.4 24.0 %weight_grad.5 = f32[2048,2048]{1,0:T(8,128)} custom-call(bf16[2048,2048]{1,0:T(8,128)(2,1)} %get-tuple-element.45.x_ref, bf16[2048,2048]{1,0:T(8,128)(2,1)} %get-tuple-element.31.x_ref.y_ref), custom_call_target="tpu_custom_call" | custom-call | flops 17179869184 | bytes 33554432 | tf_op jit(solution)/shard_map/weight_grad/pallas_call | solution.py:278
  175.4 0.3 collective-permute-start.3
  175.7 32.1 %backward_layer.2 = (bf16[2048,2048]{1,0:T(8,128)(2,1)}, f32[1,2048]{1,0:T(1,128)}, f32[1,2048]{1,0:T(1,128)}) custom-call(bf16[2048,2048]{1,0:T(8,128)(2,1)} %get-tuple-element.31.x_ref.y_ref, bf16[2048,2048]{1,0:T(8,128)(2,1)} %w_ref.2, f32[2048,2048]{1,0:T(8,128)} %get-tuple-element.32.norm_ref, f32[1,2048]{1,0:T(1,128)} %get-tuple-element.33.inv_ref, ...), custom_call_target="tpu_custom_call" | custom-call | flops 17179869184 | bytes 33554432 | tf_op jit(solution)/shard_map/backward_layer/pallas_call | solution.py:256
  207.9 24.1 %weight_grad.4 = f32[2048,2048]{1,0:T(8,128)} custom-call(bf16[2048,2048]{1,0:T(8,128)(2,1)} %get-tuple-element.44.x_ref, bf16[2048,2048]{1,0:T(8,128)(2,1)} %get-tuple-element.34.x_ref.y_ref), custom_call_target="tpu_custom_call" | custom-call | flops 17179869184 | bytes 33554432 | tf_op jit(solution)/shard_map/weight_grad/pallas_call | solution.py:278
  231.9 0.1 collective-permute-start.2
  232.0 32.3 %backward_layer.3 = (bf16[2048,2048]{1,0:T(8,128)(2,1)}, f32[1,2048]{1,0:T(1,128)}, f32[1,2048]{1,0:T(1,128)}) custom-call(bf16[2048,2048]{1,0:T(8,128)(2,1)} %get-tuple-element.34.x_ref.y_ref, bf16[2048,2048]{1,0:T(8,128)(2,1)} %w_ref.3, f32[2048,2048]{1,0:T(8,128)} %get-tuple-element.35.norm_ref, f32[1,2048]{1,0:T(1,128)} %get-tuple-element.36.inv_ref, ...), custom_call_target="tpu_custom_call" | custom-call | flops 17179869184 | bytes 33554432 | tf_op jit(solution)/shard_map/backward_layer/pallas_call | solution.py:256
  264.3 0.0 copy-start.2
  264.3 0.0 copy-start.1
  264.4 0.0 copy-start
  264.4 9.8 %weight_grad.3 = f32[512,2048]{1,0:T(8,128)} custom-call(bf16[2048,512]{1,0:T(8,128)(2,1)} %get-tuple-element.42.x_ref, bf16[2048,2048]{1,0:T(8,128)(2,1)} %get-tuple-element.43.y_ref), custom_call_target="tpu_custom_call" | custom-call | flops 4294967296 | bytes 14680064 | tf_op jit(solution)/shard_map/weight_grad/pallas_call | solution.py:278
  274.2 0.2 collective-permute-start.1
  274.5 0.3 collective-permute-start
  274.8 6.6 %collective-permute-done = f32[1,8704]{1,0:T(1,128)S(1)} collective-permute-done((f32[1,8704]{1,0:T(1,128)S(1)}, f32[1,8704]{1,0:T(1,128)S(1)}, u32[]{:S(2)}, u32[]{:S(2)}) %collective-permute-start) | collective-permute-done | bytes 34848 | tf_op jit(solution)/shard_map/ppermute | solution.py:295
  281.4 0.6 slice_reduce_fusion
  282.7 0.6 fusion
  283.3 0.0 collective-permute-done.1
  283.3 6.7 %add.13 = f32[512,2048]{1,0:T(8,128)} add(f32[512,2048]{1,0:T(8,128)} %weight_grad.3, f32[512,2048]{1,0:T(8,128)} %collective-permute-done.1) | non-fusion elementwise | flops 1048576 | bytes 12582912 | tf_op jit(solution)/shard_map/add | solution.py:315
  290.0 0.0 collective-permute-done.3
  290.0 18.1 %add.15 = f32[2048,2048]{1,0:T(8,128)} add(f32[2048,2048]{1,0:T(8,128)} %weight_grad.5, f32[2048,2048]{1,0:T(8,128)} %collective-permute-done.3) | non-fusion elementwise | flops 4194304 | bytes 50331648 | tf_op jit(solution)/shard_map/add | solution.py:315
  308.1 1.0 slice-done.2
  309.1 1.2 slice-done.3
  310.3 12.3 %add.14 = f32[2048,2048]{1,0:T(8,128)} add(f32[2048,2048]{1,0:T(8,128)S(1)} %bitcast.11, f32[2048,2048]{1,0:T(8,128)} %collective-permute-done.2) | non-fusion elementwise | flops 4194304 | bytes 50331648 | tf_op jit(solution)/shard_map/add | solution.py:315
  (21 shorter events, 0.1 us)
Async XLA Ops:
  175.4 114.6 %collective-permute-start.3 = (f32[2048,2048]{1,0:T(8,128)}, f32[2048,2048]{1,0:T(8,128)}, u32[]{:S(2)}, u32[]{:S(2)}) collective-permute-start(f32[2048,2048]{1,0:T(8,128)} %weight_grad.5), channel_id=1, source_target_pairs={{0,1},{1,0},{2,3},{3,2},{4,5},{5,4},{6,7},{7,6}} | collective-permute-start | bytes 50331656 | tf_op jit(solution)/shard_map/ppermute | solution.py:295
  231.9 76.2 %collective-permute-start.2 = (f32[2048,2048]{1,0:T(8,128)}, f32[2048,2048]{1,0:T(8,128)}, u32[]{:S(2)}, u32[]{:S(2)}) collective-permute-start(f32[2048,2048]{1,0:T(8,128)} %weight_grad.4), channel_id=1, source_target_pairs={{0,1},{1,0},{2,3},{3,2},{4,5},{5,4},{6,7},{7,6}} | collective-permute-start | bytes 50331656 | tf_op jit(solution)/shard_map/ppermute | solution.py:295
  264.3 10.1 %copy-start.3 = (f32[1,2048]{1,0:T(1,128)S(1)}, f32[1,2048]{1,0:T(1,128)}, u32[]{:S(2)}) copy-start(f32[1,2048]{1,0:T(1,128)} %get-tuple-element.37) | copy-start | bytes 24580
  264.3 10.1 %copy-start.2 = (f32[1,2048]{1,0:T(1,128)S(1)}, f32[1,2048]{1,0:T(1,128)}, u32[]{:S(2)}) copy-start(f32[1,2048]{1,0:T(1,128)} %get-tuple-element.38) | copy-start | bytes 24580
  264.3 10.1 %copy-start.1 = (f32[1,2048]{1,0:T(1,128)S(1)}, f32[1,2048]{1,0:T(1,128)}, u32[]{:S(2)}) copy-start(f32[1,2048]{1,0:T(1,128)} %get-tuple-element.39) | copy-start | bytes 24580
  264.4 10.1 %copy-start = (f32[1,2048]{1,0:T(1,128)S(1)}, f32[1,2048]{1,0:T(1,128)}, u32[]{:S(2)}) copy-start(f32[1,2048]{1,0:T(1,128)} %get-tuple-element.40) | copy-start | bytes 24580
  264.4 10.1 %copy-start.4 = (f32[1,512]{1,0:T(1,128)S(1)}, f32[1,512]{1,0:T(1,128)}, u32[]{:S(2)}) copy-start(f32[1,512]{1,0:T(1,128)} %get-tuple-element.41) | copy-start | bytes 6148
  274.2 9.1 %collective-permute-start.1 = (f32[512,2048]{1,0:T(8,128)}, f32[512,2048]{1,0:T(8,128)}, u32[]{:S(2)}, u32[]{:S(2)}) collective-permute-start(f32[512,2048]{1,0:T(8,128)} %weight_grad.3), channel_id=1, source_target_pairs={{0,1},{1,0},{2,3},{3,2},{4,5},{5,4},{6,7},{7,6}} | collective-permute-start | bytes 12582920 | tf_op jit(solution)/shard_map/ppermute | solution.py:295
  274.5 6.9 %collective-permute-start = (f32[1,8704]{1,0:T(1,128)S(1)}, f32[1,8704]{1,0:T(1,128)S(1)}, u32[]{:S(2)}, u32[]{:S(2)}) collective-permute-start(f32[1,8704]{1,0:T(1,128)S(1)} %constant_dynamic-update-slice_fusion), channel_id=1, source_target_pairs={{0,1},{1,0},{2,3},{3,2},{4,5},{5,4},{6,7},{7,6}} | collective-permute-start | bytes 104456 | tf_op jit(solution)/shard_map/ppermute | solution.py:295
  283.3 24.8 %slice-start = ((s8[16777216]{0:T(1024)(128)(4,1)}), s8[4194304]{0:T(1024)(128)(4,1)S(1)}, s32[]{:S(2)}) async-start(s8[16777216]{0:T(1024)(128)(4,1)} %bitcast.10), calls=%async_computation | async-start | bytes 8388608
  290.0 18.1 %slice-start.1 = ((s8[16777216]{0:T(1024)(128)(4,1)}), s8[4194304]{0:T(1024)(128)(4,1)S(1)}, s32[]{:S(2)}) async-start(s8[16777216]{0:T(1024)(128)(4,1)} %bitcast.10), calls=%async_computation.1 | async-start | bytes 8388608
  290.0 19.1 %slice-start.2 = ((s8[16777216]{0:T(1024)(128)(4,1)}), s8[4194304]{0:T(1024)(128)(4,1)S(1)}, s32[]{:S(2)}) async-start(s8[16777216]{0:T(1024)(128)(4,1)} %bitcast.10), calls=%async_computation.2 | async-start | bytes 8388608
  290.0 20.3 %slice-start.3 = ((s8[16777216]{0:T(1024)(128)(4,1)}), s8[4194304]{0:T(1024)(128)(4,1)S(1)}, s32[]{:S(2)}) async-start(s8[16777216]{0:T(1024)(128)(4,1)} %bitcast.10), calls=%async_computation.3 | async-start | bytes 8388608

commit v3 on v2

--- a/solution.py
+++ b/solution.py
@@ -78,7 +78,7 @@
     def fin(layer):
         norm_ref, inv_ref = ((n1_ref, i1_ref), (n2_ref, i2_ref), (n3_ref, i3_ref))[layer]
         buf = (bufa, bufb, bufa)[layer]
-        base = pl.multiple_of((j - 1 - layer * nb) * bn, bn)
+        base = pl.multiple_of(jnp.maximum(j - 1 - layer * nb, 0) * bn, bn)
         total = jnp.zeros((8, bn), F32)
         square = jnp.zeros((8, bn), F32)
         for r in range(0, rows, CHUNK):
@@ -117,7 +117,6 @@
     def _():
         gather()
         pltpu.make_async_copy(xs, x_hbm, feat_sem).start()
-        mm(0)
 
     for layer in range(3):
         @pl.when((j >= layer * nb + 2) & (j < (layer + 1) * nb + 2))
@@ -127,7 +126,7 @@
             if layer == 2:
                 emb_copy(block).start()
 
-        @pl.when((j > layer * nb) & (j < (layer + 1) * nb))
+        @pl.when((j >= layer * nb) & (j < (layer + 1) * nb))
         def _(layer=layer):
             fin(layer)
             mm(layer)
@@ -138,8 +137,6 @@
                 for block in range(nb):
                     out_copy(0, block).wait()
             fin(layer)
-            if layer < 2:
-                mm(layer + 1)
 
     @pl.when(j == 3 * nb + 1)
     def _():
@@ -181,89 +178,183 @@
     )(fa, fb, w1, w2, w3, g1, b1, g2, b2)
 
 
-def loss_kernel(rows, tile, lam_ref, own_ref, other_ref, norm_ref, inv_ref, loss_ref, out_ref, grad, dn):
+def finish_back(rows, acc, norm_ref, inv, g, b, put):
+    bn = acc.shape[1]
+    total = jnp.zeros((8, bn), F32)
+    cross = jnp.zeros((8, bn), F32)
+    for r in range(0, rows, CHUNK):
+        part = acc[r:r + CHUNK, :]
+        norm = norm_ref[r:r + CHUNK, :]
+        if b is not None:
+            part = jnp.where(norm * g + b > 0.0, part, 0.0)
+            acc[r:r + CHUNK, :] = part
+        total += fold(part)
+        cross += fold(part * norm)
+    total = jnp.sum(total, axis=0, keepdims=True)
+    cross = jnp.sum(cross, axis=0, keepdims=True)
+    scale = inv if g is None else inv * g
+    shift, slope = scale * (total / rows), scale * (cross / rows)
+    for r in range(0, rows, CHUNK):
+        put(r, (acc[r:r + CHUNK, :] * scale - shift - norm_ref[r:r + CHUNK, :] * slope).astype(BF16))
+    return total, cross
+
+
+def back_a_kernel(nb, rows, lam_ref, own_ref, other_ref, n3_ref, i3_ref, w3_ref, n2_ref, i2_ref, g2_ref, b2_ref, act2_ref,
+                  loss_ref, dw3_ref, dpre_ref, dg_ref, db_ref, corr, grad, acc, dout):
     j = pl.program_id(0)
-    bn = own_ref.shape[1]
+    bn = acc.shape[1]
     d = other_ref.shape[1]
     lam = lam_ref[0, 0]
-    own = own_ref[...]
-    loss = jnp.zeros((1, tile), F32)
-    for c in range(0, d, tile):
-        corr = dot(own, other_ref[:, c:c + tile], ((0,), (0,))) * (1.0 / rows)
-        row_id = lax.broadcasted_iota(jnp.int32, (bn, tile), 0) + j * bn
-        col_id = lax.broadcasted_iota(jnp.int32, (bn, tile), 1) + c
-        diag = row_id == col_id
-        loss += jnp.sum(jnp.where(diag, (1.0 - corr) * (1.0 - corr), lam * (corr * corr)), axis=0, keepdims=True)
-        grad[:, c:c + tile] = jnp.where(diag, -2.0 * (1.0 - corr), (2.0 * lam) * corr).astype(BF16)
+
+    def fin_loss():
+        base = pl.multiple_of(jnp.maximum(j - 1, 0) * bn, bn)
+
+        def put(r, v):
+            dout[r:r + CHUNK, pl.ds(base, bn)] = v
+
+        finish_back(rows, acc, n3_ref, i3_ref[...], None, None, put)
+
+    def mm_loss():
+        own = own_ref[...]
+        loss = jnp.zeros((8, bn), F32)
+        for c in range(0, d, bn):
+            part = dot(own, other_ref[:, c:c + bn], ((0,), (0,))) * (1.0 / rows)
+            corr[:, c:c + bn] = part
+            loss += fold(part * part)
+            grad[:, c:c + bn] = ((2.0 * lam) * part).astype(BF16)
+        here = pl.ds(pl.multiple_of(j * bn, bn), bn)
+        part = corr[:, here]
+        diag = lax.broadcasted_iota(jnp.int32, (bn, bn), 0) == lax.broadcasted_iota(jnp.int32, (bn, bn), 1)
+        grad[:, here] = jnp.where(diag, -2.0 * (1.0 - part), (2.0 * lam) * part).astype(BF16)
+        loss = lam * loss + fold(jnp.where(diag, (1.0 - part) * (1.0 - part) - lam * (part * part), 0.0))
+        loss_ref[...] += jnp.sum(loss, axis=0, keepdims=True)
+        for r in range(0, rows, TILE):
+            acc[r:r + TILE, :] = dot(other_ref[r:r + TILE, :], grad[...], ((1,), (1,))) * (1.0 / rows)
+
+    def fin_two():
+        def put(r, v):
+            dpre_ref[r:r + CHUNK, :] = v
+
+        db_ref[...], dg_ref[...] = finish_back(rows, acc, n2_ref, i2_ref[...], g2_ref[...], b2_ref[...], put)
+
+    def mm_two():
+        for r in range(0, rows, TILE):
+            acc[r:r + TILE, :] = dot(dout[r:r + TILE, :], w3_ref[...], ((1,), (1,)))
+        act = act2_ref[...]
+        for c in range(0, d, 2 * bn):
+            dw3_ref[:, c:c + 2 * bn] = dot(act, dout[:, c:c + 2 * bn], ((0,), (0,)))
 
     @pl.when(j == 0)
     def _():
         loss_ref[...] = jnp.zeros_like(loss_ref)
 
-    loss_ref[...] += loss
-    total = jnp.zeros((1, bn), F32)
-    cross = jnp.zeros((1, bn), F32)
-    for r in range(0, rows, tile):
-        part = dot(other_ref[r:r + tile, :], grad[...], ((1,), (1,))) * (1.0 / rows)
-        dn[r:r + tile, :] = part
-        total += jnp.sum(part, axis=0, keepdims=True)
-        cross += jnp.sum(part * norm_ref[r:r + tile, :], axis=0, keepdims=True)
-    total, cross = total / rows, cross / rows
-    for r in range(0, rows, tile):
-        out_ref[r:r + tile, :] = (inv_ref[...] * (dn[r:r + tile, :] - total - norm_ref[r:r + tile, :] * cross)).astype(BF16)
-
-
-def loss_layer(own, other, norm, inv, lam, bn=256, tile=512):
+    @pl.when(j < nb)
+    def _():
+        fin_loss()
+        mm_loss()
+
+    @pl.when(j == nb)
+    def _():
+        fin_loss()
+
+    @pl.when((j >= nb) & (j < 2 * nb))
+    def _():
+        fin_two()
+        mm_two()
+
+    @pl.when(j == 2 * nb)
+    def _():
+        fin_two()
+
+
+def back_a(lam, own, other, n3, i3, w3, n2, i2, g2, b2, act2, bn=256):
     rows, d = own.shape
-    col = pl.BlockSpec((1, bn), lambda j: (0, j))
-    blk = pl.BlockSpec((rows, bn), lambda j: (0, j))
+    nb = d // bn
+
+    def at(first):
+        return lambda j: (0, jnp.clip(j - first, 0, nb - 1))
+
+    def block(first):
+        return pl.BlockSpec((rows, bn), at(first))
+
+    def col(first):
+        return pl.BlockSpec((1, bn), at(first))
+
+    row = pl.BlockSpec((bn, d), lambda j: (jnp.clip(j - nb, 0, nb - 1), 0))
+    vec = jax.ShapeDtypeStruct((1, d), F32)
     return pl.pallas_call(
-        functools.partial(loss_kernel, rows, tile),
-        grid=(d // bn,),
-        in_specs=[pl.BlockSpec(memory_space=pltpu.SMEM), blk, pl.BlockSpec((rows, d), lambda j: (0, 0), pipeline_mode=ONCE), blk, col],
-        out_specs=[pl.BlockSpec((1, tile), lambda j: (0, 0)), blk],
-        out_shape=[jax.ShapeDtypeStruct((1, tile), F32), jax.ShapeDtypeStruct((rows, d), BF16)],
-        scratch_shapes=[pltpu.VMEM((bn, d), BF16), pltpu.VMEM((rows, bn), F32)],
+        functools.partial(back_a_kernel, nb, rows),
+        grid=(2 * nb + 1,),
+        in_specs=[pl.BlockSpec(memory_space=pltpu.SMEM), block(0), pl.BlockSpec((rows, d), lambda j: (0, 0), pipeline_mode=ONCE),
+                  block(1), col(1), row, block(nb + 1), col(nb + 1), col(nb + 1), col(nb + 1), block(nb)],
+        out_specs=[pl.BlockSpec((1, bn), lambda j: (0, 0)), row, block(nb + 1), col(nb + 1), col(nb + 1)],
+        out_shape=[jax.ShapeDtypeStruct((1, bn), F32), jax.ShapeDtypeStruct((d, d), F32), jax.ShapeDtypeStruct((rows, d), BF16), vec, vec],
+        scratch_shapes=[pltpu.VMEM((bn, d), F32), pltpu.VMEM((bn, d), BF16), pltpu.VMEM((rows, bn), F32), pltpu.VMEM((rows, d), BF16)],
         compiler_params=pltpu.CompilerParams(vmem_limit_bytes=VMEM_LIMIT),
-        cost_estimate=pl.CostEstimate(flops=4 * rows * d * d, bytes_accessed=rows * d * 10, transcendentals=0),
-        name='loss_layer',
-    )(lam, own, other, norm, inv)
-
-
-def bwd_kernel(rows, tile, x_ref, w_ref, norm_ref, inv_ref, g_ref, b_ref, out_ref, dg_ref, db_ref, da):
-    total = jnp.zeros((1, w_ref.shape[0]), F32)
-    cross = jnp.zeros((1, w_ref.shape[0]), F32)
-    g = g_ref[...]
-    for r in range(0, rows, tile):
-        part = dot(x_ref[r:r + tile, :], w_ref[...], ((1,), (1,)))
-        norm = norm_ref[r:r + tile, :]
-        part = jnp.where(norm * g + b_ref[...] > 0.0, part, 0.0)
-        da[r:r + tile, :] = part
-        total += jnp.sum(part, axis=0, keepdims=True)
-        cross += jnp.sum(part * norm, axis=0, keepdims=True)
-    dg_ref[...] = cross
-    db_ref[...] = total
-    total, cross = total * g / rows, cross * g / rows
-    for r in range(0, rows, tile):
-        out_ref[r:r + tile, :] = (inv_ref[...] * (da[r:r + tile, :] * g - total - norm_ref[r:r + tile, :] * cross)).astype(BF16)
-
-
-def backward_layer(x, w, norm, inv, g, b, bn=256, tile=512):
-    rows, k = x.shape
-    d = w.shape[0]
-    col = pl.BlockSpec((1, bn), lambda j: (0, j))
-    blk = pl.BlockSpec((rows, bn), lambda j: (0, j))
+        cost_estimate=pl.CostEstimate(flops=8 * rows * d * d, bytes_accessed=rows * d * 24, transcendentals=0),
+        name='back_a',
+    )(lam, own, other, n3, i3, w3, n2, i2, g2, b2, act2)
+
+
+def back_c_kernel(nb, rows, x_ref, feat_ref, w2_ref, n1_ref, i1_ref, g1_ref, b1_ref, p_ref, q_ref,
+                  sum_ref, dw1_ref, dg_ref, db_ref, acc, dpre, featt):
+    j = pl.program_id(0)
+
+    def fin():
+        def put(r, v):
+            dpre[r:r + CHUNK, :] = v
+
+        db_ref[...], dg_ref[...] = finish_back(rows, acc, n1_ref, i1_ref[...], g1_ref[...], b1_ref[...], put)
+
+    def mm():
+        for r in range(0, rows, TILE):
+            acc[r:r + TILE, :] = dot(x_ref[r:r + TILE, :], w2_ref[...], ((1,), (1,)))
+        for r in range(0, p_ref.shape[0], CHUNK // 2):
+            sum_ref[r:r + CHUNK // 2, :] = p_ref[r:r + CHUNK // 2, :] + q_ref[r:r + CHUNK // 2, :]
+
+    def dw():
+        dw1_ref[...] = dot(featt[...], dpre[...])
+
+    @pl.when(j == 0)
+    def _():
+        for r in range(0, rows, TILE):
+            featt[:, r:r + TILE] = feat_ref[r:r + TILE, :].T
+
+    @pl.when(j < nb)
+    def _():
+        fin()
+        mm()
+        dw()
+
+    @pl.when(j == nb)
+    def _():
+        fin()
+        dw()
+
+
+def back_c(x, feat, w2, n1, i1, g1, b1, p, q, bn=256):
+    rows, d = x.shape
+    k = feat.shape[1]
+    nb = d // bn
+
+    def at(first):
+        return lambda j: (0, jnp.clip(j - first, 0, nb - 1))
+
+    col = pl.BlockSpec((1, bn), at(1))
+    row = pl.BlockSpec((bn, d), lambda j: (jnp.minimum(j, nb - 1), 0))
+    vec = jax.ShapeDtypeStruct((1, d), F32)
     return pl.pallas_call(
-        functools.partial(bwd_kernel, rows, tile),
-        grid=(d // bn,),
-        in_specs=[pl.BlockSpec((rows, k), lambda j: (0, 0), pipeline_mode=ONCE), pl.BlockSpec((bn, k), lambda j: (j, 0)), blk, col, col, col],
-        out_specs=[blk, col, col],
-        out_shape=[jax.ShapeDtypeStruct((rows, d), BF16), jax.ShapeDtypeStruct((1, d), F32), jax.ShapeDtypeStruct((1, d), F32)],
-        scratch_shapes=[pltpu.VMEM((rows, bn), F32)],
+        functools.partial(back_c_kernel, nb, rows),
+        grid=(nb + 1,),
+        in_specs=[pl.BlockSpec((rows, d), lambda j: (0, 0), pipeline_mode=ONCE), pl.BlockSpec((rows, k), lambda j: (0, 0), pipeline_mode=ONCE),
+                  row, pl.BlockSpec((rows, bn), at(1)), col, col, col, row, row],
+        out_specs=[row, pl.BlockSpec((k, bn), at(1)), col, col],
+        out_shape=[jax.ShapeDtypeStruct((d, d), F32), jax.ShapeDtypeStruct((k, d), F32), vec, vec],
+        scratch_shapes=[pltpu.VMEM((rows, bn), F32), pltpu.VMEM((rows, bn), BF16), pltpu.VMEM((k, rows), BF16)],
         compiler_params=pltpu.CompilerParams(vmem_limit_bytes=VMEM_LIMIT),
-        cost_estimate=pl.CostEstimate(flops=2 * rows * k * d, bytes_accessed=rows * d * 6 + rows * k * 2, transcendentals=0),
-        name='backward_layer',
-    )(x, w, norm, inv, g, b)
+        cost_estimate=pl.CostEstimate(flops=2 * rows * d * (k + d), bytes_accessed=rows * d * 20, transcendentals=0),
+        name='back_c',
+    )(x, feat, w2, n1, i1, g1, b1, p, q)
 
 
 def dw_kernel(tile, x_ref, y_ref, out_ref):
@@ -299,20 +390,17 @@
         g1, b1, g2, b2 = (v.reshape(1, width) for v in (g_one, b_one, g_two, b_two))
         norm1, norm2, norm3, inv1, inv2, inv3, x, act1, act2, emb, other = forward(
             feat_a, feat_b, w_one, w_two, w_three, g1, b1, g2, b2, n)
-        loss, d_out = loss_layer(emb, other, norm3, inv3, lam_off.reshape(1, 1))
-        dw3 = weight_grad(act2, d_out)
+        loss, dw3, d_pre2, dg2, db2 = back_a(lam_off.reshape(1, 1), emb, other, norm3, inv3, w_three, norm2, inv2, g2, b2, act2)
         dw3_other = swap(dw3)
-        d_pre2, dg2, db2 = backward_layer(d_out, w_three, norm2, inv2, g2, b2)
         dw2 = weight_grad(act1, d_pre2)
         dw2_other = swap(dw2)
-        d_pre1, dg1, db1 = backward_layer(d_pre2, w_two, norm1, inv1, g1, b1)
-        dw1 = weight_grad(x, d_pre1)
+        dw3, dw1, dg1, db1 = back_c(d_pre2, x, w_two, norm1, inv1, g1, b1, dw3, dw3_other)
         dw1_other = swap(dw1)
         small = jnp.concatenate([dg1, db1, dg2, db2, loss], axis=1)
         small = small + swap(small)
         dg1, db1, dg2, db2 = (small[0, i * width:(i + 1) * width] for i in range(4))
         loss_val = jnp.sum(small[0, 4 * width:]) * 0.5
-        return (loss_val, dw1 + dw1_other, dw2 + dw2_other, dw3 + dw3_other, dg1, db1, dg2, db2)
+        return (loss_val, dw1 + dw1_other, dw2 + dw2_other, dw3, dg1, db1, dg2, db2)
 
     row_spec = P(AXIS, None)
     return jax.shard_map(local_step, mesh=mesh, in_specs=(row_spec, row_spec) + (P(),) * 8, out_specs=(P(),) * 8, check_vma=False)

time: 324 us -> 288 us (0.89)
  Pallas kernels: 272 us -> 256 us
  other arithmetic: 37.7 us -> 24.7 us
  waiting for transfers between devices: 6.61 us -> 0.58 us
    pallas_call x3 -> x1, Pallas kernels: 57.9 us -> 24 us  [weight_grad(): pl.pallas_call(functools.partial(dw_kernel, tile), grid=(k // bm,), in_sp...]
    pallas_call x3 -> x2, Pallas kernels: 120 us -> 134 us  [the longest x1 92.7 us: back_a(): pl.pallas_call(functools.partial(back_a_kernel, nb, rows), grid=(2 * nb +...]
    add x3 -> x2, other arithmetic: 37.1 us -> 24.1 us  [local_step(): return (loss_val, dw1 + dw1_other, dw2 + dw2_other, dw3, dg1, db1, dg2, db2)]
    ppermute x4, waiting for transfers between devices: 6.61 us -> 0.58 us  [swap(): return lax.ppermute(x, AXIS, pair)]
  transfers between devices with their start and end apart: 4 -> 4, of which waited for: 1 -> 1; matrix products, arithmetic and copies ran while one was open for 8% -> 7% of each run, Pallas kernels for 30% -> 23%
where the time goes in v3:
time: 288 us
  Pallas kernels  256 us (89%)
  other arithmetic  24.7 us (9%)
  between operations  3.11 us (1%)
    pallas_call x1, Pallas kernels, forward(): pl.pallas_call(functools.partial(forward_kernel, nb, rows), grid=(3 * nb...  97.7 us
    pallas_call x1, Pallas kernels, back_a(): pl.pallas_call(functools.partial(back_a_kernel, nb, rows), grid=(2 * nb +...  92.7 us
    pallas_call x1, Pallas kernels, back_c(): pl.pallas_call(functools.partial(back_c_kernel, nb, rows), grid=(nb + 1,)...  41.6 us
    add x2, other arithmetic, local_step(): return (loss_val, dw1 + dw1_other, dw2 + dw2_other, dw3, dg1, db1, dg2, db2)  24.1 us
    pallas_call x1, Pallas kernels, weight_grad(): pl.pallas_call(functools.partial(dw_kernel, tile), grid=(k // bm,), in_sp...  24 us
  transfers between devices with their start and end apart: 4, of which 1 were waited for; matrix products, arithmetic and copies ran while one was open for 7% of the time, Pallas kernels for 23%

profile of v3, /device:TPU:0, one launch (start us, length us, event | category | flops | bytes accessed | tf_op | source)
XLA Modules:
  0.0 287.6 jit_solution(18168265429159139791)
XLA Ops:
  1.3 97.7 %forward.1 = (f32[2048,2048]{1,0:T(8,128)}, f32[2048,2048]{1,0:T(8,128)}, f32[2048,2048]{1,0:T(8,128)}, f32[1,2048]{1,0:T(1,128)}, f32[1,2048]{1,0:T(1,128)}, /*...) custom-call(bf16[256,512]{1,0:T(8,128)(2,1)} %fa_ref.1, ...), custom_call_target="tpu_custom_call" | custom-call | flops 38654705664 | bytes 83886080 | tf_op jit(solution)/shard_map/forward/pallas_call | solution.py:164
  99.0 92.7 %back_a.1 = (f32[1,256]{1,0:T(1,128)}, f32[2048,2048]{1,0:T(8,128)}, bf16[2048,2048]{1,0:T(8,128)(2,1)}, f32[1,2048]{1,0:T(1,128)}, f32[1,2048]{1,0:T(1,128)}) custom-call(f32[1,1]{1,0:T(1,128)} %bitcast.9.lam_ref, bf16[2048,2048]{1,0:T(8,128)(2,1)} %get-tuple-element.28.own_ref, bf16[2048,2048]{1,0:T(8,128)(2,1)} %get-tuple-element.29.other_ref, ...), custom_call_target="tpu_custom_call" | custom-call | flops 68719476736 | bytes 100663296 | tf_op jit(solution)/shard_map/back_a/pallas_call | solution.py:285
  191.7 0.3 collective-permute-start
  192.0 24.0 %weight_grad.1 = f32[2048,2048]{1,0:T(8,128)} custom-call(bf16[2048,2048]{1,0:T(8,128)(2,1)} %get-tuple-element.46.x_ref, bf16[2048,2048]{1,0:T(8,128)(2,1)} %get-tuple-element.35.x_ref.y_ref), custom_call_target="tpu_custom_call" | custom-call | flops 17179869184 | bytes 33554432 | tf_op jit(solution)/shard_map/weight_grad/pallas_call | solution.py:369
  216.0 0.2 collective-permute-start.3
  216.2 0.6 collective-permute-done.q_ref
  216.8 0.0 copy-start.1
  216.8 0.0 copy-start
  216.8 0.0 copy-start.2
  216.8 41.6 %back_c.1 = (f32[2048,2048]{1,0:T(8,128)}, f32[512,2048]{1,0:T(8,128)}, f32[1,2048]{1,0:T(1,128)}, f32[1,2048]{1,0:T(1,128)}) custom-call(bf16[2048,2048]{1,0:T(8,128)(2,1)} %get-tuple-element.35.x_ref.y_ref, bf16[2048,512]{1,0:T(8,128)(2,1)} %get-tuple-element.36.feat_ref, bf16[2048,2048]{1,0:T(8,128)(2,1)} %w2_ref.3, ...), custom_call_target="tpu_custom_call" | custom-call | flops 21474836480 | bytes 83886080 | tf_op jit(solution)/shard_map/back_c/pallas_call | solution.py:346
  258.4 0.3 collective-permute-start.2
  258.7 0.7 constant_dynamic-update-slice_fusion.4
  259.4 0.7 constant_dynamic-update-slice_fusion.3
  260.1 0.0 copy-done.1
  260.1 0.0 copy-done
  260.2 0.0 copy-done.2
  260.2 0.2 collective-permute-start.1
  260.4 0.0 collective-permute-done.3
  260.4 17.5 %add.11 = f32[2048,2048]{1,0:T(8,128)} add(f32[2048,2048]{1,0:T(8,128)} %weight_grad.1, f32[2048,2048]{1,0:T(8,128)} %collective-permute-done.3) | non-fusion elementwise | flops 4194304 | bytes 50331648 | tf_op jit(solution)/shard_map/add | solution.py:403
  278.0 0.0 collective-permute-done.1
  278.0 0.6 slice_reduce_fusion
  279.2 0.6 fusion
  279.9 0.0 collective-permute-done.2
  279.9 6.6 %add.10 = f32[512,2048]{1,0:T(8,128)} add(f32[512,2048]{1,0:T(8,128)} %get-tuple-element.45, f32[512,2048]{1,0:T(8,128)} %collective-permute-done.2) | non-fusion elementwise | flops 1048576 | bytes 12582912 | tf_op jit(solution)/shard_map/add | solution.py:403
  (4 shorter events, 0.1 us)
Async XLA Ops:
  191.7 25.1 %collective-permute-start = (f32[2048,2048]{1,0:T(8,128)}, f32[2048,2048]{1,0:T(8,128)}, u32[]{:S(2)}, u32[]{:S(2)}) collective-permute-start(f32[2048,2048]{1,0:T(8,128)} %get-tuple-element.39.p_ref), channel_id=1, source_target_pairs={{0,1},{1,0},{2,3},{3,2},{4,5},{5,4},{6,7},{7,6}} | collective-permute-start | bytes 50331656 | tf_op jit(solution)/shard_map/ppermute | solution.py:386
  216.0 44.4 %collective-permute-start.3 = (f32[2048,2048]{1,0:T(8,128)}, f32[2048,2048]{1,0:T(8,128)}, u32[]{:S(2)}, u32[]{:S(2)}) collective-permute-start(f32[2048,2048]{1,0:T(8,128)} %weight_grad.1), channel_id=1, source_target_pairs={{0,1},{1,0},{2,3},{3,2},{4,5},{5,4},{6,7},{7,6}} | collective-permute-start | bytes 50331656 | tf_op jit(solution)/shard_map/ppermute | solution.py:386
  216.8 43.3 %copy-start.1 = (f32[1,2048]{1,0:T(1,128)S(1)}, f32[1,2048]{1,0:T(1,128)}, u32[]{:S(2)}) copy-start(f32[1,2048]{1,0:T(1,128)} %get-tuple-element.42) | copy-start | bytes 24580
  216.8 43.3 %copy-start = (f32[1,2048]{1,0:T(1,128)S(1)}, f32[1,2048]{1,0:T(1,128)}, u32[]{:S(2)}) copy-start(f32[1,2048]{1,0:T(1,128)} %get-tuple-element.43) | copy-start | bytes 24580
  216.8 43.3 %copy-start.2 = (f32[1,256]{1,0:T(1,128)S(1)}, f32[1,256]{1,0:T(1,128)}, u32[]{:S(2)}) copy-start(f32[1,256]{1,0:T(1,128)} %get-tuple-element.44) | copy-start | bytes 3076
  258.4 21.4 %collective-permute-start.2 = (f32[512,2048]{1,0:T(8,128)}, f32[512,2048]{1,0:T(8,128)}, u32[]{:S(2)}, u32[]{:S(2)}) collective-permute-start(f32[512,2048]{1,0:T(8,128)} %get-tuple-element.45), channel_id=1, source_target_pairs={{0,1},{1,0},{2,3},{3,2},{4,5},{5,4},{6,7},{7,6}} | collective-permute-start | bytes 12582920 | tf_op jit(solution)/shard_map/ppermute | solution.py:386
  260.2 17.8 %collective-permute-start.1 = (f32[1,8448]{1,0:T(1,128)S(1)}, f32[1,8448]{1,0:T(1,128)S(1)}, u32[]{:S(2)}, u32[]{:S(2)}) collective-permute-start(f32[1,8448]{1,0:T(1,128)S(1)} %constant_dynamic-update-slice_fusion), channel_id=1, source_target_pairs={{0,1},{1,0},{2,3},{3,2},{4,5},{5,4},{6,7},{7,6}} | collective-permute-start | bytes 101384 | tf_op jit(solution)/shard_map/ppermute | solution.py:386

commit v4 on v3

--- a/solution.py
+++ b/solution.py
@@ -27,7 +27,7 @@
 
 
 def forward_kernel(nb, rows, fa_ref, fb_ref, w1_ref, w2_ref, w3_ref, g1_ref, b1_ref, g2_ref, b2_ref,
-                   n1_ref, n2_ref, n3_ref, i1_ref, i2_ref, i3_ref, x_hbm, act1_hbm, act2_hbm, emb_hbm, other_hbm,
+                   n1_ref, n2_ref, n3_ref, i1_ref, i2_ref, i3_ref, t1_ref, t2_ref, xt_ref, emb_hbm, other_hbm,
                    xs, bufa, bufb, acc, copy_sem, feat_sem, send_sem, recv_sem, esend_sem, erecv_sem):
     j = pl.program_id(0)
     me = lax.axis_index(AXIS)
@@ -97,17 +97,19 @@
             if layer < 2:
                 norm = jnp.maximum(norm * g + b, 0.0)
             buf[r:r + CHUNK, pl.ds(base, bn)] = norm.astype(BF16)
+        if layer < 2:
+            t_ref = (t1_ref, t2_ref)[layer]
+            for r in range(0, rows, TILE):
+                t_ref[:, r:r + TILE] = buf[r:r + TILE, pl.ds(base, bn)].T
 
     def mm(layer):
         x_ref, w_ref = ((xs, w1_ref), (bufa, w2_ref), (bufb, w3_ref))[layer]
         for r in range(0, rows, TILE):
             acc[r:r + TILE, :] = dot(x_ref[r:r + TILE, :], w_ref[...])
 
-    def out_copy(layer, block):
+    def out_copy(block):
         cols = pl.ds(pl.multiple_of(block * bn, bn), bn)
-        src = (bufa, bufb, bufa)[layer].at[:, cols]
-        dst = (act1_hbm, act2_hbm, emb_hbm)[layer].at[:, cols]
-        return pltpu.make_async_copy(src, dst, copy_sem.at[layer * nb + block])
+        return pltpu.make_async_copy(bufa.at[:, cols], emb_hbm.at[:, cols], copy_sem.at[block])
 
     def emb_copy(block):
         cols = pl.ds(pl.multiple_of(block * bn, bn), bn)
@@ -116,16 +118,8 @@
     @pl.when(j == 0)
     def _():
         gather()
-        pltpu.make_async_copy(xs, x_hbm, feat_sem).start()
 
     for layer in range(3):
-        @pl.when((j >= layer * nb + 2) & (j < (layer + 1) * nb + 2))
-        def _(layer=layer):
-            block = j - 2 - layer * nb
-            out_copy(layer, block).start()
-            if layer == 2:
-                emb_copy(block).start()
-
         @pl.when((j >= layer * nb) & (j < (layer + 1) * nb))
         def _(layer=layer):
             fin(layer)
@@ -133,18 +127,20 @@
 
         @pl.when(j == (layer + 1) * nb)
         def _(layer=layer):
-            if layer == 1:
-                for block in range(nb):
-                    out_copy(0, block).wait()
             fin(layer)
 
+    @pl.when(j >= 2 * nb + 2)
+    def _():
+        block = j - 2 - 2 * nb
+        out_copy(block).start()
+        emb_copy(block).start()
+
     @pl.when(j == 3 * nb + 1)
     def _():
-        for layer in (1, 2):
-            for block in range(nb):
-                out_copy(layer, block).wait()
-        pltpu.make_async_copy(xs, x_hbm, feat_sem).wait()
+        for r in range(0, rows, TILE):
+            xt_ref[:, r:r + TILE] = xs[r:r + TILE, :].T
         for block in range(nb):
+            out_copy(block).wait()
             emb_copy(block).wait()
 
 
@@ -166,11 +162,12 @@
         grid=(3 * nb + 2,),
         in_specs=[whole, whole, pl.BlockSpec((k, bn), at(0, 0)), pl.BlockSpec((d, bn), at(1, 0)), pl.BlockSpec((d, bn), at(2, 0)),
                   col[0], col[0], col[1], col[1]],
-        out_specs=norm + col + [any_spec] * 5,
+        out_specs=norm + col + [pl.BlockSpec((bn, rows), lambda j, f=at(layer, 1): f(j)[::-1]) for layer in range(2)]
+        + [pl.BlockSpec((k, rows), lambda j: (0, 0), pipeline_mode=ONCE)] + [any_spec] * 2,
         out_shape=[jax.ShapeDtypeStruct((rows, d), F32)] * 3 + [jax.ShapeDtypeStruct((1, d), F32)] * 3
-        + [jax.ShapeDtypeStruct((rows, k), BF16)] + [big] * 4,
+        + [jax.ShapeDtypeStruct((d, rows), BF16)] * 2 + [jax.ShapeDtypeStruct((k, rows), BF16)] + [big] * 2,
         scratch_shapes=[pltpu.VMEM((rows, k), BF16), pltpu.VMEM((rows, d), BF16), pltpu.VMEM((rows, d), BF16), pltpu.VMEM((rows, bn), F32),
-                        pltpu.SemaphoreType.DMA((3 * nb,)), pltpu.SemaphoreType.DMA, pltpu.SemaphoreType.DMA((7,)), pltpu.SemaphoreType.DMA((7,)),
+                        pltpu.SemaphoreType.DMA((nb,)), pltpu.SemaphoreType.DMA, pltpu.SemaphoreType.DMA((7,)), pltpu.SemaphoreType.DMA((7,)),
                         pltpu.SemaphoreType.DMA((nb,)), pltpu.SemaphoreType.DMA((nb,))],
         compiler_params=pltpu.CompilerParams(collective_id=0, has_side_effects=True, vmem_limit_bytes=VMEM_LIMIT),
         cost_estimate=pl.CostEstimate(flops=2 * rows * d * (k + 2 * d), bytes_accessed=rows * d * 20, transcendentals=0),
@@ -199,12 +196,62 @@
     return total, cross
 
 
-def back_a_kernel(nb, rows, lam_ref, own_ref, other_ref, n3_ref, i3_ref, w3_ref, n2_ref, i2_ref, g2_ref, b2_ref, act2_ref,
-                  loss_ref, dw3_ref, dpre_ref, dg_ref, db_ref, corr, grad, acc, dout):
+def back_ab_kernel(nb, rows, lam_ref, own_ref, other_hbm, n3_ref, i3_ref, w3_ref, n2_ref, i2_ref, g2_ref, b2_ref, t2_ref, t1_hbm,
+                   loss_ref, dpre_ref, dg_ref, db_ref, dw3_hbm, dw2_hbm,
+                   big, corr, grad, acc, dout, send3, recv3, send2, recv2, load_sem, ssem, rsem, osem, free3, free2):
     j = pl.program_id(0)
+    me = lax.axis_index(AXIS)
+    partner = me + 1 - 2 * lax.rem(me, 2)
     bn = acc.shape[1]
-    d = other_ref.shape[1]
+    d = big.shape[1]
     lam = lam_ref[0, 0]
+    other_ref = big
+
+    def pair(e):
+        return ((send3, recv3, free3, nb), (send2, recv2, free2, nb + 1))[e]
+
+    def swap_copy(e, b):
+        send, recv, _, _ = pair(e)
+        return pltpu.make_async_remote_copy(
+            src_ref=send.at[lax.rem(b, 2)], dst_ref=recv.at[lax.rem(b, 3)], send_sem=ssem.at[e, lax.rem(b, 2)],
+            recv_sem=rsem.at[e, lax.rem(b, 3)], device_id=(partner,), device_id_type=MESH)
+
+    def sum_copy(e, b):
+        span = pl.ds(pl.multiple_of(b * bn, bn), bn)
+        dst = dw3_hbm.at[span, :] if e == 0 else dw2_hbm.at[:, span]
+        return pltpu.make_async_copy(pair(e)[1].at[lax.rem(b, 3)], dst, osem.at[e, lax.rem(b, 3)])
+
+    def exchange(e):
+        send, recv, free, first = pair(e)
+
+        @pl.when((j >= first + 3) & (j < first + 3 + nb))
+        def _():
+            b = j - first - 3
+            sum_copy(e, b).wait()
+
+            @pl.when(b < nb - 3)
+            def _():
+                pl.semaphore_signal(free, inc=1, device_id=(partner,), device_id_type=MESH)
+
+        @pl.when((j >= first + 2) & (j < first + 2 + nb))
+        def _():
+            b = j - first - 2
+            swap_copy(e, b).wait()
+            mine, theirs = lax.rem(b, 2), lax.rem(b, 3)
+            for r in range(0, send.shape[1], send.shape[1] // 32):
+                part = pl.ds(r, send.shape[1] // 32)
+                recv[theirs, part, :] = recv[theirs, part, :] + send[mine, part, :]
+            sum_copy(e, b).start()
+
+        @pl.when((j >= first + 1) & (j < first + 1 + nb))
+        def _():
+            b = j - first - 1
+
+            @pl.when(b >= 3)
+            def _():
+                pl.semaphore_wait(free, 1)
+
+            swap_copy(e, b).start()
 
     def fin_loss():
         base = pl.multiple_of(jnp.maximum(j - 1, 0) * bn, bn)
@@ -240,13 +287,32 @@
     def mm_two():
         for r in range(0, rows, TILE):
             acc[r:r + TILE, :] = dot(dout[r:r + TILE, :], w3_ref[...], ((1,), (1,)))
-        act = act2_ref[...]
+        act = t2_ref[...]
+        slot = lax.rem(j - nb, 2)
         for c in range(0, d, 2 * bn):
-            dw3_ref[:, c:c + 2 * bn] = dot(act, dout[:, c:c + 2 * bn], ((0,), (0,)))
+            send3[slot, :, c:c + 2 * bn] = dot(act, dout[:, c:c + 2 * bn])
+
+    def mm_dw2():
+        slot = lax.rem(j - nb - 1, 2)
+        for r in range(0, d, TILE):
+            send2[slot, r:r + TILE, :] = dot(big[r:r + TILE, :], dpre_ref[...])
 
     @pl.when(j == 0)
     def _():
+        load = pltpu.make_async_copy(other_hbm, big, load_sem)
+        load.start()
         loss_ref[...] = jnp.zeros_like(loss_ref)
+        barrier = pltpu.get_barrier_semaphore()
+        pl.semaphore_signal(barrier, inc=1, device_id=(partner,), device_id_type=MESH)
+        pl.semaphore_wait(barrier, 1)
+        load.wait()
+
+    @pl.when(j == nb)
+    def _():
+        pltpu.make_async_copy(t1_hbm, big, load_sem).start()
+
+    exchange(0)
+    exchange(1)
 
     @pl.when(j < nb)
     def _():
@@ -266,8 +332,16 @@
     def _():
         fin_two()
 
-
-def back_a(lam, own, other, n3, i3, w3, n2, i2, g2, b2, act2, bn=256):
+    @pl.when(j == nb + 1)
+    def _():
+        pltpu.make_async_copy(t1_hbm, big, load_sem).wait()
+
+    @pl.when((j > nb) & (j <= 2 * nb))
+    def _():
+        mm_dw2()
+
+
+def back_ab(lam, own, other, n3, i3, w3, n2, i2, g2, b2, t2, t1, bn=256):
     rows, d = own.shape
     nb = d // bn
 
@@ -282,22 +356,28 @@
 
     row = pl.BlockSpec((bn, d), lambda j: (jnp.clip(j - nb, 0, nb - 1), 0))
     vec = jax.ShapeDtypeStruct((1, d), F32)
+    any_spec = pl.BlockSpec(memory_space=pl.ANY)
     return pl.pallas_call(
-        functools.partial(back_a_kernel, nb, rows),
-        grid=(2 * nb + 1,),
-        in_specs=[pl.BlockSpec(memory_space=pltpu.SMEM), block(0), pl.BlockSpec((rows, d), lambda j: (0, 0), pipeline_mode=ONCE),
-                  block(1), col(1), row, block(nb + 1), col(nb + 1), col(nb + 1), col(nb + 1), block(nb)],
-        out_specs=[pl.BlockSpec((1, bn), lambda j: (0, 0)), row, block(nb + 1), col(nb + 1), col(nb + 1)],
-        out_shape=[jax.ShapeDtypeStruct((1, bn), F32), jax.ShapeDtypeStruct((d, d), F32), jax.ShapeDtypeStruct((rows, d), BF16), vec, vec],
-        scratch_shapes=[pltpu.VMEM((bn, d), F32), pltpu.VMEM((bn, d), BF16), pltpu.VMEM((rows, bn), F32), pltpu.VMEM((rows, d), BF16)],
-        compiler_params=pltpu.CompilerParams(vmem_limit_bytes=VMEM_LIMIT),
-        cost_estimate=pl.CostEstimate(flops=8 * rows * d * d, bytes_accessed=rows * d * 24, transcendentals=0),
-        name='back_a',
-    )(lam, own, other, n3, i3, w3, n2, i2, g2, b2, act2)
-
-
-def back_c_kernel(nb, rows, x_ref, feat_ref, w2_ref, n1_ref, i1_ref, g1_ref, b1_ref, p_ref, q_ref,
-                  sum_ref, dw1_ref, dg_ref, db_ref, acc, dpre, featt):
+        functools.partial(back_ab_kernel, nb, rows),
+        grid=(2 * nb + 4,),
+        in_specs=[pl.BlockSpec(memory_space=pltpu.SMEM), block(0), any_spec,
+                  block(1), col(1), row, block(nb + 1), col(nb + 1), col(nb + 1), col(nb + 1), row, any_spec],
+        out_specs=[pl.BlockSpec((1, bn), lambda j: (0, 0)), block(nb + 1), col(nb + 1), col(nb + 1), any_spec, any_spec],
+        out_shape=[jax.ShapeDtypeStruct((1, bn), F32), jax.ShapeDtypeStruct((rows, d), BF16), vec, vec]
+        + [jax.ShapeDtypeStruct((d, d), F32)] * 2,
+        scratch_shapes=[pltpu.VMEM((rows, d), BF16), pltpu.VMEM((bn, d), F32), pltpu.VMEM((bn, d), BF16), pltpu.VMEM((rows, bn), F32),
+                        pltpu.VMEM((rows, d), BF16), pltpu.VMEM((2, bn, d), F32), pltpu.VMEM((3, bn, d), F32),
+                        pltpu.VMEM((2, d, bn), F32), pltpu.VMEM((3, d, bn), F32), pltpu.SemaphoreType.DMA,
+                        pltpu.SemaphoreType.DMA((2, 2)), pltpu.SemaphoreType.DMA((2, 3)), pltpu.SemaphoreType.DMA((2, 3)),
+                        pltpu.SemaphoreType.REGULAR, pltpu.SemaphoreType.REGULAR],
+        compiler_params=pltpu.CompilerParams(collective_id=1, has_side_effects=True, vmem_limit_bytes=63 * 1024 * 1024),
+        cost_estimate=pl.CostEstimate(flops=10 * rows * d * d, bytes_accessed=rows * d * 24, transcendentals=0),
+        name='back_ab',
+    )(lam, own, other, n3, i3, w3, n2, i2, g2, b2, t2, t1)
+
+
+def back_c_kernel(nb, rows, x_ref, featt, w2_ref, n1_ref, i1_ref, g1_ref, b1_ref, p_ref, q_ref,
+                  p_out, q_out, dw1_ref, dg_ref, db_ref, acc, dpre):
     j = pl.program_id(0)
 
     def fin():
@@ -310,15 +390,11 @@
         for r in range(0, rows, TILE):
             acc[r:r + TILE, :] = dot(x_ref[r:r + TILE, :], w2_ref[...], ((1,), (1,)))
         for r in range(0, p_ref.shape[0], CHUNK // 2):
-            sum_ref[r:r + CHUNK // 2, :] = p_ref[r:r + CHUNK // 2, :] + q_ref[r:r + CHUNK // 2, :]
+            p_out[r:r + CHUNK // 2, :] = p_ref[r:r + CHUNK // 2, :]
+            q_out[r:r + CHUNK // 2, :] = q_ref[r:r + CHUNK // 2, :]
 
     def dw():
         dw1_ref[...] = dot(featt[...], dpre[...])
-
-    @pl.when(j == 0)
-    def _():
-        for r in range(0, rows, TILE):
-            featt[:, r:r + TILE] = feat_ref[r:r + TILE, :].T
 
     @pl.when(j < nb)
     def _():
@@ -332,9 +408,9 @@
         dw()
 
 
-def back_c(x, feat, w2, n1, i1, g1, b1, p, q, bn=256):
+def back_c(x, featt, w2, n1, i1, g1, b1, p, q, bn=256):
     rows, d = x.shape
-    k = feat.shape[1]
+    k = featt.shape[0]
     nb = d // bn
 
     def at(first):
@@ -346,36 +422,15 @@
     return pl.pallas_call(
         functools.partial(back_c_kernel, nb, rows),
         grid=(nb + 1,),
-        in_specs=[pl.BlockSpec((rows, d), lambda j: (0, 0), pipeline_mode=ONCE), pl.BlockSpec((rows, k), lambda j: (0, 0), pipeline_mode=ONCE),
+        in_specs=[pl.BlockSpec((rows, d), lambda j: (0, 0), pipeline_mode=ONCE), pl.BlockSpec((k, rows), lambda j: (0, 0), pipeline_mode=ONCE),
                   row, pl.BlockSpec((rows, bn), at(1)), col, col, col, row, row],
-        out_specs=[row, pl.BlockSpec((k, bn), at(1)), col, col],
-        out_shape=[jax.ShapeDtypeStruct((d, d), F32), jax.ShapeDtypeStruct((k, d), F32), vec, vec],
-        scratch_shapes=[pltpu.VMEM((rows, bn), F32), pltpu.VMEM((rows, bn), BF16), pltpu.VMEM((k, rows), BF16)],
+        out_specs=[row, row, pl.BlockSpec((k, bn), at(1)), col, col],
+        out_shape=[jax.ShapeDtypeStruct((d, d), F32)] * 2 + [jax.ShapeDtypeStruct((k, d), F32), vec, vec],
+        scratch_shapes=[pltpu.VMEM((rows, bn), F32), pltpu.VMEM((rows, bn), BF16)],
         compiler_params=pltpu.CompilerParams(vmem_limit_bytes=VMEM_LIMIT),
         cost_estimate=pl.CostEstimate(flops=2 * rows * d * (k + d), bytes_accessed=rows * d * 20, transcendentals=0),
         name='back_c',
-    )(x, feat, w2, n1, i1, g1, b1, p, q)
-
-
-def dw_kernel(tile, x_ref, y_ref, out_ref):
-    x = x_ref[...]
-    for c in range(0, y_ref.shape[1], tile):
-        out_ref[:, c:c + tile] = dot(x, y_ref[:, c:c + tile], ((0,), (0,)))
-
-
-def weight_grad(x, y, bm=256, tile=512):
-    rows, k = x.shape
-    d = y.shape[1]
-    return pl.pallas_call(
-        functools.partial(dw_kernel, tile),
-        grid=(k // bm,),
-        in_specs=[pl.BlockSpec((rows, bm), lambda j: (0, j)), pl.BlockSpec((rows, d), lambda j: (0, 0), pipeline_mode=ONCE)],
-        out_specs=pl.BlockSpec((bm, d), lambda j: (j, 0)),
-        out_shape=jax.ShapeDtypeStruct((k, d), F32),
-        compiler_params=pltpu.CompilerParams(vmem_limit_bytes=VMEM_LIMIT),
-        cost_estimate=pl.CostEstimate(flops=2 * rows * k * d, bytes_accessed=k * d * 4 + rows * (k + d) * 2, transcendentals=0),
-        name='weight_grad',
-    )(x, y)
+    )(x, featt, w2, n1, i1, g1, b1, p, q)
 
 
 def solution(mesh):
@@ -388,19 +443,17 @@
     def local_step(feat_a, feat_b, w_one, w_two, w_three, g_one, b_one, g_two, b_two, lam_off):
         width = w_two.shape[0]
         g1, b1, g2, b2 = (v.reshape(1, width) for v in (g_one, b_one, g_two, b_two))
-        norm1, norm2, norm3, inv1, inv2, inv3, x, act1, act2, emb, other = forward(
+        norm1, norm2, norm3, inv1, inv2, inv3, act1t, act2t, xt, emb, other = forward(
             feat_a, feat_b, w_one, w_two, w_three, g1, b1, g2, b2, n)
-        loss, dw3, d_pre2, dg2, db2 = back_a(lam_off.reshape(1, 1), emb, other, norm3, inv3, w_three, norm2, inv2, g2, b2, act2)
-        dw3_other = swap(dw3)
-        dw2 = weight_grad(act1, d_pre2)
-        dw2_other = swap(dw2)
-        dw3, dw1, dg1, db1 = back_c(d_pre2, x, w_two, norm1, inv1, g1, b1, dw3, dw3_other)
+        loss, d_pre2, dg2, db2, dw3, dw2 = back_ab(
+            lam_off.reshape(1, 1), emb, other, norm3, inv3, w_three, norm2, inv2, g2, b2, act2t, act1t)
+        dw3, dw2, dw1, dg1, db1 = back_c(d_pre2, xt, w_two, norm1, inv1, g1, b1, dw3, dw2)
         dw1_other = swap(dw1)
         small = jnp.concatenate([dg1, db1, dg2, db2, loss], axis=1)
         small = small + swap(small)
         dg1, db1, dg2, db2 = (small[0, i * width:(i + 1) * width] for i in range(4))
         loss_val = jnp.sum(small[0, 4 * width:]) * 0.5
-        return (loss_val, dw1 + dw1_other, dw2 + dw2_other, dw3, dg1, db1, dg2, db2)
+        return (loss_val, dw1 + dw1_other, dw2, dw3, dg1, db1, dg2, db2)
 
     row_spec = P(AXIS, None)
     return jax.shard_map(local_step, mesh=mesh, in_specs=(row_spec, row_spec) + (P(),) * 8, out_specs=(P(),) * 8, check_vma=False)

time: 288 us -> 284 us (0.986)
  other arithmetic: 24.7 us -> 7.2 us
  Pallas kernels: 256 us -> 266 us
  waiting for transfers between devices: 0.58 us -> 5.23 us
    add x2 -> x1, other arithmetic: 24.1 us -> 6.57 us  [local_step(): return (loss_val, dw1 + dw1_other, dw2, dw3, dg1, db1, dg2, db2)]
    pallas_call x2 -> x1, Pallas kernels: 117 us -> 125 us  [back_ab(): pl.pallas_call(functools.partial(back_ab_kernel, nb, rows), grid=(2 * nb...]
    ppermute x4 -> x2, waiting for transfers between devices: 0.58 us -> 5.23 us  [swap(): return lax.ppermute(x, AXIS, pair)]
    pallas_call x1, Pallas kernels: 41.6 us -> 44.6 us  [back_c(): pl.pallas_call(functools.partial(back_c_kernel, nb, rows), grid=(nb + 1,)...]
  transfers between devices with their start and end apart: 4 -> 2, of which waited for: 1 -> 1; matrix products, arithmetic and copies ran while one was open for 7% -> 1% of each run, Pallas kernels for 23% -> 0%
where the time goes in v4:
time: 284 us
  Pallas kernels  266 us (94%)
  other arithmetic  7.2 us (3%)
  waiting for transfers between devices  5.23 us (2%)
  between operations  3.13 us (1%)
    pallas_call x1, Pallas kernels, back_ab(): pl.pallas_call(functools.partial(back_ab_kernel, nb, rows), grid=(2 * nb...  125 us
    pallas_call x1, Pallas kernels, forward(): pl.pallas_call(functools.partial(forward_kernel, nb, rows), grid=(3 * nb...  95.8 us
    pallas_call x1, Pallas kernels, back_c(): pl.pallas_call(functools.partial(back_c_kernel, nb, rows), grid=(nb + 1,)...  44.6 us
    add x1, other arithmetic, local_step(): return (loss_val, dw1 + dw1_other, dw2, dw3, dg1, db1, dg2, db2)  6.57 us
  transfers between devices with their start and end apart: 2, of which 1 were waited for; matrix products, arithmetic and copies ran while one was open for 1% of the time, Pallas kernels for 0%

profile of v4, /device:TPU:0, one launch (start us, length us, event | category | flops | bytes accessed | tf_op | source)
XLA Modules:
  0.0 283.9 jit_solution(10686803522950508570)
XLA Ops:
  1.3 95.8 %forward.1 = (f32[2048,2048]{1,0:T(8,128)}, f32[2048,2048]{1,0:T(8,128)}, f32[2048,2048]{1,0:T(8,128)}, f32[1,2048]{1,0:T(1,128)}, f32[1,2048]{1,0:T(1,128)}, /*...) custom-call(bf16[256,512]{1,0:T(8,128)(2,1)} %fa_ref.1, ...), custom_call_target="tpu_custom_call" | custom-call | flops 38654705664 | bytes 83886080 | tf_op jit(solution)/shard_map/forward/pallas_call | solution.py:160
  97.1 125.4 %back_ab.1 = (f32[1,256]{1,0:T(1,128)}, bf16[2048,2048]{1,0:T(8,128)(2,1)}, f32[1,2048]{1,0:T(1,128)}, f32[1,2048]{1,0:T(1,128)}, f32[2048,2048]{1,0:T(8,128)}, /*index=5*/f32[2048,2048]{1,0:T(8,128)}) custom-call(f32[1,1]{1,0:T(1,128)} %bitcast.9.lam_ref, bf16[2048,2048]{1,0:T(8,128)(2,1)} %get-tuple-element.30.own_ref, ...), custom_call_target="tpu_custom_call" | custom-call | flops 85899345920 | bytes 100663296 | tf_op jit(solution)/shard_map/back_ab/pallas_call | solution.py:360
  222.5 0.0 copy-start.1
  222.5 0.0 copy-start
  222.5 0.0 copy-start.2
  222.5 44.6 %back_c.1 = (f32[2048,2048]{1,0:T(8,128)}, f32[2048,2048]{1,0:T(8,128)}, f32[512,2048]{1,0:T(8,128)}, f32[1,2048]{1,0:T(1,128)}, f32[1,2048]{1,0:T(1,128)}) custom-call(bf16[2048,2048]{1,0:T(8,128)(2,1)} %get-tuple-element.38.x_ref, bf16[512,2048]{1,0:T(8,128)(2,1)} %get-tuple-element.39.featt, bf16[2048,2048]{1,0:T(8,128)(2,1)} %w2_ref.3, ...), custom_call_target="tpu_custom_call" | custom-call | flops 21474836480 | bytes 83886080 | tf_op jit(solution)/shard_map/back_c/pallas_call | solution.py:422
  267.1 0.4 collective-permute-start.1
  267.4 0.7 constant_dynamic-update-slice_fusion.4
  268.1 0.7 constant_dynamic-update-slice_fusion.3
  268.9 0.0 copy-done.1
  268.9 0.0 copy-done
  268.9 0.0 copy-done.2
  268.9 0.2 collective-permute-start
  269.1 5.2 %collective-permute-done = f32[1,8448]{1,0:T(1,128)S(1)} collective-permute-done((f32[1,8448]{1,0:T(1,128)S(1)}, f32[1,8448]{1,0:T(1,128)S(1)}, u32[]{:S(2)}, u32[]{:S(2)}) %collective-permute-start) | collective-permute-done | bytes 33824 | tf_op jit(solution)/shard_map/ppermute | solution.py:441
  274.4 0.6 slice_reduce_fusion
  275.6 0.6 fusion
  276.2 0.0 collective-permute-done.1
  276.2 6.6 %add.7 = f32[512,2048]{1,0:T(8,128)} add(f32[512,2048]{1,0:T(8,128)} %get-tuple-element.49, f32[512,2048]{1,0:T(8,128)} %collective-permute-done.1) | non-fusion elementwise | flops 1048576 | bytes 12582912 | tf_op jit(solution)/shard_map/add | solution.py:456
  (4 shorter events, 0.1 us)
Async XLA Ops:
  222.5 46.4 %copy-start.1 = (f32[1,2048]{1,0:T(1,128)S(1)}, f32[1,2048]{1,0:T(1,128)}, u32[]{:S(2)}) copy-start(f32[1,2048]{1,0:T(1,128)} %get-tuple-element.46) | copy-start | bytes 24580
  222.5 46.4 %copy-start = (f32[1,2048]{1,0:T(1,128)S(1)}, f32[1,2048]{1,0:T(1,128)}, u32[]{:S(2)}) copy-start(f32[1,2048]{1,0:T(1,128)} %get-tuple-element.47) | copy-start | bytes 24580
  222.5 46.4 %copy-start.2 = (f32[1,256]{1,0:T(1,128)S(1)}, f32[1,256]{1,0:T(1,128)}, u32[]{:S(2)}) copy-start(f32[1,256]{1,0:T(1,128)} %get-tuple-element.48) | copy-start | bytes 3076
  267.1 9.1 %collective-permute-start.1 = (f32[512,2048]{1,0:T(8,128)}, f32[512,2048]{1,0:T(8,128)}, u32[]{:S(2)}, u32[]{:S(2)}) collective-permute-start(f32[512,2048]{1,0:T(8,128)} %get-tuple-element.49), channel_id=1, source_target_pairs={{0,1},{1,0},{2,3},{3,2},{4,5},{5,4},{6,7},{7,6}} | collective-permute-start | bytes 12582920 | tf_op jit(solution)/shard_map/ppermute | solution.py:441
  268.9 5.4 %collective-permute-start = (f32[1,8448]{1,0:T(1,128)S(1)}, f32[1,8448]{1,0:T(1,128)S(1)}, u32[]{:S(2)}, u32[]{:S(2)}) collective-permute-start(f32[1,8448]{1,0:T(1,128)S(1)} %constant_dynamic-update-slice_fusion), channel_id=1, source_target_pairs={{0,1},{1,0},{2,3},{3,2},{4,5},{5,4},{6,7},{7,6}} | collective-permute-start | bytes 101384 | tf_op jit(solution)/shard_map/ppermute | solution.py:441

commit v5 on v4

--- a/solution.py
+++ b/solution.py
@@ -376,22 +376,48 @@
     )(lam, own, other, n3, i3, w3, n2, i2, g2, b2, t2, t1)
 
 
-def back_c_kernel(nb, rows, x_ref, featt, w2_ref, n1_ref, i1_ref, g1_ref, b1_ref, p_ref, q_ref,
-                  p_out, q_out, dw1_ref, dg_ref, db_ref, acc, dpre):
+def back_c_kernel(nb, rows, x_ref, featt, w2_ref, n1_ref, i1_ref, g1_ref, b1_ref, dg2_ref, db2_ref, loss_ref, p_ref, q_ref,
+                  p_out, q_out, dw1_ref, small_ref, acc, dpre, ring, load_sem, store_sem):
     j = pl.program_id(0)
+    bn = acc.shape[1]
+
+    def moves(b):
+        span = pl.ds(pl.multiple_of(b * bn, bn), bn)
+        slot = lax.rem(b, 2)
+        return [(pltpu.make_async_copy(src.at[span, :], ring.at[slot, i], load_sem.at[slot, i]),
+                 pltpu.make_async_copy(ring.at[slot, i], dst.at[span, :], store_sem.at[slot, i]))
+                for i, (src, dst) in enumerate(((p_ref, p_out), (q_ref, q_out)))]
+
+    @pl.when(j >= 2)
+    def _():
+        for _, store in moves(j - 2):
+            store.wait()
+
+    @pl.when(j < nb)
+    def _():
+        for load, _ in moves(j):
+            load.start()
+
+    @pl.when((j >= 1) & (j <= nb))
+    def _():
+        for load, store in moves(j - 1):
+            load.wait()
+            store.start()
 
     def fin():
         def put(r, v):
             dpre[r:r + CHUNK, :] = v
 
-        db_ref[...], dg_ref[...] = finish_back(rows, acc, n1_ref, i1_ref[...], g1_ref[...], b1_ref[...], put)
+        db, dg = finish_back(rows, acc, n1_ref, i1_ref[...], g1_ref[...], b1_ref[...], put)
+        small_ref[0:1, :] = dg
+        small_ref[1:2, :] = db
+        small_ref[2:3, :] = dg2_ref[...]
+        small_ref[3:4, :] = db2_ref[...]
+        small_ref[4:5, :] = loss_ref[...]
 
     def mm():
         for r in range(0, rows, TILE):
             acc[r:r + TILE, :] = dot(x_ref[r:r + TILE, :], w2_ref[...], ((1,), (1,)))
-        for r in range(0, p_ref.shape[0], CHUNK // 2):
-            p_out[r:r + CHUNK // 2, :] = p_ref[r:r + CHUNK // 2, :]
-            q_out[r:r + CHUNK // 2, :] = q_ref[r:r + CHUNK // 2, :]
 
     def dw():
         dw1_ref[...] = dot(featt[...], dpre[...])
@@ -408,7 +434,7 @@
         dw()
 
 
-def back_c(x, featt, w2, n1, i1, g1, b1, p, q, bn=256):
+def back_c(x, featt, w2, n1, i1, g1, b1, dg2, db2, loss, p, q, bn=256):
     rows, d = x.shape
     k = featt.shape[0]
     nb = d // bn
@@ -418,19 +444,20 @@
 
     col = pl.BlockSpec((1, bn), at(1))
     row = pl.BlockSpec((bn, d), lambda j: (jnp.minimum(j, nb - 1), 0))
-    vec = jax.ShapeDtypeStruct((1, d), F32)
+    any_spec = pl.BlockSpec(memory_space=pl.ANY)
     return pl.pallas_call(
         functools.partial(back_c_kernel, nb, rows),
-        grid=(nb + 1,),
+        grid=(nb + 2,),
         in_specs=[pl.BlockSpec((rows, d), lambda j: (0, 0), pipeline_mode=ONCE), pl.BlockSpec((k, rows), lambda j: (0, 0), pipeline_mode=ONCE),
-                  row, pl.BlockSpec((rows, bn), at(1)), col, col, col, row, row],
-        out_specs=[row, row, pl.BlockSpec((k, bn), at(1)), col, col],
-        out_shape=[jax.ShapeDtypeStruct((d, d), F32)] * 2 + [jax.ShapeDtypeStruct((k, d), F32), vec, vec],
-        scratch_shapes=[pltpu.VMEM((rows, bn), F32), pltpu.VMEM((rows, bn), BF16)],
+                  row, pl.BlockSpec((rows, bn), at(1)), col, col, col, col, col, pl.BlockSpec((1, bn), lambda j: (0, 0)), any_spec, any_spec],
+        out_specs=[any_spec, any_spec, pl.BlockSpec((k, bn), at(1)), pl.BlockSpec((8, bn), at(1))],
+        out_shape=[jax.ShapeDtypeStruct((d, d), F32)] * 2 + [jax.ShapeDtypeStruct((k, d), F32), jax.ShapeDtypeStruct((8, d), F32)],
+        scratch_shapes=[pltpu.VMEM((rows, bn), F32), pltpu.VMEM((rows, bn), BF16), pltpu.VMEM((2, 2, bn, d), F32),
+                        pltpu.SemaphoreType.DMA((2, 2)), pltpu.SemaphoreType.DMA((2, 2))],
         compiler_params=pltpu.CompilerParams(vmem_limit_bytes=VMEM_LIMIT),
         cost_estimate=pl.CostEstimate(flops=2 * rows * d * (k + d), bytes_accessed=rows * d * 20, transcendentals=0),
         name='back_c',
-    )(x, featt, w2, n1, i1, g1, b1, p, q)
+    )(x, featt, w2, n1, i1, g1, b1, dg2, db2, loss, p, q)
 
 
 def solution(mesh):
@@ -447,12 +474,11 @@
             feat_a, feat_b, w_one, w_two, w_three, g1, b1, g2, b2, n)
         loss, d_pre2, dg2, db2, dw3, dw2 = back_ab(
             lam_off.reshape(1, 1), emb, other, norm3, inv3, w_three, norm2, inv2, g2, b2, act2t, act1t)
-        dw3, dw2, dw1, dg1, db1 = back_c(d_pre2, xt, w_two, norm1, inv1, g1, b1, dw3, dw2)
+        dw3, dw2, dw1, small = back_c(d_pre2, xt, w_two, norm1, inv1, g1, b1, dg2, db2, loss, dw3, dw2)
         dw1_other = swap(dw1)
-        small = jnp.concatenate([dg1, db1, dg2, db2, loss], axis=1)
         small = small + swap(small)
-        dg1, db1, dg2, db2 = (small[0, i * width:(i + 1) * width] for i in range(4))
-        loss_val = jnp.sum(small[0, 4 * width:]) * 0.5
+        dg1, db1, dg2, db2 = (small[i] for i in range(4))
+        loss_val = jnp.sum(small[4, :loss.shape[1]]) * 0.5
         return (loss_val, dw1 + dw1_other, dw2, dw3, dg1, db1, dg2, db2)
 
     row_spec = P(AXIS, None)

time: 284 us -> 282 us (level)
  Pallas kernels: 266 us -> 262 us
    pallas_call x1, Pallas kernels: 44.6 us -> 41.4 us  [back_c(): pl.pallas_call(functools.partial(back_c_kernel, nb, rows), grid=(nb + 2,)...]
where the time goes in v5:
time: 282 us
  Pallas kernels  262 us (93%)
  other arithmetic  8.02 us (3%)
  waiting for transfers between devices  6.75 us (2%)
  between operations  3.09 us (1%)
    pallas_call x1, Pallas kernels, back_ab(): pl.pallas_call(functools.partial(back_ab_kernel, nb, rows), grid=(2 * nb...  125 us
    pallas_call x1, Pallas kernels, forward(): pl.pallas_call(functools.partial(forward_kernel, nb, rows), grid=(3 * nb...  95.7 us
    pallas_call x1, Pallas kernels, back_c(): pl.pallas_call(functools.partial(back_c_kernel, nb, rows), grid=(nb + 2,)...  41.4 us
    ppermute x2, waiting for transfers between devices, swap(): return lax.ppermute(x, AXIS, pair)  6.75 us
    add x1, other arithmetic, local_step(): return (loss_val, dw1 + dw1_other, dw2, dw3, dg1, db1, dg2, db2)  6.57 us
  transfers between devices with their start and end apart: 2, of which 1 were waited for; matrix products, arithmetic and copies ran while one was open for 1% of the time, Pallas kernels for 0%

profile of v5, /device:TPU:0, one launch (start us, length us, event | category | flops | bytes accessed | tf_op | source)
XLA Modules:
  0.0 281.5 jit_solution(10821695911322854042)
XLA Ops:
  1.3 95.7 %forward.1 = (f32[2048,2048]{1,0:T(8,128)}, f32[2048,2048]{1,0:T(8,128)}, f32[2048,2048]{1,0:T(8,128)}, f32[1,2048]{1,0:T(1,128)}, f32[1,2048]{1,0:T(1,128)}, /*...) custom-call(bf16[256,512]{1,0:T(8,128)(2,1)} %fa_ref.1, ...), custom_call_target="tpu_custom_call" | custom-call | flops 38654705664 | bytes 83886080 | tf_op jit(solution)/shard_map/forward/pallas_call | solution.py:160
  97.0 125.4 %back_ab.1 = (f32[1,256]{1,0:T(1,128)}, bf16[2048,2048]{1,0:T(8,128)(2,1)}, f32[1,2048]{1,0:T(1,128)}, f32[1,2048]{1,0:T(1,128)}, f32[2048,2048]{1,0:T(8,128)}, /*index=5*/f32[2048,2048]{1,0:T(8,128)}) custom-call(f32[1,1]{1,0:T(1,128)} %bitcast.9.lam_ref, bf16[2048,2048]{1,0:T(8,128)(2,1)} %get-tuple-element.29.own_ref, ...), custom_call_target="tpu_custom_call" | custom-call | flops 85899345920 | bytes 100663296 | tf_op jit(solution)/shard_map/back_ab/pallas_call | solution.py:360
  222.4 41.4 %back_c.1 = (f32[2048,2048]{1,0:T(8,128)}, f32[2048,2048]{1,0:T(8,128)}, f32[512,2048]{1,0:T(8,128)}, f32[8,2048]{1,0:T(8,128)}) custom-call(bf16[2048,2048]{1,0:T(8,128)(2,1)} %get-tuple-element.37.x_ref, bf16[512,2048]{1,0:T(8,128)(2,1)} %get-tuple-element.38.featt, bf16[2048,2048]{1,0:T(8,128)(2,1)} %w2_ref.3, f32[2048,2048]{1,0:T(8,128)} %get-tuple-element.39.n1_ref, ...), custom_call_target="tpu_custom_call" | custom-call | flops 21474836480 | bytes 83886080 | tf_op jit(solution)/shard_map/back_c/pallas_call | solution.py:448
  263.8 0.3 collective-permute-start.1
  264.1 0.2 collective-permute-start
  264.3 6.7 %collective-permute-done = f32[8,2048]{1,0:T(8,128)S(1)} collective-permute-done((f32[8,2048]{1,0:T(8,128)}, f32[8,2048]{1,0:T(8,128)S(1)}, u32[]{:S(2)}, u32[]{:S(2)}) %collective-permute-start) | collective-permute-done | bytes 65568 | tf_op jit(solution)/shard_map/ppermute | solution.py:468
  271.1 0.9 add.6
  271.9 0.6 slice_reduce_fusion
  273.2 0.6 fusion
  273.8 0.0 collective-permute-done.1
  273.8 6.6 %add.7 = f32[512,2048]{1,0:T(8,128)} add(f32[512,2048]{1,0:T(8,128)} %get-tuple-element.47, f32[512,2048]{1,0:T(8,128)} %collective-permute-done.1) | non-fusion elementwise | flops 1048576 | bytes 12582912 | tf_op jit(solution)/shard_map/add | solution.py:482
Async XLA Ops:
  263.8 10.0 %collective-permute-start.1 = (f32[512,2048]{1,0:T(8,128)}, f32[512,2048]{1,0:T(8,128)}, u32[]{:S(2)}, u32[]{:S(2)}) collective-permute-start(f32[512,2048]{1,0:T(8,128)} %get-tuple-element.47), channel_id=1, source_target_pairs={{0,1},{1,0},{2,3},{3,2},{4,5},{5,4},{6,7},{7,6}} | collective-permute-start | bytes 12582920 | tf_op jit(solution)/shard_map/ppermute | solution.py:468
  264.1 6.9 %collective-permute-start = (f32[8,2048]{1,0:T(8,128)}, f32[8,2048]{1,0:T(8,128)S(1)}, u32[]{:S(2)}, u32[]{:S(2)}) collective-permute-start(f32[8,2048]{1,0:T(8,128)} %get-tuple-element.46), channel_id=1, source_target_pairs={{0,1},{1,0},{2,3},{3,2},{4,5},{5,4},{6,7},{7,6}} | collective-permute-start | bytes 196616 | tf_op jit(solution)/shard_map/ppermute | solution.py:468

commit v6 on v5

--- a/solution.py
+++ b/solution.py
@@ -381,29 +381,6 @@
     j = pl.program_id(0)
     bn = acc.shape[1]
 
-    def moves(b):
-        span = pl.ds(pl.multiple_of(b * bn, bn), bn)
-        slot = lax.rem(b, 2)
-        return [(pltpu.make_async_copy(src.at[span, :], ring.at[slot, i], load_sem.at[slot, i]),
-                 pltpu.make_async_copy(ring.at[slot, i], dst.at[span, :], store_sem.at[slot, i]))
-                for i, (src, dst) in enumerate(((p_ref, p_out), (q_ref, q_out)))]
-
-    @pl.when(j >= 2)
-    def _():
-        for _, store in moves(j - 2):
-            store.wait()
-
-    @pl.when(j < nb)
-    def _():
-        for load, _ in moves(j):
-            load.start()
-
-    @pl.when((j >= 1) & (j <= nb))
-    def _():
-        for load, store in moves(j - 1):
-            load.wait()
-            store.start()
-
     def fin():
         def put(r, v):
             dpre[r:r + CHUNK, :] = v
@@ -450,6 +427,7 @@
         grid=(nb + 2,),
         in_specs=[pl.BlockSpec((rows, d), lambda j: (0, 0), pipeline_mode=ONCE), pl.BlockSpec((k, rows), lambda j: (0, 0), pipeline_mode=ONCE),
                   row, pl.BlockSpec((rows, bn), at(1)), col, col, col, col, col, pl.BlockSpec((1, bn), lambda j: (0, 0)), any_spec, any_spec],
+        input_output_aliases={10: 0, 11: 1},
         out_specs=[any_spec, any_spec, pl.BlockSpec((k, bn), at(1)), pl.BlockSpec((8, bn), at(1))],
         out_shape=[jax.ShapeDtypeStruct((d, d), F32)] * 2 + [jax.ShapeDtypeStruct((k, d), F32), jax.ShapeDtypeStruct((8, d), F32)],
         scratch_shapes=[pltpu.VMEM((rows, bn), F32), pltpu.VMEM((rows, bn), BF16), pltpu.VMEM((2, 2, bn, d), F32),

time: 282 us -> 296 us (1.050)
  local copies, waits for them, and re-layouts: 0.63 us -> 19.8 us
  Pallas kernels: 262 us -> 257 us
    unnamed x0 -> x10, local copies, waits for them, and re-layouts: none -> 19.2 us
    pallas_call x1, Pallas kernels: 41.4 us -> 35.8 us  [back_c(): pl.pallas_call(functools.partial(back_c_kernel, nb, rows), grid=(nb + 2,)...]
where the time goes in v6:
time: 296 us; the launch traced here: 295 us
  Pallas kernels  257 us (87%)
  local copies, waits for them, and re-layouts  19.8 us (7%)
  other arithmetic  8.16 us (3%)
  waiting for transfers between devices  6.75 us (2%)
  between operations  3.11 us (1%)
    pallas_call x1, Pallas kernels, back_ab(): pl.pallas_call(functools.partial(back_ab_kernel, nb, rows), grid=(2 * nb...  125 us
    pallas_call x1, Pallas kernels, forward(): pl.pallas_call(functools.partial(forward_kernel, nb, rows), grid=(3 * nb...  95.7 us
    pallas_call x1, Pallas kernels, back_c(): pl.pallas_call(functools.partial(back_c_kernel, nb, rows), grid=(nb + 2,)...  35.8 us
    unnamed x10, local copies, waits for them, and re-layouts  19.2 us
    ppermute x2, waiting for transfers between devices, swap(): return lax.ppermute(x, AXIS, pair)  6.75 us
    add x1, other arithmetic, local_step(): return (loss_val, dw1 + dw1_other, dw2, dw3, dg1, db1, dg2, db2)  6.7 us
  transfers between devices with their start and end apart: 2, of which 1 were waited for; matrix products, arithmetic and copies ran while one was open for 1% of the time, Pallas kernels for 0%

profile of v6, /device:TPU:0, one launch (start us, length us, event | category | flops | bytes accessed | tf_op | source)
XLA Modules:
  0.0 295.3 jit_solution(6406587210588244995)
XLA Ops:
  1.3 95.7 %forward.1 = (f32[2048,2048]{1,0:T(8,128)}, f32[2048,2048]{1,0:T(8,128)}, f32[2048,2048]{1,0:T(8,128)}, f32[1,2048]{1,0:T(1,128)}, f32[1,2048]{1,0:T(1,128)}, /*...) custom-call(bf16[256,512]{1,0:T(8,128)(2,1)} %fa_ref.1, ...), custom_call_target="tpu_custom_call" | custom-call | flops 38654705664 | bytes 83886080 | tf_op jit(solution)/shard_map/forward/pallas_call | solution.py:160
  97.0 125.4 %back_ab.1 = (f32[1,256]{1,0:T(1,128)}, bf16[2048,2048]{1,0:T(8,128)(2,1)}, f32[1,2048]{1,0:T(1,128)}, f32[1,2048]{1,0:T(1,128)}, f32[2048,2048]{1,0:T(8,128)}, /*index=5*/f32[2048,2048]{1,0:T(8,128)}) custom-call(f32[1,1]{1,0:T(1,128)} %bitcast.9.lam_ref, bf16[2048,2048]{1,0:T(8,128)(2,1)} %get-tuple-element.29.own_ref, ...), custom_call_target="tpu_custom_call" | custom-call | flops 85899345920 | bytes 100663296 | tf_op jit(solution)/shard_map/back_ab/pallas_call | solution.py:360
  222.4 35.8 %back_c.1 = (f32[2048,2048]{1,0:T(8,128)}, f32[2048,2048]{1,0:T(8,128)}, f32[512,2048]{1,0:T(8,128)}, f32[8,2048]{1,0:T(8,128)}) custom-call(bf16[2048,2048]{1,0:T(8,128)(2,1)} %get-tuple-element.37.x_ref, bf16[512,2048]{1,0:T(8,128)(2,1)} %get-tuple-element.38.featt, bf16[2048,2048]{1,0:T(8,128)(2,1)} %w2_ref.3, ...), custom_call_target="tpu_custom_call", output_to_operand_aliasing={{0}: (10, {}), {1}: (11, {})} | custom-call | flops 21474836480 | bytes 83886080 | tf_op jit(solution)/shard_map/back_c/pallas_call | solution.py:425
  258.2 0.4 collective-permute-start.1
  258.6 0.2 collective-permute-start
  258.8 6.7 %collective-permute-done = f32[8,2048]{1,0:T(8,128)S(1)} collective-permute-done((f32[8,2048]{1,0:T(8,128)}, f32[8,2048]{1,0:T(8,128)S(1)}, u32[]{:S(2)}, u32[]{:S(2)}) %collective-permute-start) | collective-permute-done | bytes 65568 | tf_op jit(solution)/shard_map/ppermute | solution.py:446
  265.5 0.9 add.6
  266.4 0.6 slice_reduce_fusion
  267.6 0.6 fusion
  268.2 0.0 collective-permute-done.1
  268.3 0.0 slice-start
  268.3 0.0 slice-start.1
  268.3 6.7 %add.7 = f32[512,2048]{1,0:T(8,128)} add(f32[512,2048]{1,0:T(8,128)} %get-tuple-element.47, f32[512,2048]{1,0:T(8,128)} %collective-permute-done.1) | non-fusion elementwise | flops 1048576 | bytes 12582912 | tf_op jit(solution)/shard_map/add | solution.py:460
  275.0 0.0 slice-start.2
  275.0 0.0 slice-start.3
  275.0 13.0 %copy.25 = f32[2048,2048]{1,0:T(8,128)} copy(f32[2048,2048]{1,0:T(8,128)} %get-tuple-element.64) | data formatting | bytes 33554432
  288.0 0.0 slice-done
  288.0 0.0 slice-done.1
  288.0 0.0 slice-done.2
  288.0 0.0 slice-done.3
  288.0 6.2 %copy.26 = f32[2048,2048]{1,0:T(8,128)} copy(f32[2048,2048]{1,0:T(8,128)S(1)} %bitcast.11) | data formatting | bytes 33554432
  (1 shorter events, 0.0 us)
Async XLA Ops:
  258.2 10.0 %collective-permute-start.1 = (f32[512,2048]{1,0:T(8,128)}, f32[512,2048]{1,0:T(8,128)}, u32[]{:S(2)}, u32[]{:S(2)}) collective-permute-start(f32[512,2048]{1,0:T(8,128)} %get-tuple-element.47), channel_id=1, source_target_pairs={{0,1},{1,0},{2,3},{3,2},{4,5},{5,4},{6,7},{7,6}} | collective-permute-start | bytes 12582920 | tf_op jit(solution)/shard_map/ppermute | solution.py:446
  258.6 6.9 %collective-permute-start = (f32[8,2048]{1,0:T(8,128)}, f32[8,2048]{1,0:T(8,128)S(1)}, u32[]{:S(2)}, u32[]{:S(2)}) collective-permute-start(f32[8,2048]{1,0:T(8,128)} %get-tuple-element.46), channel_id=1, source_target_pairs={{0,1},{1,0},{2,3},{3,2},{4,5},{5,4},{6,7},{7,6}} | collective-permute-start | bytes 196616 | tf_op jit(solution)/shard_map/ppermute | solution.py:446
  268.3 19.7 %slice-start = ((s8[16777216]{0:T(1024)(128)(4,1)}), s8[4194304]{0:T(1024)(128)(4,1)S(1)}, s32[]{:S(2)}) async-start(s8[16777216]{0:T(1024)(128)(4,1)} %bitcast.10), calls=%async_computation | async-start | bytes 8388608
  268.3 19.7 %slice-start.1 = ((s8[16777216]{0:T(1024)(128)(4,1)}), s8[4194304]{0:T(1024)(128)(4,1)S(1)}, s32[]{:S(2)}) async-start(s8[16777216]{0:T(1024)(128)(4,1)} %bitcast.10), calls=%async_computation.1 | async-start | bytes 8388608
  275.0 13.0 %slice-start.2 = ((s8[16777216]{0:T(1024)(128)(4,1)}), s8[4194304]{0:T(1024)(128)(4,1)S(1)}, s32[]{:S(2)}) async-start(s8[16777216]{0:T(1024)(128)(4,1)} %bitcast.10), calls=%async_computation.2 | async-start | bytes 8388608
  275.0 13.0 %slice-start.3 = ((s8[16777216]{0:T(1024)(128)(4,1)}), s8[4194304]{0:T(1024)(128)(4,1)S(1)}, s32[]{:S(2)}) async-start(s8[16777216]{0:T(1024)(128)(4,1)} %bitcast.10), calls=%async_computation.3 | async-start | bytes 8388608

commit v7 on v5

--- a/solution.py
+++ b/solution.py
@@ -27,8 +27,8 @@
 
 
 def forward_kernel(nb, rows, fa_ref, fb_ref, w1_ref, w2_ref, w3_ref, g1_ref, b1_ref, g2_ref, b2_ref,
-                   n1_ref, n2_ref, n3_ref, i1_ref, i2_ref, i3_ref, t1_ref, t2_ref, xt_ref, emb_hbm, other_hbm,
-                   xs, bufa, bufb, acc, copy_sem, feat_sem, send_sem, recv_sem, esend_sem, erecv_sem):
+                   n1_hbm, n2_ref, n3_ref, i1_ref, i2_ref, i3_ref, t1_ref, t2_ref, xt_ref, emb_hbm, other_hbm,
+                   xs, pre1, sums1, bufa, bufb, acc, norm_sem, copy_sem, feat_sem, send_sem, recv_sem, esend_sem, erecv_sem):
     j = pl.program_id(0)
     me = lax.axis_index(AXIS)
     core = lax.rem(me, 2)
@@ -68,16 +68,57 @@
         relay_x.start()
         pltpu.make_async_copy(fa_ref, part(me), feat_sem).wait()
         remote(fa_ref, part(me), send_sem.at[0], recv_sem.at[0], me).wait()
+        layer_one(me, partner)
+        layer_one(2 * x_chip, 2 * y_chip + 1)
         remote(fa_ref, part(me), send_sem.at[1], recv_sem.at[2], me).wait()
         remote(fa_ref, part(me), send_sem.at[2], recv_sem.at[3], me).wait()
+        layer_one(2 * x_chip + 1, 2 * y_chip)
         remote(fa_ref, part(me), send_sem.at[3], recv_sem.at[5], me).wait()
         remote(fa_ref, part(me), send_sem.at[4], recv_sem.at[6], me).wait()
+        far = 2 * (3 - chip)
+        layer_one(far, far + 1)
         relay_y.wait_send()
         relay_x.wait_send()
 
+    def layer_one(dev_p, dev_q):
+        def work(i, carry):
+            here = pl.ds(pl.multiple_of(jnp.where(i == 0, dev_p, dev_q) * piece, piece), piece)
+            feats = xs[here, :]
+            for c in range(0, w1_ref.shape[1], bn):
+                pre = dot(feats, w1_ref[:, c:c + bn])
+                pre1[here, c:c + bn] = pre
+                sums1[0:8, c:c + bn] += fold(pre)
+                sums1[8:16, c:c + bn] += fold(pre * pre)
+            return carry
+
+        lax.fori_loop(0, 2, work, 0)
+
+    def norm_copy(block):
+        cols = pl.ds(pl.multiple_of(block * bn, bn), bn)
+        return pltpu.make_async_copy(pre1.at[:, cols], n1_hbm.at[:, cols], norm_sem.at[block])
+
+    def finish_one():
+        mean = jnp.sum(sums1[0:8, :], axis=0, keepdims=True) / rows
+        inv = lax.rsqrt(jnp.sum(sums1[8:16, :], axis=0, keepdims=True) / rows - mean * mean + NORM_EPS)
+        sums1[0:1, :] = mean
+        i1_ref[...] = inv
+
+        def work(block, carry):
+            cols = pl.ds(pl.multiple_of(block * bn, bn), bn)
+            mean, inv, g, b = sums1[0:1, cols], i1_ref[:, cols], g1_ref[:, cols], b1_ref[:, cols]
+            for r in range(0, rows, CHUNK):
+                norm = (pre1[r:r + CHUNK, cols] - mean) * inv
+                pre1[r:r + CHUNK, cols] = norm
+                bufa[r:r + CHUNK, cols] = jnp.maximum(norm * g + b, 0.0).astype(BF16)
+            return carry
+
+        lax.fori_loop(0, nb, work, 0)
+        for block in range(nb):
+            norm_copy(block).start()
+
     def fin(layer):
-        norm_ref, inv_ref = ((n1_ref, i1_ref), (n2_ref, i2_ref), (n3_ref, i3_ref))[layer]
-        buf = (bufa, bufb, bufa)[layer]
+        norm_ref, inv_ref = ((n2_ref, i2_ref), (n3_ref, i3_ref))[layer]
+        buf = (bufb, bufa)[layer]
         base = pl.multiple_of(jnp.maximum(j - 1 - layer * nb, 0) * bn, bn)
         total = jnp.zeros((8, bn), F32)
         square = jnp.zeros((8, bn), F32)
@@ -88,22 +129,20 @@
         mean = jnp.sum(total, axis=0, keepdims=True) / rows
         inv = lax.rsqrt(jnp.sum(square, axis=0, keepdims=True) / rows - mean * mean + NORM_EPS)
         inv_ref[...] = inv
-        if layer < 2:
-            g_ref, b_ref = ((g1_ref, b1_ref), (g2_ref, b2_ref))[layer]
-            g, b = g_ref[...], b_ref[...]
+        if layer == 0:
+            g, b = g2_ref[...], b2_ref[...]
         for r in range(0, rows, CHUNK):
             norm = (acc[r:r + CHUNK, :] - mean) * inv
             norm_ref[r:r + CHUNK, :] = norm
-            if layer < 2:
+            if layer == 0:
                 norm = jnp.maximum(norm * g + b, 0.0)
             buf[r:r + CHUNK, pl.ds(base, bn)] = norm.astype(BF16)
-        if layer < 2:
-            t_ref = (t1_ref, t2_ref)[layer]
+        if layer == 0:
             for r in range(0, rows, TILE):
-                t_ref[:, r:r + TILE] = buf[r:r + TILE, pl.ds(base, bn)].T
+                t2_ref[:, r:r + TILE] = buf[r:r + TILE, pl.ds(base, bn)].T
 
     def mm(layer):
-        x_ref, w_ref = ((xs, w1_ref), (bufa, w2_ref), (bufb, w3_ref))[layer]
+        x_ref, w_ref = ((bufa, w2_ref), (bufb, w3_ref))[layer]
         for r in range(0, rows, TILE):
             acc[r:r + TILE, :] = dot(x_ref[r:r + TILE, :], w_ref[...])
 
@@ -117,29 +156,39 @@
 
     @pl.when(j == 0)
     def _():
+        sums1[...] = jnp.zeros_like(sums1)
         gather()
-
-    for layer in range(3):
+        finish_one()
+
+    for layer in range(2):
         @pl.when((j >= layer * nb) & (j < (layer + 1) * nb))
         def _(layer=layer):
             fin(layer)
             mm(layer)
+            if layer == 0:
+                base = pl.multiple_of(j * bn, bn)
+                for r in range(0, rows, TILE):
+                    t1_ref[:, r:r + TILE] = bufa[r:r + TILE, pl.ds(base, bn)].T
 
         @pl.when(j == (layer + 1) * nb)
         def _(layer=layer):
             fin(layer)
 
-    @pl.when(j >= 2 * nb + 2)
-    def _():
-        block = j - 2 - 2 * nb
+    @pl.when(j >= nb + 2)
+    def _():
+        block = j - 2 - nb
         out_copy(block).start()
         emb_copy(block).start()
 
-    @pl.when(j == 3 * nb + 1)
+    @pl.when(j == nb + 1)
     def _():
         for r in range(0, rows, TILE):
             xt_ref[:, r:r + TILE] = xs[r:r + TILE, :].T
+
+    @pl.when(j == 2 * nb + 1)
+    def _():
         for block in range(nb):
+            norm_copy(block).wait()
             out_copy(block).wait()
             emb_copy(block).wait()
 
@@ -154,22 +203,24 @@
 
     whole = pl.BlockSpec((piece, k), lambda j: (0, 0), pipeline_mode=ONCE)
     any_spec = pl.BlockSpec(memory_space=pl.ANY)
-    col = [pl.BlockSpec((1, bn), at(layer, 1)) for layer in range(3)]
-    norm = [pl.BlockSpec((rows, bn), at(layer, 1)) for layer in range(3)]
+    col = [pl.BlockSpec((1, bn), at(layer, 1)) for layer in range(2)]
+    norm = [pl.BlockSpec((rows, bn), at(layer, 1)) for layer in range(2)]
+    vec = pl.BlockSpec((1, d), lambda j: (0, 0))
     big = jax.ShapeDtypeStruct((rows, d), BF16)
     return pl.pallas_call(
         functools.partial(forward_kernel, nb, rows),
-        grid=(3 * nb + 2,),
-        in_specs=[whole, whole, pl.BlockSpec((k, bn), at(0, 0)), pl.BlockSpec((d, bn), at(1, 0)), pl.BlockSpec((d, bn), at(2, 0)),
-                  col[0], col[0], col[1], col[1]],
-        out_specs=norm + col + [pl.BlockSpec((bn, rows), lambda j, f=at(layer, 1): f(j)[::-1]) for layer in range(2)]
+        grid=(2 * nb + 2,),
+        in_specs=[whole, whole, pl.BlockSpec((k, d), lambda j: (0, 0), pipeline_mode=ONCE), pl.BlockSpec((d, bn), at(0, 0)), pl.BlockSpec((d, bn), at(1, 0)),
+                  vec, vec, col[0], col[0]],
+        out_specs=[any_spec] + norm + [vec] + col + [pl.BlockSpec((bn, rows), lambda j, f=at(0, delay): f(j)[::-1]) for delay in range(2)]
         + [pl.BlockSpec((k, rows), lambda j: (0, 0), pipeline_mode=ONCE)] + [any_spec] * 2,
         out_shape=[jax.ShapeDtypeStruct((rows, d), F32)] * 3 + [jax.ShapeDtypeStruct((1, d), F32)] * 3
         + [jax.ShapeDtypeStruct((d, rows), BF16)] * 2 + [jax.ShapeDtypeStruct((k, rows), BF16)] + [big] * 2,
-        scratch_shapes=[pltpu.VMEM((rows, k), BF16), pltpu.VMEM((rows, d), BF16), pltpu.VMEM((rows, d), BF16), pltpu.VMEM((rows, bn), F32),
+        scratch_shapes=[pltpu.VMEM((rows, k), BF16), pltpu.VMEM((rows, d), F32), pltpu.VMEM((16, d), F32), pltpu.VMEM((rows, d), BF16),
+                        pltpu.VMEM((rows, d), BF16), pltpu.VMEM((rows, bn), F32), pltpu.SemaphoreType.DMA((nb,)),
                         pltpu.SemaphoreType.DMA((nb,)), pltpu.SemaphoreType.DMA, pltpu.SemaphoreType.DMA((7,)), pltpu.SemaphoreType.DMA((7,)),
                         pltpu.SemaphoreType.DMA((nb,)), pltpu.SemaphoreType.DMA((nb,))],
-        compiler_params=pltpu.CompilerParams(collective_id=0, has_side_effects=True, vmem_limit_bytes=VMEM_LIMIT),
+        compiler_params=pltpu.CompilerParams(collective_id=0, has_side_effects=True, vmem_limit_bytes=63 * 1024 * 1024),
         cost_estimate=pl.CostEstimate(flops=2 * rows * d * (k + 2 * d), bytes_accessed=rows * d * 20, transcendentals=0),
         name='forward',
     )(fa, fb, w1, w2, w3, g1, b1, g2, b2)

time: 282 us -> 275 us (0.975)
  Pallas kernels: 262 us -> 256 us
    pallas_call x1, Pallas kernels: 95.7 us -> 89.3 us  [forward(): pl.pallas_call(functools.partial(forward_kernel, nb, rows), grid=(2 * nb...]
where the time goes in v7:
time: 275 us
  Pallas kernels  256 us (93%)
  other arithmetic  8.02 us (3%)
  waiting for transfers between devices  6.75 us (2%)
  between operations  3.09 us (1%)
    pallas_call x1, Pallas kernels, back_ab(): pl.pallas_call(functools.partial(back_ab_kernel, nb, rows), grid=(2 * nb...  125 us
    pallas_call x1, Pallas kernels, forward(): pl.pallas_call(functools.partial(forward_kernel, nb, rows), grid=(2 * nb...  89.3 us
    pallas_call x1, Pallas kernels, back_c(): pl.pallas_call(functools.partial(back_c_kernel, nb, rows), grid=(nb + 2,)...  41.4 us
    ppermute x2, waiting for transfers between devices, swap(): return lax.ppermute(x, AXIS, pair)  6.75 us
    add x1, other arithmetic, local_step(): return (loss_val, dw1 + dw1_other, dw2, dw3, dg1, db1, dg2, db2)  6.57 us
  transfers between devices with their start and end apart: 2, of which 1 were waited for; matrix products, arithmetic and copies ran while one was open for 1% of the time, Pallas kernels for 0%

profile of v7, /device:TPU:0, one launch (start us, length us, event | category | flops | bytes accessed | tf_op | source)
XLA Modules:
  0.0 275.1 jit_solution(5218310522473386379)
XLA Ops:
  1.3 89.3 %forward.1 = (f32[2048,2048]{1,0:T(8,128)}, f32[2048,2048]{1,0:T(8,128)}, f32[2048,2048]{1,0:T(8,128)}, f32[1,2048]{1,0:T(1,128)}, f32[1,2048]{1,0:T(1,128)}, /*...) custom-call(bf16[256,512]{1,0:T(8,128)(2,1)} %fa_ref.1, ...), custom_call_target="tpu_custom_call" | custom-call | flops 38654705664 | bytes 83886080 | tf_op jit(solution)/shard_map/forward/pallas_call | solution.py:210
  90.6 125.4 %back_ab.1 = (f32[1,256]{1,0:T(1,128)}, bf16[2048,2048]{1,0:T(8,128)(2,1)}, f32[1,2048]{1,0:T(1,128)}, f32[1,2048]{1,0:T(1,128)}, f32[2048,2048]{1,0:T(8,128)}, /*index=5*/f32[2048,2048]{1,0:T(8,128)}) custom-call(f32[1,1]{1,0:T(1,128)} %bitcast.9.lam_ref, bf16[2048,2048]{1,0:T(8,128)(2,1)} %get-tuple-element.29.own_ref, ...), custom_call_target="tpu_custom_call" | custom-call | flops 85899345920 | bytes 100663296 | tf_op jit(solution)/shard_map/back_ab/pallas_call | solution.py:411
  216.0 41.4 %back_c.1 = (f32[2048,2048]{1,0:T(8,128)}, f32[2048,2048]{1,0:T(8,128)}, f32[512,2048]{1,0:T(8,128)}, f32[8,2048]{1,0:T(8,128)}) custom-call(bf16[2048,2048]{1,0:T(8,128)(2,1)} %get-tuple-element.37.x_ref, bf16[512,2048]{1,0:T(8,128)(2,1)} %get-tuple-element.38.featt, bf16[2048,2048]{1,0:T(8,128)(2,1)} %w2_ref.3, f32[2048,2048]{1,0:T(8,128)} %get-tuple-element.39.n1_ref, ...), custom_call_target="tpu_custom_call" | custom-call | flops 21474836480 | bytes 83886080 | tf_op jit(solution)/shard_map/back_c/pallas_call | solution.py:499
  257.4 0.3 collective-permute-start.1
  257.7 0.2 collective-permute-start
  257.9 6.7 %collective-permute-done = f32[8,2048]{1,0:T(8,128)S(1)} collective-permute-done((f32[8,2048]{1,0:T(8,128)}, f32[8,2048]{1,0:T(8,128)S(1)}, u32[]{:S(2)}, u32[]{:S(2)}) %collective-permute-start) | collective-permute-done | bytes 65568 | tf_op jit(solution)/shard_map/ppermute | solution.py:519
  264.7 0.9 add.6
  265.5 0.6 slice_reduce_fusion
  266.8 0.6 fusion
  267.4 0.0 collective-permute-done.1
  267.4 6.6 %add.7 = f32[512,2048]{1,0:T(8,128)} add(f32[512,2048]{1,0:T(8,128)} %get-tuple-element.47, f32[512,2048]{1,0:T(8,128)} %collective-permute-done.1) | non-fusion elementwise | flops 1048576 | bytes 12582912 | tf_op jit(solution)/shard_map/add | solution.py:533
Async XLA Ops:
  257.4 10.0 %collective-permute-start.1 = (f32[512,2048]{1,0:T(8,128)}, f32[512,2048]{1,0:T(8,128)}, u32[]{:S(2)}, u32[]{:S(2)}) collective-permute-start(f32[512,2048]{1,0:T(8,128)} %get-tuple-element.47), channel_id=1, source_target_pairs={{0,1},{1,0},{2,3},{3,2},{4,5},{5,4},{6,7},{7,6}} | collective-permute-start | bytes 12582920 | tf_op jit(solution)/shard_map/ppermute | solution.py:519
  257.7 6.9 %collective-permute-start = (f32[8,2048]{1,0:T(8,128)}, f32[8,2048]{1,0:T(8,128)S(1)}, u32[]{:S(2)}, u32[]{:S(2)}) collective-permute-start(f32[8,2048]{1,0:T(8,128)} %get-tuple-element.46), channel_id=1, source_target_pairs={{0,1},{1,0},{2,3},{3,2},{4,5},{5,4},{6,7},{7,6}} | collective-permute-start | bytes 196616 | tf_op jit(solution)/shard_map/ppermute | solution.py:519

commit v8 on v7

--- a/solution.py
+++ b/solution.py
@@ -28,7 +28,7 @@
 
 def forward_kernel(nb, rows, fa_ref, fb_ref, w1_ref, w2_ref, w3_ref, g1_ref, b1_ref, g2_ref, b2_ref,
                    n1_hbm, n2_ref, n3_ref, i1_ref, i2_ref, i3_ref, t1_ref, t2_ref, xt_ref, emb_hbm, other_hbm,
-                   xs, pre1, sums1, bufa, bufb, acc, norm_sem, copy_sem, feat_sem, send_sem, recv_sem, esend_sem, erecv_sem):
+                   xs, w1_buf, pre1, sums1, bufa, bufb, acc, w1_sem, norm_sem, copy_sem, feat_sem, send_sem, recv_sem, esend_sem, erecv_sem):
     j = pl.program_id(0)
     me = lax.axis_index(AXIS)
     core = lax.rem(me, 2)
@@ -46,6 +46,7 @@
         return xs.at[pl.ds(pl.multiple_of(dev * piece, piece), piece), :]
 
     def gather():
+        pltpu.make_async_copy(w1_ref, w1_buf, w1_sem).start()
         barrier = pltpu.get_barrier_semaphore()
         for dev in (partner, 2 * x_chip, 2 * x_chip + 1, 2 * y_chip, 2 * y_chip + 1):
             pl.semaphore_signal(barrier, inc=1, device_id=(dev,), device_id_type=MESH)
@@ -68,6 +69,7 @@
         relay_x.start()
         pltpu.make_async_copy(fa_ref, part(me), feat_sem).wait()
         remote(fa_ref, part(me), send_sem.at[0], recv_sem.at[0], me).wait()
+        pltpu.make_async_copy(w1_ref, w1_buf, w1_sem).wait()
         layer_one(me, partner)
         layer_one(2 * x_chip, 2 * y_chip + 1)
         remote(fa_ref, part(me), send_sem.at[1], recv_sem.at[2], me).wait()
@@ -84,8 +86,8 @@
         def work(i, carry):
             here = pl.ds(pl.multiple_of(jnp.where(i == 0, dev_p, dev_q) * piece, piece), piece)
             feats = xs[here, :]
-            for c in range(0, w1_ref.shape[1], bn):
-                pre = dot(feats, w1_ref[:, c:c + bn])
+            for c in range(0, w1_buf.shape[1], bn):
+                pre = dot(feats, w1_buf[:, c:c + bn])
                 pre1[here, c:c + bn] = pre
                 sums1[0:8, c:c + bn] += fold(pre)
                 sums1[8:16, c:c + bn] += fold(pre * pre)
@@ -210,14 +212,14 @@
     return pl.pallas_call(
         functools.partial(forward_kernel, nb, rows),
         grid=(2 * nb + 2,),
-        in_specs=[whole, whole, pl.BlockSpec((k, d), lambda j: (0, 0), pipeline_mode=ONCE), pl.BlockSpec((d, bn), at(0, 0)), pl.BlockSpec((d, bn), at(1, 0)),
+        in_specs=[whole, whole, any_spec, pl.BlockSpec((d, bn), at(0, 0)), pl.BlockSpec((d, bn), at(1, 0)),
                   vec, vec, col[0], col[0]],
         out_specs=[any_spec] + norm + [vec] + col + [pl.BlockSpec((bn, rows), lambda j, f=at(0, delay): f(j)[::-1]) for delay in range(2)]
         + [pl.BlockSpec((k, rows), lambda j: (0, 0), pipeline_mode=ONCE)] + [any_spec] * 2,
         out_shape=[jax.ShapeDtypeStruct((rows, d), F32)] * 3 + [jax.ShapeDtypeStruct((1, d), F32)] * 3
         + [jax.ShapeDtypeStruct((d, rows), BF16)] * 2 + [jax.ShapeDtypeStruct((k, rows), BF16)] + [big] * 2,
-        scratch_shapes=[pltpu.VMEM((rows, k), BF16), pltpu.VMEM((rows, d), F32), pltpu.VMEM((16, d), F32), pltpu.VMEM((rows, d), BF16),
-                        pltpu.VMEM((rows, d), BF16), pltpu.VMEM((rows, bn), F32), pltpu.SemaphoreType.DMA((nb,)),
+        scratch_shapes=[pltpu.VMEM((rows, k), BF16), pltpu.VMEM((k, d), BF16), pltpu.VMEM((rows, d), F32), pltpu.VMEM((16, d), F32),
+                        pltpu.VMEM((rows, d), BF16), pltpu.VMEM((rows, d), BF16), pltpu.VMEM((rows, bn), F32), pltpu.SemaphoreType.DMA, pltpu.SemaphoreType.DMA((nb,)),
                         pltpu.SemaphoreType.DMA((nb,)), pltpu.SemaphoreType.DMA, pltpu.SemaphoreType.DMA((7,)), pltpu.SemaphoreType.DMA((7,)),
                         pltpu.SemaphoreType.DMA((nb,)), pltpu.SemaphoreType.DMA((nb,))],
         compiler_params=pltpu.CompilerParams(collective_id=0, has_side_effects=True, vmem_limit_bytes=63 * 1024 * 1024),
@@ -261,10 +263,13 @@
     def pair(e):
         return ((send3, recv3, free3, nb), (send2, recv2, free2, nb + 1))[e]
 
-    def swap_copy(e, b):
+    def swap_copy(e, b, part=None):
         send, recv, _, _ = pair(e)
+        src, dst = send.at[lax.rem(b, 2)], recv.at[lax.rem(b, 3)]
+        if part is not None:
+            src, dst = src.at[part, :], dst.at[part, :]
         return pltpu.make_async_remote_copy(
-            src_ref=send.at[lax.rem(b, 2)], dst_ref=recv.at[lax.rem(b, 3)], send_sem=ssem.at[e, lax.rem(b, 2)],
+            src_ref=src, dst_ref=dst, send_sem=ssem.at[e, lax.rem(b, 2)],
             recv_sem=rsem.at[e, lax.rem(b, 3)], device_id=(partner,), device_id_type=MESH)
 
     def sum_copy(e, b):
@@ -294,15 +299,10 @@
                 recv[theirs, part, :] = recv[theirs, part, :] + send[mine, part, :]
             sum_copy(e, b).start()
 
-        @pl.when((j >= first + 1) & (j < first + 1 + nb))
+    def ready(e, b):
+        @pl.when(b >= 3)
         def _():
-            b = j - first - 1
-
-            @pl.when(b >= 3)
-            def _():
-                pl.semaphore_wait(free, 1)
-
-            swap_copy(e, b).start()
+            pl.semaphore_wait(pair(e)[2], 1)
 
     def fin_loss():
         base = pl.multiple_of(jnp.maximum(j - 1, 0) * bn, bn)
@@ -343,9 +343,9 @@
         for c in range(0, d, 2 * bn):
             send3[slot, :, c:c + 2 * bn] = dot(act, dout[:, c:c + 2 * bn])
 
-    def mm_dw2():
+    def mm_dw2(first, last):
         slot = lax.rem(j - nb - 1, 2)
-        for r in range(0, d, TILE):
+        for r in range(first, last, TILE):
             send2[slot, r:r + TILE, :] = dot(big[r:r + TILE, :], dpre_ref[...])
 
     @pl.when(j == 0)
@@ -378,6 +378,8 @@
     def _():
         fin_two()
         mm_two()
+        ready(0, j - nb)
+        swap_copy(0, j - nb).start()
 
     @pl.when(j == 2 * nb)
     def _():
@@ -387,9 +389,18 @@
     def _():
         pltpu.make_async_copy(t1_hbm, big, load_sem).wait()
 
-    @pl.when((j > nb) & (j <= 2 * nb))
-    def _():
-        mm_dw2()
+    @pl.when((j > nb) & (j < 2 * nb))
+    def _():
+        mm_dw2(0, d)
+        ready(1, j - nb - 1)
+        swap_copy(1, j - nb - 1).start()
+
+    @pl.when(j == 2 * nb)
+    def _():
+        ready(1, nb - 1)
+        for r in range(0, d, d // 4):
+            mm_dw2(r, r + d // 4)
+            swap_copy(1, nb - 1, pl.ds(r, d // 4)).start()
 
 
 def back_ab(lam, own, other, n3, i3, w3, n2, i2, g2, b2, t2, t1, bn=256):
@@ -428,7 +439,7 @@
 
 
 def back_c_kernel(nb, rows, x_ref, featt, w2_ref, n1_ref, i1_ref, g1_ref, b1_ref, dg2_ref, db2_ref, loss_ref, p_ref, q_ref,
-                  p_out, q_out, dw1_ref, small_ref, acc, dpre, ring, load_sem, store_sem):
+                  p_out, q_out, dw1a_ref, dw1b_ref, acc, dpre, ring, load_sem, store_sem):
     j = pl.program_id(0)
     bn = acc.shape[1]
 
@@ -460,18 +471,18 @@
             dpre[r:r + CHUNK, :] = v
 
         db, dg = finish_back(rows, acc, n1_ref, i1_ref[...], g1_ref[...], b1_ref[...], put)
-        small_ref[0:1, :] = dg
-        small_ref[1:2, :] = db
-        small_ref[2:3, :] = dg2_ref[...]
-        small_ref[3:4, :] = db2_ref[...]
-        small_ref[4:5, :] = loss_ref[...]
+        half = dw1b_ref.shape[0]
+        for i, row in enumerate((dg, db, dg2_ref[...], db2_ref[...], loss_ref[...])):
+            dw1a_ref[half + i:half + i + 1, :] = row
 
     def mm():
         for r in range(0, rows, TILE):
             acc[r:r + TILE, :] = dot(x_ref[r:r + TILE, :], w2_ref[...], ((1,), (1,)))
 
     def dw():
-        dw1_ref[...] = dot(featt[...], dpre[...])
+        half = dw1b_ref.shape[0]
+        dw1a_ref[:half, :] = dot(featt[:half, :], dpre[...])
+        dw1b_ref[...] = dot(featt[half:, :], dpre[...])
 
     @pl.when(j < nb)
     def _():
@@ -501,14 +512,47 @@
         grid=(nb + 2,),
         in_specs=[pl.BlockSpec((rows, d), lambda j: (0, 0), pipeline_mode=ONCE), pl.BlockSpec((k, rows), lambda j: (0, 0), pipeline_mode=ONCE),
                   row, pl.BlockSpec((rows, bn), at(1)), col, col, col, col, col, pl.BlockSpec((1, bn), lambda j: (0, 0)), any_spec, any_spec],
-        out_specs=[any_spec, any_spec, pl.BlockSpec((k, bn), at(1)), pl.BlockSpec((8, bn), at(1))],
-        out_shape=[jax.ShapeDtypeStruct((d, d), F32)] * 2 + [jax.ShapeDtypeStruct((k, d), F32), jax.ShapeDtypeStruct((8, d), F32)],
+        out_specs=[any_spec, any_spec, pl.BlockSpec((k // 2 + 8, bn), at(1)), pl.BlockSpec((k // 2, bn), at(1))],
+        out_shape=[jax.ShapeDtypeStruct((d, d), F32)] * 2 + [jax.ShapeDtypeStruct((k // 2 + 8, d), F32), jax.ShapeDtypeStruct((k // 2, d), F32)],
         scratch_shapes=[pltpu.VMEM((rows, bn), F32), pltpu.VMEM((rows, bn), BF16), pltpu.VMEM((2, 2, bn, d), F32),
                         pltpu.SemaphoreType.DMA((2, 2)), pltpu.SemaphoreType.DMA((2, 2))],
         compiler_params=pltpu.CompilerParams(vmem_limit_bytes=VMEM_LIMIT),
         cost_estimate=pl.CostEstimate(flops=2 * rows * d * (k + d), bytes_accessed=rows * d * 20, transcendentals=0),
         name='back_c',
     )(x, featt, w2, n1, i1, g1, b1, dg2, db2, loss, p, q)
+
+
+def add_first_kernel(p_ref, q_ref, out_ref, small_ref):
+    half = out_ref.shape[0]
+    out_ref[...] = p_ref[:half, :] + q_ref[:half, :]
+    small_ref[...] = p_ref[half:, :] + q_ref[half:, :]
+
+
+def add_second_kernel(p_ref, q_ref, _, out_ref):
+    out_ref[...] = p_ref[...] + q_ref[...]
+
+
+def add_half(p, q, half, whole=None):
+    rows, d = p.shape
+    blk = d // 2
+    spec = pl.BlockSpec((rows, blk), lambda j: (0, j))
+    first = whole is None
+    out_specs = [pl.BlockSpec((half, blk), lambda j: (0 if first else 1, j))]
+    out_shape = [jax.ShapeDtypeStruct((2 * half, d), F32)]
+    if first:
+        out_specs.append(pl.BlockSpec((rows - half, blk), lambda j: (0, j)))
+        out_shape.append(jax.ShapeDtypeStruct((rows - half, d), F32))
+    return pl.pallas_call(
+        add_first_kernel if first else add_second_kernel,
+        grid=(2,),
+        in_specs=[spec, spec] + ([] if first else [pl.BlockSpec(memory_space=pl.ANY)]),
+        out_specs=out_specs,
+        out_shape=out_shape,
+        input_output_aliases={} if first else {2: 0},
+        compiler_params=pltpu.CompilerParams(vmem_limit_bytes=24 * 1024 * 1024),
+        cost_estimate=pl.CostEstimate(flops=rows * d * 2000, bytes_accessed=rows * d * 12, transcendentals=0),
+        name='add_half',
+    )(*([p, q] if first else [p, q, whole]))
 
 
 def solution(mesh):
@@ -525,12 +569,13 @@
             feat_a, feat_b, w_one, w_two, w_three, g1, b1, g2, b2, n)
         loss, d_pre2, dg2, db2, dw3, dw2 = back_ab(
             lam_off.reshape(1, 1), emb, other, norm3, inv3, w_three, norm2, inv2, g2, b2, act2t, act1t)
-        dw3, dw2, dw1, small = back_c(d_pre2, xt, w_two, norm1, inv1, g1, b1, dg2, db2, loss, dw3, dw2)
-        dw1_other = swap(dw1)
-        small = small + swap(small)
+        dw3, dw2, dw1a, dw1b = back_c(d_pre2, xt, w_two, norm1, inv1, g1, b1, dg2, db2, loss, dw3, dw2)
+        half = dw1b.shape[0]
+        dw1, small = add_half(dw1a, swap(dw1a), half)
+        dw1, = add_half(dw1b, swap(dw1b), half, dw1)
         dg1, db1, dg2, db2 = (small[i] for i in range(4))
         loss_val = jnp.sum(small[4, :loss.shape[1]]) * 0.5
-        return (loss_val, dw1 + dw1_other, dw2, dw3, dg1, db1, dg2, db2)
+        return (loss_val, dw1, dw2, dw3, dg1, db1, dg2, db2)
 
     row_spec = P(AXIS, None)
     return jax.shard_map(local_step, mesh=mesh, in_specs=(row_spec, row_spec) + (P(),) * 8, out_specs=(P(),) * 8, check_vma=False)

time: 275 us -> 266 us (0.967)
  other arithmetic: 8.02 us -> 0.6 us
  local copies, waits for them, and re-layouts: 0.63 us -> 3.83 us
  waiting for transfers between devices: 6.75 us -> 3.75 us
    add x2 -> x0, other arithmetic: 7.42 us -> none  [the longest x1 6.57 us: local_step(): return (loss_val, dw1 + dw1_other, dw2, dw3, dg1, db1, dg2, db2)]
    pallas_call x1, Pallas kernels: 125 us -> 121 us  [back_ab(): pl.pallas_call(functools.partial(back_ab_kernel, nb, rows), grid=(2 * nb...]
    pallas_call x0 -> x2, Pallas kernels: none -> 3.44 us  [add_half(): pl.pallas_call(add_first_kernel if first else add_second_kernel, grid=(2,...]
    unnamed x0 -> x4, local copies, waits for them, and re-layouts: none -> 3.2 us
    ppermute x2, waiting for transfers between devices: 6.75 us -> 3.75 us  [swap(): return lax.ppermute(x, AXIS, pair)]
  transfers between devices with their start and end apart: 2 -> 2, of which waited for: 1 -> 1; matrix products, arithmetic and copies ran while one was open for 1% -> 0% of each run, Pallas kernels for 0% -> 1%
where the time goes in v8:
time: 266 us
  Pallas kernels  254 us (95%)
  local copies, waits for them, and re-layouts  3.83 us (1%)
  waiting for transfers between devices  3.75 us (1%)
  between operations  3.09 us (1%)
    pallas_call x1, Pallas kernels, back_ab(): pl.pallas_call(functools.partial(back_ab_kernel, nb, rows), grid=(2 * nb...  121 us
    pallas_call x1, Pallas kernels, forward(): pl.pallas_call(functools.partial(forward_kernel, nb, rows), grid=(2 * nb...  88.5 us
    pallas_call x1, Pallas kernels, back_c(): pl.pallas_call(functools.partial(back_c_kernel, nb, rows), grid=(nb + 2,)...  41.1 us
  transfers between devices with their start and end apart: 2, of which 1 were waited for; matrix products, arithmetic and copies ran while one was open for 0% of the time, Pallas kernels for 1%

profile of v8, /device:TPU:0, one launch (start us, length us, event | category | flops | bytes accessed | tf_op | source)
XLA Modules:
  0.0 265.6 jit_solution(4928672402663730197)
XLA Ops:
  1.3 88.5 %forward.1 = (f32[2048,2048]{1,0:T(8,128)}, f32[2048,2048]{1,0:T(8,128)}, f32[2048,2048]{1,0:T(8,128)}, f32[1,2048]{1,0:T(1,128)}, f32[1,2048]{1,0:T(1,128)}, /*...) custom-call(bf16[256,512]{1,0:T(8,128)(2,1)} %fa_ref.1, ...), custom_call_target="tpu_custom_call" | custom-call | flops 38654705664 | bytes 83886080 | tf_op jit(solution)/shard_map/forward/pallas_call | solution.py:212
  89.8 120.8 %back_ab.1 = (f32[1,256]{1,0:T(1,128)}, bf16[2048,2048]{1,0:T(8,128)(2,1)}, f32[1,2048]{1,0:T(1,128)}, f32[1,2048]{1,0:T(1,128)}, f32[2048,2048]{1,0:T(8,128)}, /*index=5*/f32[2048,2048]{1,0:T(8,128)}) custom-call(f32[1,1]{1,0:T(1,128)} %bitcast.9.lam_ref, bf16[2048,2048]{1,0:T(8,128)(2,1)} %get-tuple-element.31.own_ref, ...), custom_call_target="tpu_custom_call" | custom-call | flops 85899345920 | bytes 100663296 | tf_op jit(solution)/shard_map/back_ab/pallas_call | solution.py:422
  210.6 41.1 %back_c.1 = (f32[2048,2048]{1,0:T(8,128)}, f32[2048,2048]{1,0:T(8,128)}, f32[264,2048]{1,0:T(8,128)}, f32[256,2048]{1,0:T(8,128)}) custom-call(bf16[2048,2048]{1,0:T(8,128)(2,1)} %get-tuple-element.39.x_ref, bf16[512,2048]{1,0:T(8,128)(2,1)} %get-tuple-element.40.featt, bf16[2048,2048]{1,0:T(8,128)(2,1)} %w2_ref.3, f32[2048,2048]{1,0:T(8,128)} %get-tuple-element.41.n1_ref, ...), custom_call_target="tpu_custom_call" | custom-call | flops 21474836480 | bytes 83886080 | tf_op jit(solution)/shard_map/back_c/pallas_call | solution.py:510
  251.6 0.2 collective-permute-start
  251.9 0.3 collective-permute-start.1
  252.2 3.7 %collective-permute-done.q_ref = f32[264,2048]{1,0:T(8,128)S(1)} collective-permute-done((f32[264,2048]{1,0:T(8,128)}, f32[264,2048]{1,0:T(8,128)S(1)}, u32[]{:S(2)}, u32[]{:S(2)}) %collective-permute-start) | collective-permute-done | bytes 2162720 | tf_op jit(solution)/shard_map/ppermute | solution.py:563
  255.9 0.0 copy-start
  255.9 1.6 copy-done
  257.5 1.7 add_half.2
  259.3 0.6 slice_reduce_fusion
  260.5 0.6 fusion
  261.1 0.0 collective-permute-done.1.q_ref
  261.1 0.0 copy-start.1
  261.1 1.6 copy-done.1
  262.7 1.7 add_half.3
Async XLA Ops:
  251.6 4.3 %collective-permute-start = (f32[264,2048]{1,0:T(8,128)}, f32[264,2048]{1,0:T(8,128)S(1)}, u32[]{:S(2)}, u32[]{:S(2)}) collective-permute-start(f32[264,2048]{1,0:T(8,128)} %get-tuple-element.48.p_ref), channel_id=1, source_target_pairs={{0,1},{1,0},{2,3},{3,2},{4,5},{5,4},{6,7},{7,6}} | collective-permute-start | bytes 6488072 | tf_op jit(solution)/shard_map/ppermute | solution.py:563
  251.9 9.3 %collective-permute-start.1 = (f32[256,2048]{1,0:T(8,128)}, f32[256,2048]{1,0:T(8,128)S(1)}, u32[]{:S(2)}, u32[]{:S(2)}) collective-permute-start(f32[256,2048]{1,0:T(8,128)} %get-tuple-element.50.p_ref), channel_id=1, source_target_pairs={{0,1},{1,0},{2,3},{3,2},{4,5},{5,4},{6,7},{7,6}} | collective-permute-start | bytes 6291464 | tf_op jit(solution)/shard_map/ppermute | solution.py:563
  255.9 1.6 copy-start
  261.1 1.6 copy-start.1

commit v9 on v8

--- a/solution.py
+++ b/solution.py
@@ -251,7 +251,7 @@
 
 def back_ab_kernel(nb, rows, lam_ref, own_ref, other_hbm, n3_ref, i3_ref, w3_ref, n2_ref, i2_ref, g2_ref, b2_ref, t2_ref, t1_hbm,
                    loss_ref, dpre_ref, dg_ref, db_ref, dw3_hbm, dw2_hbm,
-                   big, corr, grad, acc, dout, send3, recv3, send2, recv2, load_sem, ssem, rsem, osem, free3, free2):
+                   big, corr, grad, acc, dout, send3, recv3, send2, recv2, load_sem, chunk_sem, ssem, rsem, osem, free3, free2):
     j = pl.program_id(0)
     me = lax.axis_index(AXIS)
     partner = me + 1 - 2 * lax.rem(me, 2)
@@ -312,14 +312,28 @@
 
         finish_back(rows, acc, n3_ref, i3_ref[...], None, None, put)
 
-    def mm_loss():
+    def load_other(c):
+        cols = pl.ds(pl.multiple_of(c * bn, bn), bn)
+        return pltpu.make_async_copy(other_hbm.at[:, cols], big.at[:, cols], chunk_sem.at[c])
+
+    def mm_loss(arriving):
         own = own_ref[...]
+
+        def correlate(c, loss):
+            cols = pl.ds(pl.multiple_of(c * bn, bn), bn)
+            if arriving:
+                load_other(c).wait()
+            part = dot(own, other_ref[:, cols], ((0,), (0,))) * (1.0 / rows)
+            corr[:, cols] = part
+            grad[:, cols] = ((2.0 * lam) * part).astype(BF16)
+            return loss + fold(part * part)
+
         loss = jnp.zeros((8, bn), F32)
-        for c in range(0, d, bn):
-            part = dot(own, other_ref[:, c:c + bn], ((0,), (0,))) * (1.0 / rows)
-            corr[:, c:c + bn] = part
-            loss += fold(part * part)
-            grad[:, c:c + bn] = ((2.0 * lam) * part).astype(BF16)
+        if arriving:
+            loss = lax.fori_loop(0, nb, correlate, loss)
+        else:
+            for c in range(nb):
+                loss = correlate(c, loss)
         here = pl.ds(pl.multiple_of(j * bn, bn), bn)
         part = corr[:, here]
         diag = lax.broadcasted_iota(jnp.int32, (bn, bn), 0) == lax.broadcasted_iota(jnp.int32, (bn, bn), 1)
@@ -350,13 +364,13 @@
 
     @pl.when(j == 0)
     def _():
-        load = pltpu.make_async_copy(other_hbm, big, load_sem)
-        load.start()
+        for c in range(nb):
+            load_other(c).start()
         loss_ref[...] = jnp.zeros_like(loss_ref)
         barrier = pltpu.get_barrier_semaphore()
         pl.semaphore_signal(barrier, inc=1, device_id=(partner,), device_id_type=MESH)
         pl.semaphore_wait(barrier, 1)
-        load.wait()
+        mm_loss(True)
 
     @pl.when(j == nb)
     def _():
@@ -365,10 +379,10 @@
     exchange(0)
     exchange(1)
 
-    @pl.when(j < nb)
+    @pl.when((j > 0) & (j < nb))
     def _():
         fin_loss()
-        mm_loss()
+        mm_loss(False)
 
     @pl.when(j == nb)
     def _():
@@ -429,7 +443,7 @@
         + [jax.ShapeDtypeStruct((d, d), F32)] * 2,
         scratch_shapes=[pltpu.VMEM((rows, d), BF16), pltpu.VMEM((bn, d), F32), pltpu.VMEM((bn, d), BF16), pltpu.VMEM((rows, bn), F32),
                         pltpu.VMEM((rows, d), BF16), pltpu.VMEM((2, bn, d), F32), pltpu.VMEM((3, bn, d), F32),
-                        pltpu.VMEM((2, d, bn), F32), pltpu.VMEM((3, d, bn), F32), pltpu.SemaphoreType.DMA,
+                        pltpu.VMEM((2, d, bn), F32), pltpu.VMEM((3, d, bn), F32), pltpu.SemaphoreType.DMA, pltpu.SemaphoreType.DMA((nb,)),
                         pltpu.SemaphoreType.DMA((2, 2)), pltpu.SemaphoreType.DMA((2, 3)), pltpu.SemaphoreType.DMA((2, 3)),
                         pltpu.SemaphoreType.REGULAR, pltpu.SemaphoreType.REGULAR],
         compiler_params=pltpu.CompilerParams(collective_id=1, has_side_effects=True, vmem_limit_bytes=63 * 1024 * 1024),
@@ -438,10 +452,24 @@
     )(lam, own, other, n3, i3, w3, n2, i2, g2, b2, t2, t1)
 
 
-def back_c_kernel(nb, rows, x_ref, featt, w2_ref, n1_ref, i1_ref, g1_ref, b1_ref, dg2_ref, db2_ref, loss_ref, p_ref, q_ref,
-                  p_out, q_out, dw1a_ref, dw1b_ref, acc, dpre, ring, load_sem, store_sem):
+def back_c_kernel(nb, rows, x_hbm, featt_hbm, w2_ref, n1_ref, i1_ref, g1_ref, b1_ref, dg2_ref, db2_ref, loss_ref, p_ref, q_ref,
+                  p_out, q_out, dw1a_ref, dw1b_ref, acc, dpre, ring, x_ref, featt, load_sem, store_sem, x_sem, feat_sem):
     j = pl.program_id(0)
     bn = acc.shape[1]
+
+    def load_x(r):
+        here = pl.ds(pl.multiple_of(r * TILE, TILE), TILE)
+        return pltpu.make_async_copy(x_hbm.at[here, :], x_ref.at[here, :], x_sem.at[r])
+
+    @pl.when(j == 0)
+    def _():
+        for r in range(rows // TILE):
+            load_x(r).start()
+        pltpu.make_async_copy(featt_hbm, featt, feat_sem).start()
+
+    @pl.when(j == 1)
+    def _():
+        pltpu.make_async_copy(featt_hbm, featt, feat_sem).wait()
 
     def moves(b):
         span = pl.ds(pl.multiple_of(b * bn, bn), bn)
@@ -484,7 +512,17 @@
         dw1a_ref[:half, :] = dot(featt[:half, :], dpre[...])
         dw1b_ref[...] = dot(featt[half:, :], dpre[...])
 
-    @pl.when(j < nb)
+    @pl.when(j == 0)
+    def _():
+        def work(r, carry):
+            load_x(r).wait()
+            here = pl.ds(pl.multiple_of(r * TILE, TILE), TILE)
+            acc[here, :] = dot(x_ref[here, :], w2_ref[...], ((1,), (1,)))
+            return carry
+
+        lax.fori_loop(0, rows // TILE, work, 0)
+
+    @pl.when((j > 0) & (j < nb))
     def _():
         fin()
         mm()
@@ -510,12 +548,13 @@
     return pl.pallas_call(
         functools.partial(back_c_kernel, nb, rows),
         grid=(nb + 2,),
-        in_specs=[pl.BlockSpec((rows, d), lambda j: (0, 0), pipeline_mode=ONCE), pl.BlockSpec((k, rows), lambda j: (0, 0), pipeline_mode=ONCE),
+        in_specs=[any_spec, any_spec,
                   row, pl.BlockSpec((rows, bn), at(1)), col, col, col, col, col, pl.BlockSpec((1, bn), lambda j: (0, 0)), any_spec, any_spec],
         out_specs=[any_spec, any_spec, pl.BlockSpec((k // 2 + 8, bn), at(1)), pl.BlockSpec((k // 2, bn), at(1))],
         out_shape=[jax.ShapeDtypeStruct((d, d), F32)] * 2 + [jax.ShapeDtypeStruct((k // 2 + 8, d), F32), jax.ShapeDtypeStruct((k // 2, d), F32)],
         scratch_shapes=[pltpu.VMEM((rows, bn), F32), pltpu.VMEM((rows, bn), BF16), pltpu.VMEM((2, 2, bn, d), F32),
-                        pltpu.SemaphoreType.DMA((2, 2)), pltpu.SemaphoreType.DMA((2, 2))],
+                        pltpu.VMEM((rows, d), BF16), pltpu.VMEM((k, rows), BF16), pltpu.SemaphoreType.DMA((2, 2)),
+                        pltpu.SemaphoreType.DMA((2, 2)), pltpu.SemaphoreType.DMA((rows // TILE,)), pltpu.SemaphoreType.DMA],
         compiler_params=pltpu.CompilerParams(vmem_limit_bytes=VMEM_LIMIT),
         cost_estimate=pl.CostEstimate(flops=2 * rows * d * (k + d), bytes_accessed=rows * d * 20, transcendentals=0),
         name='back_c',

time: 266 us -> 264 us (level)
  no operation moved by 1% of the time
where the time goes in v9:
time: 264 us
  Pallas kernels  252 us (95%)
  local copies, waits for them, and re-layouts  3.83 us (1%)
  waiting for transfers between devices  3.75 us (1%)
  between operations  3.09 us (1%)
    pallas_call x1, Pallas kernels, back_ab(): pl.pallas_call(functools.partial(back_ab_kernel, nb, rows), grid=(2 * nb...  120 us
    pallas_call x1, Pallas kernels, forward(): pl.pallas_call(functools.partial(forward_kernel, nb, rows), grid=(2 * nb...  88.5 us
    pallas_call x1, Pallas kernels, back_c(): pl.pallas_call(functools.partial(back_c_kernel, nb, rows), grid=(nb + 2,)...  39.6 us
  transfers between devices with their start and end apart: 2, of which 1 were waited for; matrix products, arithmetic and copies ran while one was open for 0% of the time, Pallas kernels for 1%

profile of v9, /device:TPU:0, one launch (start us, length us, event | category | flops | bytes accessed | tf_op | source)
XLA Modules:
  0.0 263.6 jit_solution(10706935742346720647)
XLA Ops:
  1.3 88.5 %forward.1 = (f32[2048,2048]{1,0:T(8,128)}, f32[2048,2048]{1,0:T(8,128)}, f32[2048,2048]{1,0:T(8,128)}, f32[1,2048]{1,0:T(1,128)}, f32[1,2048]{1,0:T(1,128)}, /*...) custom-call(bf16[256,512]{1,0:T(8,128)(2,1)} %fa_ref.1, ...), custom_call_target="tpu_custom_call" | custom-call | flops 38654705664 | bytes 83886080 | tf_op jit(solution)/shard_map/forward/pallas_call | solution.py:212
  89.8 120.3 %back_ab.1 = (f32[1,256]{1,0:T(1,128)}, bf16[2048,2048]{1,0:T(8,128)(2,1)}, f32[1,2048]{1,0:T(1,128)}, f32[1,2048]{1,0:T(1,128)}, f32[2048,2048]{1,0:T(8,128)}, /*index=5*/f32[2048,2048]{1,0:T(8,128)}) custom-call(f32[1,1]{1,0:T(1,128)} %bitcast.9.lam_ref, bf16[2048,2048]{1,0:T(8,128)(2,1)} %get-tuple-element.31.own_ref, ...), custom_call_target="tpu_custom_call" | custom-call | flops 85899345920 | bytes 100663296 | tf_op jit(solution)/shard_map/back_ab/pallas_call | solution.py:436
  210.1 39.6 %back_c.1 = (f32[2048,2048]{1,0:T(8,128)}, f32[2048,2048]{1,0:T(8,128)}, f32[264,2048]{1,0:T(8,128)}, f32[256,2048]{1,0:T(8,128)}) custom-call(bf16[2048,2048]{1,0:T(8,128)(2,1)} %get-tuple-element.39.x_hbm, bf16[512,2048]{1,0:T(8,128)(2,1)} %get-tuple-element.40.featt_hbm, bf16[2048,2048]{1,0:T(8,128)(2,1)} %w2_ref.3, ...), custom_call_target="tpu_custom_call" | custom-call | flops 21474836480 | bytes 83886080 | tf_op jit(solution)/shard_map/back_c/pallas_call | solution.py:548
  249.7 0.3 collective-permute-start
  250.0 0.3 collective-permute-start.1
  250.2 3.7 %collective-permute-done.q_ref = f32[264,2048]{1,0:T(8,128)S(1)} collective-permute-done((f32[264,2048]{1,0:T(8,128)}, f32[264,2048]{1,0:T(8,128)S(1)}, u32[]{:S(2)}, u32[]{:S(2)}) %collective-permute-start) | collective-permute-done | bytes 2162720 | tf_op jit(solution)/shard_map/ppermute | solution.py:602
  254.0 0.0 copy-start
  254.0 1.6 copy-done
  255.6 1.7 add_half.2
  257.3 0.6 slice_reduce_fusion
  258.6 0.6 fusion
  259.2 0.0 collective-permute-done.1.q_ref
  259.2 0.0 copy-start.1
  259.2 1.6 copy-done.1
  260.8 1.7 add_half.3
Async XLA Ops:
  249.7 4.3 %collective-permute-start = (f32[264,2048]{1,0:T(8,128)}, f32[264,2048]{1,0:T(8,128)S(1)}, u32[]{:S(2)}, u32[]{:S(2)}) collective-permute-start(f32[264,2048]{1,0:T(8,128)} %get-tuple-element.48.p_ref), channel_id=1, source_target_pairs={{0,1},{1,0},{2,3},{3,2},{4,5},{5,4},{6,7},{7,6}} | collective-permute-start | bytes 6488072 | tf_op jit(solution)/shard_map/ppermute | solution.py:602
  250.0 9.2 %collective-permute-start.1 = (f32[256,2048]{1,0:T(8,128)}, f32[256,2048]{1,0:T(8,128)S(1)}, u32[]{:S(2)}, u32[]{:S(2)}) collective-permute-start(f32[256,2048]{1,0:T(8,128)} %get-tuple-element.50.p_ref), channel_id=1, source_target_pairs={{0,1},{1,0},{2,3},{3,2},{4,5},{5,4},{6,7},{7,6}} | collective-permute-start | bytes 6291464 | tf_op jit(solution)/shard_map/ppermute | solution.py:602
  254.0 1.6 copy-start
  259.2 1.6 copy-start.1

commit v10 on v9

--- a/solution.py
+++ b/solution.py
@@ -15,6 +15,7 @@
 ONCE = pl.Buffered(1)
 VMEM_LIMIT = 60 * 1024 * 1024
 TILE = 256
+SMALL = 128
 CHUNK = 64
 
 
@@ -28,7 +29,7 @@
 
 def forward_kernel(nb, rows, fa_ref, fb_ref, w1_ref, w2_ref, w3_ref, g1_ref, b1_ref, g2_ref, b2_ref,
                    n1_hbm, n2_ref, n3_ref, i1_ref, i2_ref, i3_ref, t1_ref, t2_ref, xt_ref, emb_hbm, other_hbm,
-                   xs, w1_buf, pre1, sums1, bufa, bufb, acc, w1_sem, norm_sem, copy_sem, feat_sem, send_sem, recv_sem, esend_sem, erecv_sem):
+                   xs, w1_buf, pre1, sums1, bufa, bufb, acc, sums, w1_sem, norm_sem, copy_sem, feat_sem, send_sem, recv_sem, esend_sem, erecv_sem):
     j = pl.program_id(0)
     me = lax.axis_index(AXIS)
     core = lax.rem(me, 2)
@@ -122,14 +123,8 @@
         norm_ref, inv_ref = ((n2_ref, i2_ref), (n3_ref, i3_ref))[layer]
         buf = (bufb, bufa)[layer]
         base = pl.multiple_of(jnp.maximum(j - 1 - layer * nb, 0) * bn, bn)
-        total = jnp.zeros((8, bn), F32)
-        square = jnp.zeros((8, bn), F32)
-        for r in range(0, rows, CHUNK):
-            pre = acc[r:r + CHUNK, :]
-            total += fold(pre)
-            square += fold(pre * pre)
-        mean = jnp.sum(total, axis=0, keepdims=True) / rows
-        inv = lax.rsqrt(jnp.sum(square, axis=0, keepdims=True) / rows - mean * mean + NORM_EPS)
+        mean = jnp.sum(sums[0:8, :], axis=0, keepdims=True) / rows
+        inv = lax.rsqrt(jnp.sum(sums[8:16, :], axis=0, keepdims=True) / rows - mean * mean + NORM_EPS)
         inv_ref[...] = inv
         if layer == 0:
             g, b = g2_ref[...], b2_ref[...]
@@ -145,8 +140,15 @@
 
     def mm(layer):
         x_ref, w_ref = ((bufa, w2_ref), (bufb, w3_ref))[layer]
-        for r in range(0, rows, TILE):
-            acc[r:r + TILE, :] = dot(x_ref[r:r + TILE, :], w_ref[...])
+        total = jnp.zeros((8, bn), F32)
+        square = jnp.zeros((8, bn), F32)
+        for r in range(0, rows, SMALL):
+            pre = dot(x_ref[r:r + SMALL, :], w_ref[...])
+            acc[r:r + SMALL, :] = pre
+            total += fold(pre)
+            square += fold(pre * pre)
+        sums[0:8, :] = total
+        sums[8:16, :] = square
 
     def out_copy(block):
         cols = pl.ds(pl.multiple_of(block * bn, bn), bn)
@@ -219,7 +221,8 @@
         out_shape=[jax.ShapeDtypeStruct((rows, d), F32)] * 3 + [jax.ShapeDtypeStruct((1, d), F32)] * 3
         + [jax.ShapeDtypeStruct((d, rows), BF16)] * 2 + [jax.ShapeDtypeStruct((k, rows), BF16)] + [big] * 2,
         scratch_shapes=[pltpu.VMEM((rows, k), BF16), pltpu.VMEM((k, d), BF16), pltpu.VMEM((rows, d), F32), pltpu.VMEM((16, d), F32),
-                        pltpu.VMEM((rows, d), BF16), pltpu.VMEM((rows, d), BF16), pltpu.VMEM((rows, bn), F32), pltpu.SemaphoreType.DMA, pltpu.SemaphoreType.DMA((nb,)),
+                        pltpu.VMEM((rows, d), BF16), pltpu.VMEM((rows, d), BF16), pltpu.VMEM((rows, bn), F32), pltpu.VMEM((16, bn), F32),
+                        pltpu.SemaphoreType.DMA, pltpu.SemaphoreType.DMA((nb,)),
                         pltpu.SemaphoreType.DMA((nb,)), pltpu.SemaphoreType.DMA, pltpu.SemaphoreType.DMA((7,)), pltpu.SemaphoreType.DMA((7,)),
                         pltpu.SemaphoreType.DMA((nb,)), pltpu.SemaphoreType.DMA((nb,))],
         compiler_params=pltpu.CompilerParams(collective_id=0, has_side_effects=True, vmem_limit_bytes=63 * 1024 * 1024),
@@ -228,30 +231,35 @@
     )(fa, fb, w1, w2, w3, g1, b1, g2, b2)
 
 
-def finish_back(rows, acc, norm_ref, inv, g, b, put):
-    bn = acc.shape[1]
-    total = jnp.zeros((8, bn), F32)
-    cross = jnp.zeros((8, bn), F32)
-    for r in range(0, rows, CHUNK):
-        part = acc[r:r + CHUNK, :]
-        norm = norm_ref[r:r + CHUNK, :]
+def first_pass(products, acc, keep, sums, norm_ref, g, b):
+    total = jnp.zeros((8, acc.shape[1]), F32)
+    cross = jnp.zeros((8, acc.shape[1]), F32)
+    for r, part in products:
+        here = pl.ds(r, part.shape[0])
+        norm = norm_ref[here, :]
+        keep[here, :] = norm
         if b is not None:
             part = jnp.where(norm * g + b > 0.0, part, 0.0)
-            acc[r:r + CHUNK, :] = part
+        acc[here, :] = part
         total += fold(part)
         cross += fold(part * norm)
-    total = jnp.sum(total, axis=0, keepdims=True)
-    cross = jnp.sum(cross, axis=0, keepdims=True)
+    sums[0:8, :] = total
+    sums[8:16, :] = cross
+
+
+def second_pass(rows, acc, keep, sums, inv, g, put):
+    total = jnp.sum(sums[0:8, :], axis=0, keepdims=True)
+    cross = jnp.sum(sums[8:16, :], axis=0, keepdims=True)
     scale = inv if g is None else inv * g
     shift, slope = scale * (total / rows), scale * (cross / rows)
     for r in range(0, rows, CHUNK):
-        put(r, (acc[r:r + CHUNK, :] * scale - shift - norm_ref[r:r + CHUNK, :] * slope).astype(BF16))
+        put(r, (acc[r:r + CHUNK, :] * scale - shift - keep[r:r + CHUNK, :] * slope).astype(BF16))
     return total, cross
 
 
-def back_ab_kernel(nb, rows, lam_ref, own_ref, other_hbm, n3_ref, i3_ref, w3_ref, n2_ref, i2_ref, g2_ref, b2_ref, t2_ref, t1_hbm,
+def back_ab_kernel(nb, rows, lam_ref, own_ref, other_hbm, n3_ref, i3_ref, w3_ref, n2_ref, i2_ref, g2d_ref, g2_ref, b2_ref, t2_ref, t1_hbm,
                    loss_ref, dpre_ref, dg_ref, db_ref, dw3_hbm, dw2_hbm,
-                   big, corr, grad, acc, dout, send3, recv3, send2, recv2, load_sem, chunk_sem, ssem, rsem, osem, free3, free2):
+                   big, corr, grad, acc, keep, sums, dout, send3, recv3, send2, recv2, load_sem, chunk_sem, ssem, rsem, osem, free3, free2):
     j = pl.program_id(0)
     me = lax.axis_index(AXIS)
     partner = me + 1 - 2 * lax.rem(me, 2)
@@ -310,7 +318,7 @@
         def put(r, v):
             dout[r:r + CHUNK, pl.ds(base, bn)] = v
 
-        finish_back(rows, acc, n3_ref, i3_ref[...], None, None, put)
+        second_pass(rows, acc, keep, sums, i3_ref[...], None, put)
 
     def load_other(c):
         cols = pl.ds(pl.multiple_of(c * bn, bn), bn)
@@ -340,18 +348,18 @@
         grad[:, here] = jnp.where(diag, -2.0 * (1.0 - part), (2.0 * lam) * part).astype(BF16)
         loss = lam * loss + fold(jnp.where(diag, (1.0 - part) * (1.0 - part) - lam * (part * part), 0.0))
         loss_ref[...] += jnp.sum(loss, axis=0, keepdims=True)
-        for r in range(0, rows, TILE):
-            acc[r:r + TILE, :] = dot(other_ref[r:r + TILE, :], grad[...], ((1,), (1,))) * (1.0 / rows)
+        first_pass(((r, dot(other_ref[r:r + TILE, :], grad[...], ((1,), (1,))) * (1.0 / rows)) for r in range(0, rows, TILE)),
+                   acc, keep, sums, n3_ref, None, None)
 
     def fin_two():
         def put(r, v):
             dpre_ref[r:r + CHUNK, :] = v
 
-        db_ref[...], dg_ref[...] = finish_back(rows, acc, n2_ref, i2_ref[...], g2_ref[...], b2_ref[...], put)
+        db_ref[...], dg_ref[...] = second_pass(rows, acc, keep, sums, i2_ref[...], g2d_ref[...], put)
 
     def mm_two():
-        for r in range(0, rows, TILE):
-            acc[r:r + TILE, :] = dot(dout[r:r + TILE, :], w3_ref[...], ((1,), (1,)))
+        first_pass(((r, dot(dout[r:r + TILE, :], w3_ref[...], ((1,), (1,)))) for r in range(0, rows, TILE)),
+                   acc, keep, sums, n2_ref, g2_ref[...], b2_ref[...])
         act = t2_ref[...]
         slot = lax.rem(j - nb, 2)
         for c in range(0, d, 2 * bn):
@@ -359,8 +367,8 @@
 
     def mm_dw2(first, last):
         slot = lax.rem(j - nb - 1, 2)
-        for r in range(first, last, TILE):
-            send2[slot, r:r + TILE, :] = dot(big[r:r + TILE, :], dpre_ref[...])
+        for r in range(first, last, SMALL):
+            send2[slot, r:r + SMALL, :] = dot(big[r:r + SMALL, :], dpre_ref[...])
 
     @pl.when(j == 0)
     def _():
@@ -437,11 +445,12 @@
         functools.partial(back_ab_kernel, nb, rows),
         grid=(2 * nb + 4,),
         in_specs=[pl.BlockSpec(memory_space=pltpu.SMEM), block(0), any_spec,
-                  block(1), col(1), row, block(nb + 1), col(nb + 1), col(nb + 1), col(nb + 1), row, any_spec],
+                  block(0), col(1), row, block(nb), col(nb + 1), col(nb + 1), col(nb), col(nb), row, any_spec],
         out_specs=[pl.BlockSpec((1, bn), lambda j: (0, 0)), block(nb + 1), col(nb + 1), col(nb + 1), any_spec, any_spec],
         out_shape=[jax.ShapeDtypeStruct((1, bn), F32), jax.ShapeDtypeStruct((rows, d), BF16), vec, vec]
         + [jax.ShapeDtypeStruct((d, d), F32)] * 2,
         scratch_shapes=[pltpu.VMEM((rows, d), BF16), pltpu.VMEM((bn, d), F32), pltpu.VMEM((bn, d), BF16), pltpu.VMEM((rows, bn), F32),
+                        pltpu.VMEM((rows, bn), F32), pltpu.VMEM((16, bn), F32),
                         pltpu.VMEM((rows, d), BF16), pltpu.VMEM((2, bn, d), F32), pltpu.VMEM((3, bn, d), F32),
                         pltpu.VMEM((2, d, bn), F32), pltpu.VMEM((3, d, bn), F32), pltpu.SemaphoreType.DMA, pltpu.SemaphoreType.DMA((nb,)),
                         pltpu.SemaphoreType.DMA((2, 2)), pltpu.SemaphoreType.DMA((2, 3)), pltpu.SemaphoreType.DMA((2, 3)),
@@ -449,11 +458,11 @@
         compiler_params=pltpu.CompilerParams(collective_id=1, has_side_effects=True, vmem_limit_bytes=63 * 1024 * 1024),
         cost_estimate=pl.CostEstimate(flops=10 * rows * d * d, bytes_accessed=rows * d * 24, transcendentals=0),
         name='back_ab',
-    )(lam, own, other, n3, i3, w3, n2, i2, g2, b2, t2, t1)
-
-
-def back_c_kernel(nb, rows, x_hbm, featt_hbm, w2_ref, n1_ref, i1_ref, g1_ref, b1_ref, dg2_ref, db2_ref, loss_ref, p_ref, q_ref,
-                  p_out, q_out, dw1a_ref, dw1b_ref, acc, dpre, ring, x_ref, featt, load_sem, store_sem, x_sem, feat_sem):
+    )(lam, own, other, n3, i3, w3, n2, i2, g2, g2, b2, t2, t1)
+
+
+def back_c_kernel(nb, rows, x_hbm, featt_hbm, w2_ref, n1_ref, i1_ref, g1d_ref, g1_ref, b1_ref, dg2_ref, db2_ref, loss_ref, p_ref, q_ref,
+                  p_out, q_out, dw1a_ref, dw1b_ref, acc, keep, sums, dpre, ring, x_ref, featt, load_sem, store_sem, x_sem, feat_sem):
     j = pl.program_id(0)
     bn = acc.shape[1]
 
@@ -498,14 +507,14 @@
         def put(r, v):
             dpre[r:r + CHUNK, :] = v
 
-        db, dg = finish_back(rows, acc, n1_ref, i1_ref[...], g1_ref[...], b1_ref[...], put)
+        db, dg = second_pass(rows, acc, keep, sums, i1_ref[...], g1d_ref[...], put)
         half = dw1b_ref.shape[0]
         for i, row in enumerate((dg, db, dg2_ref[...], db2_ref[...], loss_ref[...])):
             dw1a_ref[half + i:half + i + 1, :] = row
 
     def mm():
-        for r in range(0, rows, TILE):
-            acc[r:r + TILE, :] = dot(x_ref[r:r + TILE, :], w2_ref[...], ((1,), (1,)))
+        first_pass(((r, dot(x_ref[r:r + TILE, :], w2_ref[...], ((1,), (1,)))) for r in range(0, rows, TILE)),
+                   acc, keep, sums, n1_ref, g1_ref[...], b1_ref[...])
 
     def dw():
         half = dw1b_ref.shape[0]
@@ -517,10 +526,14 @@
         def work(r, carry):
             load_x(r).wait()
             here = pl.ds(pl.multiple_of(r * TILE, TILE), TILE)
-            acc[here, :] = dot(x_ref[here, :], w2_ref[...], ((1,), (1,)))
-            return carry
-
-        lax.fori_loop(0, rows // TILE, work, 0)
+            norm = n1_ref[here, :]
+            keep[here, :] = norm
+            part = jnp.where(norm * g1_ref[...] + b1_ref[...] > 0.0, dot(x_ref[here, :], w2_ref[...], ((1,), (1,))), 0.0)
+            acc[here, :] = part
+            return carry[0] + fold(part), carry[1] + fold(part * norm)
+
+        zero = jnp.zeros((8, bn), F32)
+        sums[0:8, :], sums[8:16, :] = lax.fori_loop(0, rows // TILE, work, (zero, zero))
 
     @pl.when((j > 0) & (j < nb))
     def _():
@@ -542,23 +555,24 @@
     def at(first):
         return lambda j: (0, jnp.clip(j - first, 0, nb - 1))
 
-    col = pl.BlockSpec((1, bn), at(1))
+    col, now = pl.BlockSpec((1, bn), at(1)), pl.BlockSpec((1, bn), at(0))
     row = pl.BlockSpec((bn, d), lambda j: (jnp.minimum(j, nb - 1), 0))
     any_spec = pl.BlockSpec(memory_space=pl.ANY)
     return pl.pallas_call(
         functools.partial(back_c_kernel, nb, rows),
         grid=(nb + 2,),
         in_specs=[any_spec, any_spec,
-                  row, pl.BlockSpec((rows, bn), at(1)), col, col, col, col, col, pl.BlockSpec((1, bn), lambda j: (0, 0)), any_spec, any_spec],
+                  row, pl.BlockSpec((rows, bn), at(0)), col, col, now, now, col, col, pl.BlockSpec((1, bn), lambda j: (0, 0)), any_spec, any_spec],
         out_specs=[any_spec, any_spec, pl.BlockSpec((k // 2 + 8, bn), at(1)), pl.BlockSpec((k // 2, bn), at(1))],
         out_shape=[jax.ShapeDtypeStruct((d, d), F32)] * 2 + [jax.ShapeDtypeStruct((k // 2 + 8, d), F32), jax.ShapeDtypeStruct((k // 2, d), F32)],
-        scratch_shapes=[pltpu.VMEM((rows, bn), F32), pltpu.VMEM((rows, bn), BF16), pltpu.VMEM((2, 2, bn, d), F32),
+        scratch_shapes=[pltpu.VMEM((rows, bn), F32), pltpu.VMEM((rows, bn), F32), pltpu.VMEM((16, bn), F32),
+                        pltpu.VMEM((rows, bn), BF16), pltpu.VMEM((2, 2, bn, d), F32),
                         pltpu.VMEM((rows, d), BF16), pltpu.VMEM((k, rows), BF16), pltpu.SemaphoreType.DMA((2, 2)),
                         pltpu.SemaphoreType.DMA((2, 2)), pltpu.SemaphoreType.DMA((rows // TILE,)), pltpu.SemaphoreType.DMA],
         compiler_params=pltpu.CompilerParams(vmem_limit_bytes=VMEM_LIMIT),
         cost_estimate=pl.CostEstimate(flops=2 * rows * d * (k + d), bytes_accessed=rows * d * 20, transcendentals=0),
         name='back_c',
-    )(x, featt, w2, n1, i1, g1, b1, dg2, db2, loss, p, q)
+    )(x, featt, w2, n1, i1, g1, g1, b1, dg2, db2, loss, p, q)
 
 
 def add_first_kernel(p_ref, q_ref, out_ref, small_ref):

time: 264 us -> 263 us (level)
    pallas_call x1, Pallas kernels: 88.5 us -> 85.4 us  [forward(): pl.pallas_call(functools.partial(forward_kernel, nb, rows), grid=(2 * nb...]
where the time goes in v10:
time: 263 us; the launch traced here: 262 us
  Pallas kernels  251 us (95%)
  local copies, waits for them, and re-layouts  3.83 us (1%)
  waiting for transfers between devices  3.75 us (1%)
  between operations  3.09 us (1%)
    pallas_call x1, Pallas kernels, back_ab(): pl.pallas_call(functools.partial(back_ab_kernel, nb, rows), grid=(2 * nb...  121 us
    pallas_call x1, Pallas kernels, forward(): pl.pallas_call(functools.partial(forward_kernel, nb, rows), grid=(2 * nb...  85.4 us
    pallas_call x1, Pallas kernels, back_c(): pl.pallas_call(functools.partial(back_c_kernel, nb, rows), grid=(nb + 2,)...  40.5 us
  transfers between devices with their start and end apart: 2, of which 1 were waited for; matrix products, arithmetic and copies ran while one was open for 0% of the time, Pallas kernels for 1%

profile of v10, /device:TPU:0, one launch (start us, length us, event | category | flops | bytes accessed | tf_op | source)
XLA Modules:
  0.0 262.4 jit_solution(3126464552772015792)
XLA Ops:
  1.3 85.4 %forward.1 = (f32[2048,2048]{1,0:T(8,128)}, f32[2048,2048]{1,0:T(8,128)}, f32[2048,2048]{1,0:T(8,128)}, f32[1,2048]{1,0:T(1,128)}, f32[1,2048]{1,0:T(1,128)}, /*...) custom-call(bf16[256,512]{1,0:T(8,128)(2,1)} %fa_ref.1, ...), custom_call_target="tpu_custom_call" | custom-call | flops 38654705664 | bytes 83886080 | tf_op jit(solution)/shard_map/forward/pallas_call | solution.py:214
  86.7 121.3 %back_ab.1 = (f32[1,256]{1,0:T(1,128)}, bf16[2048,2048]{1,0:T(8,128)(2,1)}, f32[1,2048]{1,0:T(1,128)}, f32[1,2048]{1,0:T(1,128)}, f32[2048,2048]{1,0:T(8,128)}, /*index=5*/f32[2048,2048]{1,0:T(8,128)}) custom-call(f32[1,1]{1,0:T(1,128)} %bitcast.9.lam_ref, bf16[2048,2048]{1,0:T(8,128)(2,1)} %get-tuple-element.31.own_ref, ...), custom_call_target="tpu_custom_call" | custom-call | flops 85899345920 | bytes 100663296 | tf_op jit(solution)/shard_map/back_ab/pallas_call | solution.py:444
  208.0 40.5 %back_c.1 = (f32[2048,2048]{1,0:T(8,128)}, f32[2048,2048]{1,0:T(8,128)}, f32[264,2048]{1,0:T(8,128)}, f32[256,2048]{1,0:T(8,128)}) custom-call(bf16[2048,2048]{1,0:T(8,128)(2,1)} %get-tuple-element.39.x_hbm, bf16[512,2048]{1,0:T(8,128)(2,1)} %get-tuple-element.40.featt_hbm, bf16[2048,2048]{1,0:T(8,128)(2,1)} %w2_ref.3, ...), custom_call_target="tpu_custom_call" | custom-call | flops 21474836480 | bytes 83886080 | tf_op jit(solution)/shard_map/back_c/pallas_call | solution.py:561
  248.5 0.2 collective-permute-start
  248.7 0.3 collective-permute-start.1
  249.0 3.7 %collective-permute-done.q_ref = f32[264,2048]{1,0:T(8,128)S(1)} collective-permute-done((f32[264,2048]{1,0:T(8,128)}, f32[264,2048]{1,0:T(8,128)S(1)}, u32[]{:S(2)}, u32[]{:S(2)}) %collective-permute-start) | collective-permute-done | bytes 2162720 | tf_op jit(solution)/shard_map/ppermute | solution.py:616
  252.7 0.0 copy-start
  252.7 1.6 copy-done
  254.4 1.7 add_half.2
  256.1 0.6 slice_reduce_fusion
  257.3 0.6 fusion
  258.0 0.0 collective-permute-done.1.q_ref
  258.0 0.0 copy-start.1
  258.0 1.6 copy-done.1
  259.6 1.7 add_half.3
Async XLA Ops:
  248.5 4.3 %collective-permute-start = (f32[264,2048]{1,0:T(8,128)}, f32[264,2048]{1,0:T(8,128)S(1)}, u32[]{:S(2)}, u32[]{:S(2)}) collective-permute-start(f32[264,2048]{1,0:T(8,128)} %get-tuple-element.48.p_ref), channel_id=1, source_target_pairs={{0,1},{1,0},{2,3},{3,2},{4,5},{5,4},{6,7},{7,6}} | collective-permute-start | bytes 6488072 | tf_op jit(solution)/shard_map/ppermute | solution.py:616
  248.7 9.3 %collective-permute-start.1 = (f32[256,2048]{1,0:T(8,128)}, f32[256,2048]{1,0:T(8,128)S(1)}, u32[]{:S(2)}, u32[]{:S(2)}) collective-permute-start(f32[256,2048]{1,0:T(8,128)} %get-tuple-element.50.p_ref), channel_id=1, source_target_pairs={{0,1},{1,0},{2,3},{3,2},{4,5},{5,4},{6,7},{7,6}} | collective-permute-start | bytes 6291464 | tf_op jit(solution)/shard_map/ppermute | solution.py:616
  252.7 1.6 copy-start
  258.0 1.6 copy-start.1

commit v11 on v9

--- a/solution.py
+++ b/solution.py
@@ -15,6 +15,7 @@
 ONCE = pl.Buffered(1)
 VMEM_LIMIT = 60 * 1024 * 1024
 TILE = 256
+SMALL = 128
 CHUNK = 64
 
 
@@ -28,7 +29,7 @@
 
 def forward_kernel(nb, rows, fa_ref, fb_ref, w1_ref, w2_ref, w3_ref, g1_ref, b1_ref, g2_ref, b2_ref,
                    n1_hbm, n2_ref, n3_ref, i1_ref, i2_ref, i3_ref, t1_ref, t2_ref, xt_ref, emb_hbm, other_hbm,
-                   xs, w1_buf, pre1, sums1, bufa, bufb, acc, w1_sem, norm_sem, copy_sem, feat_sem, send_sem, recv_sem, esend_sem, erecv_sem):
+                   xs, w1_buf, pre1, sums1, bufa, bufb, acc, sums, w1_sem, norm_sem, copy_sem, feat_sem, send_sem, recv_sem, esend_sem, erecv_sem):
     j = pl.program_id(0)
     me = lax.axis_index(AXIS)
     core = lax.rem(me, 2)
@@ -122,14 +123,8 @@
         norm_ref, inv_ref = ((n2_ref, i2_ref), (n3_ref, i3_ref))[layer]
         buf = (bufb, bufa)[layer]
         base = pl.multiple_of(jnp.maximum(j - 1 - layer * nb, 0) * bn, bn)
-        total = jnp.zeros((8, bn), F32)
-        square = jnp.zeros((8, bn), F32)
-        for r in range(0, rows, CHUNK):
-            pre = acc[r:r + CHUNK, :]
-            total += fold(pre)
-            square += fold(pre * pre)
-        mean = jnp.sum(total, axis=0, keepdims=True) / rows
-        inv = lax.rsqrt(jnp.sum(square, axis=0, keepdims=True) / rows - mean * mean + NORM_EPS)
+        mean = jnp.sum(sums[0:8, :], axis=0, keepdims=True) / rows
+        inv = lax.rsqrt(jnp.sum(sums[8:16, :], axis=0, keepdims=True) / rows - mean * mean + NORM_EPS)
         inv_ref[...] = inv
         if layer == 0:
             g, b = g2_ref[...], b2_ref[...]
@@ -145,8 +140,15 @@
 
     def mm(layer):
         x_ref, w_ref = ((bufa, w2_ref), (bufb, w3_ref))[layer]
-        for r in range(0, rows, TILE):
-            acc[r:r + TILE, :] = dot(x_ref[r:r + TILE, :], w_ref[...])
+        total = jnp.zeros((8, bn), F32)
+        square = jnp.zeros((8, bn), F32)
+        for r in range(0, rows, SMALL):
+            pre = dot(x_ref[r:r + SMALL, :], w_ref[...])
+            acc[r:r + SMALL, :] = pre
+            total += fold(pre)
+            square += fold(pre * pre)
+        sums[0:8, :] = total
+        sums[8:16, :] = square
 
     def out_copy(block):
         cols = pl.ds(pl.multiple_of(block * bn, bn), bn)
@@ -219,7 +221,8 @@
         out_shape=[jax.ShapeDtypeStruct((rows, d), F32)] * 3 + [jax.ShapeDtypeStruct((1, d), F32)] * 3
         + [jax.ShapeDtypeStruct((d, rows), BF16)] * 2 + [jax.ShapeDtypeStruct((k, rows), BF16)] + [big] * 2,
         scratch_shapes=[pltpu.VMEM((rows, k), BF16), pltpu.VMEM((k, d), BF16), pltpu.VMEM((rows, d), F32), pltpu.VMEM((16, d), F32),
-                        pltpu.VMEM((rows, d), BF16), pltpu.VMEM((rows, d), BF16), pltpu.VMEM((rows, bn), F32), pltpu.SemaphoreType.DMA, pltpu.SemaphoreType.DMA((nb,)),
+                        pltpu.VMEM((rows, d), BF16), pltpu.VMEM((rows, d), BF16), pltpu.VMEM((rows, bn), F32), pltpu.VMEM((16, bn), F32),
+                        pltpu.SemaphoreType.DMA, pltpu.SemaphoreType.DMA((nb,)),
                         pltpu.SemaphoreType.DMA((nb,)), pltpu.SemaphoreType.DMA, pltpu.SemaphoreType.DMA((7,)), pltpu.SemaphoreType.DMA((7,)),
                         pltpu.SemaphoreType.DMA((nb,)), pltpu.SemaphoreType.DMA((nb,))],
         compiler_params=pltpu.CompilerParams(collective_id=0, has_side_effects=True, vmem_limit_bytes=63 * 1024 * 1024),

time: 264 us -> 261 us (0.989)
  Pallas kernels: 252 us -> 249 us
    pallas_call x1, Pallas kernels: 88.5 us -> 85.4 us  [forward(): pl.pallas_call(functools.partial(forward_kernel, nb, rows), grid=(2 * nb...]
where the time goes in v11:
time: 261 us
  Pallas kernels  249 us (95%)
  local copies, waits for them, and re-layouts  3.83 us (1%)
  waiting for transfers between devices  3.75 us (1%)
  between operations  3.09 us (1%)
    pallas_call x1, Pallas kernels, back_ab(): pl.pallas_call(functools.partial(back_ab_kernel, nb, rows), grid=(2 * nb...  120 us
    pallas_call x1, Pallas kernels, forward(): pl.pallas_call(functools.partial(forward_kernel, nb, rows), grid=(2 * nb...  85.4 us
    pallas_call x1, Pallas kernels, back_c(): pl.pallas_call(functools.partial(back_c_kernel, nb, rows), grid=(nb + 2,)...  39.6 us
  transfers between devices with their start and end apart: 2, of which 1 were waited for; matrix products, arithmetic and copies ran while one was open for 0% of the time, Pallas kernels for 1%

profile of v11, /device:TPU:0, one launch (start us, length us, event | category | flops | bytes accessed | tf_op | source)
XLA Modules:
  0.0 260.5 jit_solution(15365442860735728076)
XLA Ops:
  1.3 85.4 %forward.1 = (f32[2048,2048]{1,0:T(8,128)}, f32[2048,2048]{1,0:T(8,128)}, f32[2048,2048]{1,0:T(8,128)}, f32[1,2048]{1,0:T(1,128)}, f32[1,2048]{1,0:T(1,128)}, /*...) custom-call(bf16[256,512]{1,0:T(8,128)(2,1)} %fa_ref.1, ...), custom_call_target="tpu_custom_call" | custom-call | flops 38654705664 | bytes 83886080 | tf_op jit(solution)/shard_map/forward/pallas_call | solution.py:214
  86.7 120.3 %back_ab.1 = (f32[1,256]{1,0:T(1,128)}, bf16[2048,2048]{1,0:T(8,128)(2,1)}, f32[1,2048]{1,0:T(1,128)}, f32[1,2048]{1,0:T(1,128)}, f32[2048,2048]{1,0:T(8,128)}, /*index=5*/f32[2048,2048]{1,0:T(8,128)}) custom-call(f32[1,1]{1,0:T(1,128)} %bitcast.9.lam_ref, bf16[2048,2048]{1,0:T(8,128)(2,1)} %get-tuple-element.31.own_ref, ...), custom_call_target="tpu_custom_call" | custom-call | flops 85899345920 | bytes 100663296 | tf_op jit(solution)/shard_map/back_ab/pallas_call | solution.py:439
  207.0 39.6 %back_c.1 = (f32[2048,2048]{1,0:T(8,128)}, f32[2048,2048]{1,0:T(8,128)}, f32[264,2048]{1,0:T(8,128)}, f32[256,2048]{1,0:T(8,128)}) custom-call(bf16[2048,2048]{1,0:T(8,128)(2,1)} %get-tuple-element.39.x_hbm, bf16[512,2048]{1,0:T(8,128)(2,1)} %get-tuple-element.40.featt_hbm, bf16[2048,2048]{1,0:T(8,128)(2,1)} %w2_ref.3, ...), custom_call_target="tpu_custom_call" | custom-call | flops 21474836480 | bytes 83886080 | tf_op jit(solution)/shard_map/back_c/pallas_call | solution.py:551
  246.6 0.3 collective-permute-start
  246.9 0.3 collective-permute-start.1
  247.1 3.7 %collective-permute-done.q_ref = f32[264,2048]{1,0:T(8,128)S(1)} collective-permute-done((f32[264,2048]{1,0:T(8,128)}, f32[264,2048]{1,0:T(8,128)S(1)}, u32[]{:S(2)}, u32[]{:S(2)}) %collective-permute-start) | collective-permute-done | bytes 2162720 | tf_op jit(solution)/shard_map/ppermute | solution.py:605
  250.9 0.0 copy-start
  250.9 1.6 copy-done
  252.5 1.7 add_half.2
  254.2 0.6 slice_reduce_fusion
  255.4 0.6 fusion
  256.1 0.0 collective-permute-done.1.q_ref
  256.1 0.0 copy-start.1
  256.1 1.6 copy-done.1
  257.7 1.7 add_half.3
Async XLA Ops:
  246.6 4.3 %collective-permute-start = (f32[264,2048]{1,0:T(8,128)}, f32[264,2048]{1,0:T(8,128)S(1)}, u32[]{:S(2)}, u32[]{:S(2)}) collective-permute-start(f32[264,2048]{1,0:T(8,128)} %get-tuple-element.48.p_ref), channel_id=1, source_target_pairs={{0,1},{1,0},{2,3},{3,2},{4,5},{5,4},{6,7},{7,6}} | collective-permute-start | bytes 6488072 | tf_op jit(solution)/shard_map/ppermute | solution.py:605
  246.9 9.2 %collective-permute-start.1 = (f32[256,2048]{1,0:T(8,128)}, f32[256,2048]{1,0:T(8,128)S(1)}, u32[]{:S(2)}, u32[]{:S(2)}) collective-permute-start(f32[256,2048]{1,0:T(8,128)} %get-tuple-element.50.p_ref), channel_id=1, source_target_pairs={{0,1},{1,0},{2,3},{3,2},{4,5},{5,4},{6,7},{7,6}} | collective-permute-start | bytes 6291464 | tf_op jit(solution)/shard_map/ppermute | solution.py:605
  250.9 1.6 copy-start
  256.1 1.6 copy-start.1

commit v12 on v11

--- a/solution.py
+++ b/solution.py
@@ -564,17 +564,23 @@
     )(x, featt, w2, n1, i1, g1, b1, dg2, db2, loss, p, q)
 
 
-def add_first_kernel(p_ref, q_ref, out_ref, small_ref):
+def add_first_kernel(loss_width, p_ref, q_ref, out_ref, dg1_ref, db1_ref, dg2_ref, db2_ref, loss_ref):
     half = out_ref.shape[0]
     out_ref[...] = p_ref[:half, :] + q_ref[:half, :]
-    small_ref[...] = p_ref[half:, :] + q_ref[half:, :]
+    small = p_ref[half:, :] + q_ref[half:, :]
+    for i, ref in enumerate((dg1_ref, db1_ref, dg2_ref, db2_ref)):
+        ref[...] = small[i:i + 1, :]
+
+    @pl.when(pl.program_id(0) == 0)
+    def _():
+        loss_ref[0, 0] = jnp.sum(small[4:5, :loss_width]) * 0.5
 
 
 def add_second_kernel(p_ref, q_ref, _, out_ref):
     out_ref[...] = p_ref[...] + q_ref[...]
 
 
-def add_half(p, q, half, whole=None):
+def add_half(p, q, half, whole=None, loss_width=0):
     rows, d = p.shape
     blk = d // 2
     spec = pl.BlockSpec((rows, blk), lambda j: (0, j))
@@ -582,10 +588,10 @@
     out_specs = [pl.BlockSpec((half, blk), lambda j: (0 if first else 1, j))]
     out_shape = [jax.ShapeDtypeStruct((2 * half, d), F32)]
     if first:
-        out_specs.append(pl.BlockSpec((rows - half, blk), lambda j: (0, j)))
-        out_shape.append(jax.ShapeDtypeStruct((rows - half, d), F32))
+        out_specs += [pl.BlockSpec((1, blk), lambda j: (0, j))] * 4 + [pl.BlockSpec(memory_space=pltpu.SMEM)]
+        out_shape += [jax.ShapeDtypeStruct((1, d), F32)] * 4 + [jax.ShapeDtypeStruct((1, 1), F32)]
     return pl.pallas_call(
-        add_first_kernel if first else add_second_kernel,
+        functools.partial(add_first_kernel, loss_width) if first else add_second_kernel,
         grid=(2,),
         in_specs=[spec, spec] + ([] if first else [pl.BlockSpec(memory_space=pl.ANY)]),
         out_specs=out_specs,
@@ -613,10 +619,10 @@
             lam_off.reshape(1, 1), emb, other, norm3, inv3, w_three, norm2, inv2, g2, b2, act2t, act1t)
         dw3, dw2, dw1a, dw1b = back_c(d_pre2, xt, w_two, norm1, inv1, g1, b1, dg2, db2, loss, dw3, dw2)
         half = dw1b.shape[0]
-        dw1, small = add_half(dw1a, swap(dw1a), half)
+        dw1, dg1, db1, dg2, db2, loss = add_half(dw1a, swap(dw1a), half, loss_width=loss.shape[1])
         dw1, = add_half(dw1b, swap(dw1b), half, dw1)
-        dg1, db1, dg2, db2 = (small[i] for i in range(4))
-        loss_val = jnp.sum(small[4, :loss.shape[1]]) * 0.5
+        dg1, db1, dg2, db2 = (v.reshape(width) for v in (dg1, db1, dg2, db2))
+        loss_val = loss.reshape(())
         return (loss_val, dw1, dw2, dw3, dg1, db1, dg2, db2)
 
     row_spec = P(AXIS, None)

time: 261 us -> 258 us (0.989)
  no operation moved by 1% of the time
where the time goes in v12:
time: 258 us
  Pallas kernels  249 us (97%)
  waiting for transfers between devices  3.75 us (1%)
  local copies, waits for them, and re-layouts  3.19 us (1%)
    pallas_call x1, Pallas kernels, back_ab(): pl.pallas_call(functools.partial(back_ab_kernel, nb, rows), grid=(2 * nb...  120 us
    pallas_call x1, Pallas kernels, forward(): pl.pallas_call(functools.partial(forward_kernel, nb, rows), grid=(2 * nb...  85.5 us
    pallas_call x1, Pallas kernels, back_c(): pl.pallas_call(functools.partial(back_c_kernel, nb, rows), grid=(nb + 2,)...  39.5 us
  transfers between devices with their start and end apart: 2, of which 1 were waited for; matrix products, arithmetic and copies ran while one was open for 0% of the time, Pallas kernels for 1%

profile of v12, /device:TPU:0, one launch (start us, length us, event | category | flops | bytes accessed | tf_op | source)
XLA Modules:
  0.0 257.6 jit_solution(16497658736330985979)
XLA Ops:
  1.3 85.5 %forward.1 = (f32[2048,2048]{1,0:T(8,128)}, f32[2048,2048]{1,0:T(8,128)}, f32[2048,2048]{1,0:T(8,128)}, f32[1,2048]{1,0:T(1,128)}, f32[1,2048]{1,0:T(1,128)}, /*...) custom-call(bf16[256,512]{1,0:T(8,128)(2,1)} %fa_ref.1, ...), custom_call_target="tpu_custom_call" | custom-call | flops 38654705664 | bytes 83886080 | tf_op jit(solution)/shard_map/forward/pallas_call | solution.py:214
  86.7 120.2 %back_ab.1 = (f32[1,256]{1,0:T(1,128)}, bf16[2048,2048]{1,0:T(8,128)(2,1)}, f32[1,2048]{1,0:T(1,128)}, f32[1,2048]{1,0:T(1,128)}, f32[2048,2048]{1,0:T(8,128)}, /*index=5*/f32[2048,2048]{1,0:T(8,128)}) custom-call(f32[1,1]{1,0:T(1,128)} %bitcast.10.lam_ref, bf16[2048,2048]{1,0:T(8,128)(2,1)} %get-tuple-element.35.own_ref, ...), custom_call_target="tpu_custom_call" | custom-call | flops 85899345920 | bytes 100663296 | tf_op jit(solution)/shard_map/back_ab/pallas_call | solution.py:439
  206.9 39.5 %back_c.1 = (f32[2048,2048]{1,0:T(8,128)}, f32[2048,2048]{1,0:T(8,128)}, f32[264,2048]{1,0:T(8,128)}, f32[256,2048]{1,0:T(8,128)}) custom-call(bf16[2048,2048]{1,0:T(8,128)(2,1)} %get-tuple-element.43.x_hbm, bf16[512,2048]{1,0:T(8,128)(2,1)} %get-tuple-element.44.featt_hbm, bf16[2048,2048]{1,0:T(8,128)(2,1)} %w2_ref.3, ...), custom_call_target="tpu_custom_call" | custom-call | flops 21474836480 | bytes 83886080 | tf_op jit(solution)/shard_map/back_c/pallas_call | solution.py:551
  246.5 0.3 collective-permute-start
  246.8 0.2 collective-permute-start.1
  247.0 3.7 %collective-permute-done.q_ref = f32[264,2048]{1,0:T(8,128)S(1)} collective-permute-done((f32[264,2048]{1,0:T(8,128)}, f32[264,2048]{1,0:T(8,128)S(1)}, u32[]{:S(2)}, u32[]{:S(2)}) %collective-permute-start) | collective-permute-done | bytes 2162720 | tf_op jit(solution)/shard_map/ppermute | solution.py:611
  250.7 0.0 copy-start
  250.7 1.6 copy-done
  252.3 1.9 add_half.2
  254.2 0.0 collective-permute-done.1.q_ref
  254.2 0.0 copy-start.1
  254.3 1.6 copy-done.1
  255.8 1.7 add_half.3
Async XLA Ops:
  246.5 4.3 %collective-permute-start = (f32[264,2048]{1,0:T(8,128)}, f32[264,2048]{1,0:T(8,128)S(1)}, u32[]{:S(2)}, u32[]{:S(2)}) collective-permute-start(f32[264,2048]{1,0:T(8,128)} %get-tuple-element.52.p_ref), channel_id=1, source_target_pairs={{0,1},{1,0},{2,3},{3,2},{4,5},{5,4},{6,7},{7,6}} | collective-permute-start | bytes 6488072 | tf_op jit(solution)/shard_map/ppermute | solution.py:611
  246.8 7.5 %collective-permute-start.1 = (f32[256,2048]{1,0:T(8,128)}, f32[256,2048]{1,0:T(8,128)S(1)}, u32[]{:S(2)}, u32[]{:S(2)}) collective-permute-start(f32[256,2048]{1,0:T(8,128)} %get-tuple-element.54.p_ref), channel_id=1, source_target_pairs={{0,1},{1,0},{2,3},{3,2},{4,5},{5,4},{6,7},{7,6}} | collective-permute-start | bytes 6291464 | tf_op jit(solution)/shard_map/ppermute | solution.py:611
  250.7 1.6 copy-start
  254.2 1.6 copy-start.1
